TPU v7x, 32 devices: a whole 2x2x4 slice. The times are simulated.
32 devices in a mesh: gx: 2 (over x), gy: 4 (over y, core), gz: 4 (over z).
Axes of the slice: x: 2, y: 2, z: 4, core: 2. Of those that a mesh axis runs over, the one named last changes fastest.
Arguments:
- right_side: float32 [24, 64, 512], P('gx', 'gy', 'gz'), may hold values from -8 to 8
- coefficient: float32 [24, 64, 512], P('gx', 'gy', 'gz'), may hold values from 0.02 to 1
Outputs:
- solution: float32 [24, 64, 512], P('gx', 'gy', 'gz')
- residual: float32 [24, 64, 512], P('gx', 'gy', 'gz')
- precond: float32 [24, 64, 512], P('gx', 'gy', 'gz')
- image: float32 [24, 64, 512], P('gx', 'gy', 'gz')
All inputs are finite; a program needn't handle non-finite values.
Results may differ from a plain program's by a relative error of at most 0.00021.
Values sent between devices are 32-bit elements; how exact they have to be, the bound alone decides.
No kernel may reach another device: no remote copies, remote signals or barrier semaphores. Data moves between devices by JAX's collectives and lax.ppermute only.
A program may use at most 64 MiB of HBM per device.

v0:
```python
import jax
import jax.numpy as jnp
from jax import lax
from jax.sharding import PartitionSpec as P

SWEEPS = 4


relaxation = 0.6


def with_halo(block, sides, width):
    for axis, dim in sides:
        count = lax.axis_size(axis)
        forward = [(i, i + 1) for i in range(count - 1)]
        backward = [(target, source) for source, target in forward]
        low = lax.ppermute(
            lax.slice_in_dim(block, block.shape[dim] - width, None, axis=dim), axis, forward
        )
        high = lax.ppermute(lax.slice_in_dim(block, 0, width, axis=dim), axis, backward)
        block = jnp.concatenate([low, block, high], axis=dim)
    return block


def block_sum(padded):
    summed = padded[:-2] + padded[1:-1] + padded[2:]
    summed = summed[:, :-2] + summed[:, 1:-1] + summed[:, 2:]
    return summed[:, :, :-2] + summed[:, :, 1:-1] + summed[:, :, 2:]


def restrict(values):
    extent = values.shape
    grouped = values.reshape(extent[0] // 2, 2, extent[1] // 2, 2, extent[2] // 2, 2)
    return 0.5 * grouped.sum(axis=(1, 3, 5))


def prolong(values):
    return jnp.repeat(jnp.repeat(jnp.repeat(values, 2, axis=0), 2, axis=1), 2, axis=2)


def stencil(values, reaction):
    padded = with_halo(values, (("gx", 0), ("gy", 1), ("gz", 2)), 1)
    return (27.0 + reaction) * values - block_sum(padded)


def spread_deep(source, reaction):
    margin = SWEEPS - 1
    stacked = jnp.stack([source, reaction, jnp.ones_like(source)])
    widened = with_halo(stacked, (("gx", 1), ("gy", 2), ("gz", 3)), margin)
    wide_source = widened[0]
    wide_reaction = widened[1]
    inside = widened[2]
    correction = relaxation * wide_source / (26.0 + wide_reaction)
    for sweep in range(SWEEPS - 1):
        applied = (27.0 + wide_reaction) * correction - block_sum(jnp.pad(correction, 1))
        correction = (
            correction + relaxation * (wide_source - applied) / (26.0 + wide_reaction)
        ) * inside
    return correction[margin:-margin, margin:-margin, margin:-margin]


def coarsest(source, reaction):
    return spread_deep(source, reaction)


def multigrid(source, reactions, level_index):
    if level_index == 2:
        return coarsest(source, reactions[2])
    reaction = reactions[level_index]
    correction = relaxation * source / (26.0 + reaction)
    remainder = source - stencil(correction, reaction)
    correction = correction + prolong(multigrid(restrict(remainder), reactions, level_index + 1))
    return correction + relaxation * (source - stencil(correction, reaction)) / (26.0 + reaction)


def shards(right_side, coefficient):
    middle = restrict(coefficient)
    reactions = (coefficient, middle, restrict(middle))
    residual = right_side
    precond = multigrid(residual, reactions, 0)
    image = stencil(precond, coefficient)
    gamma_now, delta_now = lax.psum(
        (jnp.sum(residual * precond), jnp.sum(image * precond)), ("gx", "gy", "gz")
    )
    precond_image = multigrid(image, reactions, 0)
    image_twice = stencil(precond_image, coefficient)
    alpha_now = gamma_now / delta_now
    direction = precond
    dir_image = image
    solution = alpha_now * direction
    residual = residual - alpha_now * dir_image
    precond = precond - alpha_now * precond_image
    image = image - alpha_now * image_twice
    return (solution, residual, precond, image)


def solution(mesh):
    placed = (P("gx", "gy", "gz"), P("gx", "gy", "gz"))
    return jax.shard_map(
        shards,
        mesh=mesh,
        in_specs=placed,
        out_specs=(
            P("gx", "gy", "gz"),
            P("gx", "gy", "gz"),
            P("gx", "gy", "gz"),
            P("gx", "gy", "gz"),
        ),
        check_vma=False,
    )
```

profile of v0, /device:TPU:0, one launch (start us, length us, event | category | flops | bytes accessed | tf_op | source)
XLA Modules:
  0.0 375.8 jit_solution(6938410697397260277)
XLA Ops:
  1.6 4.9 %collective-permute-start = (f32[1,16,128]{2,1,0:T(8,128)S(1)}, f32[1,16,128]{2,1,0:T(8,128)S(1)}, u32[]{:S(2)}, u32[]{:S(2)}) collective-permute-start(f32[1,16,128]{2,1,0:T(8,128)S(1)} %get-tuple-element.98), channel_id=1, source_target_pairs={{0,16},{1,17},{2,18},{3,19},{4,20},{5,21},{6,22},{7,23},{8,24},{9,... | collective-permute-start | bytes 24584 | tf_op jit(solution)/shard_map/ppermute | solution.py:17
  7.8 4.2 %collective-permute-done.1 = f32[1,16,128]{2,1,0:T(8,128)S(1)} collective-permute-done((f32[1,16,128]{2,1,0:T(8,128)S(1)}, f32[1,16,128]{2,1,0:T(8,128)S(1)}, u32[]{:S(2)}, u32[]{:S(2)}) %collective-permute-start.1) | collective-permute-done | bytes 8224 | tf_op jit(solution)/shard_map/ppermute | solution.py:20
  14.7 3.5 collective-permute-done.3
  18.3 3.5 collective-permute-start.4
  23.1 8.4 %reshape.99 = f32[6,2,8,2,64,2]{5,4,3,2,1,0:T(8,128)} reshape(f32[12,16,128]{2,1,0:T(8,128)} %param.3) | data formatting | bytes 196608 | tf_op jit(solution)/shard_map/reshape | solution.py:33
  31.5 3.3 reduce_sum.73
  35.6 7.6 %reshape.98 = f32[6,2,8,2,64,2]{5,4,3,2,1,0:T(8,128)} reshape(f32[12,16,128]{2,1,0:T(8,128)S(1)} %fusion.37) | data formatting | bytes 196608 | tf_op jit(solution)/shard_map/reshape | solution.py:33
  43.3 3.3 reduce_sum.72
  49.5 4.2 %collective-permute-done.7 = f32[1,8,64]{2,1,0:T(8,128)S(1)} collective-permute-done((f32[1,8,64]{2,1,0:T(8,128)S(1)}, f32[1,8,64]{2,1,0:T(8,128)S(1)}, u32[]{:S(2)}, u32[]{:S(2)}) %collective-permute-start.7) | collective-permute-done | bytes 2080 | tf_op jit(solution)/shard_map/ppermute | solution.py:20
  53.7 2.6 collective-permute-start.8
  57.7 3.0 collective-permute-done.9
  60.7 4.5 %collective-permute-start.10 = (f32[8,10,1]{2,0,1:T(8,128)S(1)}, f32[8,10,1]{2,0,1:T(8,128)S(1)}, u32[]{:S(2)}, u32[]{:S(2)}) collective-permute-start(f32[8,10,1]{2,0,1:T(8,128)S(1)} %get-tuple-element.122), channel_id=1, source_target_pairs={{0,1},{1,2},{2,3},{4,5},{5,6},{6,7},{8,9},{9,10},{10,11},{12,13},{... | collective-permute-start | bytes 968 | tf_op jit(solution)/shard_map/ppermute | solution.py:17
  66.9 4.2 %collective-permute-done.11 = f32[8,10,1]{2,0,1:T(8,128)S(1)} collective-permute-done((f32[8,10,1]{2,0,1:T(8,128)S(1)}, f32[8,10,1]{2,0,1:T(8,128)S(1)}, u32[]{:S(2)}, u32[]{:S(2)}) %collective-permute-start.11) | collective-permute-done | bytes 352 | tf_op jit(solution)/shard_map/ppermute | solution.py:20
  74.7 4.5 %collective-permute-start.12 = (f32[3,3,4,32]{3,2,1,0:T(4,128)S(1)}, f32[3,3,4,32]{3,2,1,0:T(4,128)S(1)}, u32[]{:S(2)}, u32[]{:S(2)}) collective-permute-start(f32[3,3,4,32]{3,2,1,0:T(4,128)S(1)} %pad_maximum_fusion.37), channel_id=1, source_target_pairs={{0,16},{1,17},{2,18},{3,19},{4,20},{5,21},{6,22},{7,23},{8,24},{9,... | collective-permute-start | bytes 13832 | tf_op jit(solution)/shard_map/ppermute | solution.py:17
  80.7 1.7 collective-permute-start.14
  83.7 3.9 %collective-permute-done.15 = f32[3,9,3,32]{3,2,1,0:T(4,128)S(1)} collective-permute-done((f32[3,9,3,32]{3,2,1,0:T(4,128)S(1)}, f32[3,9,3,32]{3,2,1,0:T(4,128)S(1)}, u32[]{:S(2)}, u32[]{:S(2)}) %collective-permute-start.15) | collective-permute-done | bytes 10400 | tf_op jit(solution)/shard_map/ppermute | solution.py:20
  87.9 3.5 collective-permute-start.16
  92.7 2.6 collective-permute-done.16
  95.3 4.7 %collective-permute-done.17 = f32[3,9,10,3]{3,2,1,0:T(8,128)S(1)} collective-permute-done((f32[3,9,10,3]{3,2,1,0:T(8,128)S(1)}, f32[3,9,10,3]{3,2,1,0:T(8,128)S(1)}, u32[]{:S(2)}, u32[]{:S(2)}) %collective-permute-start.17) | collective-permute-done | bytes 3272 | tf_op jit(solution)/shard_map/ppermute | solution.py:20
  101.5 4.2 %collective-permute-start.18 = (f32[1,8,64]{2,1,0:T(8,128)S(1)}, f32[1,8,64]{2,1,0:T(8,128)S(1)}, u32[]{:S(2)}, u32[]{:S(2)}) collective-permute-start(f32[1,8,64]{2,1,0:T(8,128)S(1)} %get-tuple-element.136), channel_id=1, source_target_pairs={{0,16},{1,17},{2,18},{3,19},{4,20},{5,21},{6,22},{7,23},{8,24},{9,... | collective-permute-start | bytes 6152 | tf_op jit(solution)/shard_map/ppermute | solution.py:17
  107.1 4.2 %collective-permute-done.19 = f32[1,8,64]{2,1,0:T(8,128)S(1)} collective-permute-done((f32[1,8,64]{2,1,0:T(8,128)S(1)}, f32[1,8,64]{2,1,0:T(8,128)S(1)}, u32[]{:S(2)}, u32[]{:S(2)}) %collective-permute-start.19) | collective-permute-done | bytes 2080 | tf_op jit(solution)/shard_map/ppermute | solution.py:20
  111.3 2.0 collective-permute-start.20
  114.6 3.2 collective-permute-done.21
  117.9 3.5 collective-permute-start.22
  123.0 4.2 %collective-permute-done.23 = f32[8,10,1]{2,0,1:T(8,128)S(1)} collective-permute-done((f32[8,10,1]{2,0,1:T(8,128)S(1)}, f32[8,10,1]{2,0,1:T(8,128)S(1)}, u32[]{:S(2)}, u32[]{:S(2)}) %collective-permute-start.23) | collective-permute-done | bytes 352 | tf_op jit(solution)/shard_map/ppermute | solution.py:20
  131.3 4.2 %collective-permute-done.25 = f32[1,16,128]{2,1,0:T(8,128)S(1)} collective-permute-done((f32[1,16,128]{2,1,0:T(8,128)S(1)}, f32[1,16,128]{2,1,0:T(8,128)S(1)}, u32[]{:S(2)}, u32[]{:S(2)}) %collective-permute-start.25) | collective-permute-done | bytes 8224 | tf_op jit(solution)/shard_map/ppermute | solution.py:20
  138.3 4.1 %collective-permute-done.27 = f32[14,1,128]{2,1,0:T(1,128)S(1)} collective-permute-done((f32[14,1,128]{2,1,0:T(1,128)S(1)}, f32[14,1,128]{2,1,0:T(1,128)S(1)}, u32[]{:S(2)}, u32[]{:S(2)}) %collective-permute-start.27) | collective-permute-done | bytes 7200 | tf_op jit(solution)/shard_map/ppermute | solution.py:20
  142.5 1.9 collective-permute-start.28
  147.2 4.7 %collective-permute-done.29 = f32[14,18,1]{2,0,1:T(8,128)S(1)} collective-permute-done((f32[14,18,1]{2,0,1:T(8,128)S(1)}, f32[14,18,1]{2,0,1:T(8,128)S(1)}, u32[]{:S(2)}, u32[]{:S(2)}) %collective-permute-start.29) | collective-permute-done | bytes 1040 | tf_op jit(solution)/shard_map/ppermute | solution.py:20
  155.8 4.2 %collective-permute-done.31 = f32[1,16,128]{2,1,0:T(8,128)S(1)} collective-permute-done((f32[1,16,128]{2,1,0:T(8,128)S(1)}, f32[1,16,128]{2,1,0:T(8,128)S(1)}, u32[]{:S(2)}, u32[]{:S(2)}) %collective-permute-start.31) | collective-permute-done | bytes 8224 | tf_op jit(solution)/shard_map/ppermute | solution.py:20
  162.8 3.7 collective-permute-done.33
  166.6 1.9 collective-permute-start.34
  171.3 4.7 %collective-permute-done.35 = f32[14,18,1]{2,0,1:T(8,128)S(1)} collective-permute-done((f32[14,18,1]{2,0,1:T(8,128)S(1)}, f32[14,18,1]{2,0,1:T(8,128)S(1)}, u32[]{:S(2)}, u32[]{:S(2)}) %collective-permute-start.35) | collective-permute-done | bytes 1040 | tf_op jit(solution)/shard_map/ppermute | solution.py:20
  179.9 4.2 %collective-permute-done.37 = f32[1,16,128]{2,1,0:T(8,128)S(1)} collective-permute-done((f32[1,16,128]{2,1,0:T(8,128)S(1)}, f32[1,16,128]{2,1,0:T(8,128)S(1)}, u32[]{:S(2)}, u32[]{:S(2)}) %collective-permute-start.37) | collective-permute-done | bytes 8224 | tf_op jit(solution)/shard_map/ppermute | solution.py:20
  187.0 3.7 collective-permute-done.39
  190.8 1.9 collective-permute-start.40
  195.5 4.7 %collective-permute-done.41 = f32[14,18,1]{2,0,1:T(8,128)S(1)} collective-permute-done((f32[14,18,1]{2,0,1:T(8,128)S(1)}, f32[14,18,1]{2,0,1:T(8,128)S(1)}, u32[]{:S(2)}, u32[]{:S(2)}) %collective-permute-start.41) | collective-permute-done | bytes 1040 | tf_op jit(solution)/shard_map/ppermute | solution.py:20
  201.0 7.6 %reshape.107 = f32[6,2,8,2,64,2]{5,4,3,2,1,0:T(8,128)} reshape(f32[12,16,128]{2,1,0:T(8,128)S(1)} %fusion.29) | data formatting | bytes 196608 | tf_op jit(solution)/shard_map/reshape | solution.py:33
  208.6 3.3 reduce_sum.78
  214.9 4.2 %collective-permute-done.43 = f32[1,8,64]{2,1,0:T(8,128)S(1)} collective-permute-done((f32[1,8,64]{2,1,0:T(8,128)S(1)}, f32[1,8,64]{2,1,0:T(8,128)S(1)}, u32[]{:S(2)}, u32[]{:S(2)}) %collective-permute-start.43) | collective-permute-done | bytes 2080 | tf_op jit(solution)/shard_map/ppermute | solution.py:20
  221.9 3.7 collective-permute-done.45
  225.7 1.9 collective-permute-start.46
  229.3 4.2 %collective-permute-done.47 = f32[8,10,1]{2,0,1:T(8,128)S(1)} collective-permute-done((f32[8,10,1]{2,0,1:T(8,128)S(1)}, f32[8,10,1]{2,0,1:T(8,128)S(1)}, u32[]{:S(2)}, u32[]{:S(2)}) %collective-permute-start.47) | collective-permute-done | bytes 352 | tf_op jit(solution)/shard_map/ppermute | solution.py:20
  236.0 4.5 %collective-permute-start.48 = (f32[3,3,4,32]{3,2,1,0:T(4,128)S(1)}, f32[3,3,4,32]{3,2,1,0:T(4,128)S(1)}, u32[]{:S(2)}, u32[]{:S(2)}) collective-permute-start(f32[3,3,4,32]{3,2,1,0:T(4,128)S(1)} %pad_maximum_fusion.36), channel_id=1, source_target_pairs={{0,16},{1,17},{2,18},{3,19},{4,20},{5,21},{6,22},{7,23},{8,24},{9,... | collective-permute-start | bytes 13832 | tf_op jit(solution)/shard_map/ppermute | solution.py:17
  242.1 1.7 collective-permute-start.50
  245.1 3.9 %collective-permute-done.51 = f32[3,9,3,32]{3,2,1,0:T(4,128)S(1)} collective-permute-done((f32[3,9,3,32]{3,2,1,0:T(4,128)S(1)}, f32[3,9,3,32]{3,2,1,0:T(4,128)S(1)}, u32[]{:S(2)}, u32[]{:S(2)}) %collective-permute-start.51) | collective-permute-done | bytes 10400 | tf_op jit(solution)/shard_map/ppermute | solution.py:20
  249.2 1.9 collective-permute-start.52
  252.5 2.6 collective-permute-done.52
  255.1 4.7 %collective-permute-done.53 = f32[3,9,10,3]{3,2,1,0:T(8,128)S(1)} collective-permute-done((f32[3,9,10,3]{3,2,1,0:T(8,128)S(1)}, f32[3,9,10,3]{3,2,1,0:T(8,128)S(1)}, u32[]{:S(2)}, u32[]{:S(2)}) %collective-permute-start.53) | collective-permute-done | bytes 3272 | tf_op jit(solution)/shard_map/ppermute | solution.py:20
  261.3 4.2 %collective-permute-start.54 = (f32[1,8,64]{2,1,0:T(8,128)S(1)}, f32[1,8,64]{2,1,0:T(8,128)S(1)}, u32[]{:S(2)}, u32[]{:S(2)}) collective-permute-start(f32[1,8,64]{2,1,0:T(8,128)S(1)} %get-tuple-element.132), channel_id=1, source_target_pairs={{0,16},{1,17},{2,18},{3,19},{4,20},{5,21},{6,22},{7,23},{8,24},{9,... | collective-permute-start | bytes 6152 | tf_op jit(solution)/shard_map/ppermute | solution.py:17
  266.9 4.2 %collective-permute-done.55 = f32[1,8,64]{2,1,0:T(8,128)S(1)} collective-permute-done((f32[1,8,64]{2,1,0:T(8,128)S(1)}, f32[1,8,64]{2,1,0:T(8,128)S(1)}, u32[]{:S(2)}, u32[]{:S(2)}) %collective-permute-start.55) | collective-permute-done | bytes 2080 | tf_op jit(solution)/shard_map/ppermute | solution.py:20
  271.1 2.0 collective-permute-start.56
  274.4 3.2 collective-permute-done.57
  277.7 1.9 collective-permute-start.58
  281.2 4.2 %collective-permute-done.59 = f32[8,10,1]{2,0,1:T(8,128)S(1)} collective-permute-done((f32[8,10,1]{2,0,1:T(8,128)S(1)}, f32[8,10,1]{2,0,1:T(8,128)S(1)}, u32[]{:S(2)}, u32[]{:S(2)}) %collective-permute-start.59) | collective-permute-done | bytes 352 | tf_op jit(solution)/shard_map/ppermute | solution.py:20
  290.1 4.2 %collective-permute-done.61 = f32[1,16,128]{2,1,0:T(8,128)S(1)} collective-permute-done((f32[1,16,128]{2,1,0:T(8,128)S(1)}, f32[1,16,128]{2,1,0:T(8,128)S(1)}, u32[]{:S(2)}, u32[]{:S(2)}) %collective-permute-start.61) | collective-permute-done | bytes 8224 | tf_op jit(solution)/shard_map/ppermute | solution.py:20
  297.1 4.1 %collective-permute-done.63 = f32[14,1,128]{2,1,0:T(1,128)S(1)} collective-permute-done((f32[14,1,128]{2,1,0:T(1,128)S(1)}, f32[14,1,128]{2,1,0:T(1,128)S(1)}, u32[]{:S(2)}, u32[]{:S(2)}) %collective-permute-start.63) | collective-permute-done | bytes 7200 | tf_op jit(solution)/shard_map/ppermute | solution.py:20
  301.3 1.9 collective-permute-start.64
  304.6 41.1 %all-reduce.6 = (f32[]{:T(128)}, f32[]{:T(128)}) all-reduce(f32[]{:T(128)} %get-tuple-element.21, f32[]{:T(128)} %get-tuple-element.20), channel_id=1, replica_groups=mesh['gx'=2,'gy'=4,'gz'=4] {'gx','gy','gz'}, use_global_device_ids=true, to_apply=%region_5.6 | all-reduce | flops 2 | bytes 16 | tf_op jit(solution)/shard_map/psum | solution.py:82
  348.5 4.2 %collective-permute-start.66 = (f32[1,16,128]{2,1,0:T(8,128)S(1)}, f32[1,16,128]{2,1,0:T(8,128)S(1)}, u32[]{:S(2)}, u32[]{:S(2)}) collective-permute-start(f32[1,16,128]{2,1,0:T(8,128)S(1)} %get-tuple-element.86), channel_id=1, source_target_pairs={{0,16},{1,17},{2,18},{3,19},{4,20},{5,21},{6,22},{7,23},{8,24},{9,... | collective-permute-start | bytes 24584 | tf_op jit(solution)/shard_map/ppermute | solution.py:17
  354.0 4.2 %collective-permute-done.67 = f32[1,16,128]{2,1,0:T(8,128)S(1)} collective-permute-done((f32[1,16,128]{2,1,0:T(8,128)S(1)}, f32[1,16,128]{2,1,0:T(8,128)S(1)}, u32[]{:S(2)}, u32[]{:S(2)}) %collective-permute-start.67) | collective-permute-done | bytes 8224 | tf_op jit(solution)/shard_map/ppermute | solution.py:20
  360.9 4.0 %collective-permute-done.69 = f32[14,1,128]{2,1,0:T(1,128)S(1)} collective-permute-done((f32[14,1,128]{2,1,0:T(1,128)S(1)}, f32[14,1,128]{2,1,0:T(1,128)S(1)}, u32[]{:S(2)}, u32[]{:S(2)}) %collective-permute-start.69) | collective-permute-done | bytes 7200 | tf_op jit(solution)/shard_map/ppermute | solution.py:20
  365.0 1.8 collective-permute-start.70
  369.6 4.7 %collective-permute-done.71 = f32[14,18,1]{2,0,1:T(8,128)S(1)} collective-permute-done((f32[14,18,1]{2,0,1:T(8,128)S(1)}, f32[14,18,1]{2,0,1:T(8,128)S(1)}, u32[]{:S(2)}, u32[]{:S(2)}) %collective-permute-start.71) | collective-permute-done | bytes 1040 | tf_op jit(solution)/shard_map/ppermute | solution.py:20
  (279 shorter events, 94.4 us)
Async XLA Ops:
  1.6 6.2 %collective-permute-start = (f32[1,16,128]{2,1,0:T(8,128)S(1)}, f32[1,16,128]{2,1,0:T(8,128)S(1)}, u32[]{:S(2)}, u32[]{:S(2)}) collective-permute-start(f32[1,16,128]{2,1,0:T(8,128)S(1)} %get-tuple-element.98), channel_id=1, source_target_pairs={{0,16},{1,17},{2,18},{3,19},{4,20},{5,21},{6,22},{7,23},{8,24},{9,... | collective-permute-start | bytes 24584 | tf_op jit(solution)/shard_map/ppermute | solution.py:17
  6.5 5.5 %collective-permute-start.1 = (f32[1,16,128]{2,1,0:T(8,128)S(1)}, f32[1,16,128]{2,1,0:T(8,128)S(1)}, u32[]{:S(2)}, u32[]{:S(2)}) collective-permute-start(f32[1,16,128]{2,1,0:T(8,128)S(1)} %get-tuple-element.99), channel_id=1, source_target_pairs={{16,0},{17,1},{18,2},{19,3},{20,4},{21,5},{22,6},{23,7},{24,8},{25... | collective-permute-start | bytes 24584 | tf_op jit(solution)/shard_map/ppermute | solution.py:20
  13.4 4.8 %collective-permute-start.3 = (f32[14,1,128]{2,1,0:T(1,128)S(1)}, f32[14,1,128]{2,1,0:T(1,128)S(1)}, u32[]{:S(2)}, u32[]{:S(2)}) collective-permute-start(f32[14,1,128]{2,1,0:T(1,128)S(1)} %get-tuple-element.82), channel_id=1, source_target_pairs={{4,0},{8,4},{12,8},{5,1},{9,5},{13,9},{6,2},{10,6},{14,10},{7,3},{... | collective-permute-start | bytes 21512 | tf_op jit(solution)/shard_map/ppermute | solution.py:20
  18.3 16.5 %collective-permute-start.4 = (f32[14,18,1]{2,0,1:T(8,128)S(1)}, f32[14,18,1]{2,0,1:T(8,128)S(1)}, u32[]{:S(2)}, u32[]{:S(2)}) collective-permute-start(f32[14,18,1]{2,0,1:T(8,128)S(1)} %get-tuple-element.70), channel_id=1, source_target_pairs={{0,1},{1,2},{2,3},{4,5},{5,6},{6,7},{8,9},{9,10},{10,11},{12,13},{... | collective-permute-start | bytes 3032 | tf_op jit(solution)/shard_map/ppermute | solution.py:17
  21.8 13.0 %collective-permute-start.5 = (f32[14,18,1]{2,0,1:T(8,128)S(1)}, f32[14,18,1]{2,0,1:T(8,128)S(1)}, u32[]{:S(2)}, u32[]{:S(2)}) collective-permute-start(f32[14,18,1]{2,0,1:T(8,128)S(1)} %get-tuple-element.71), channel_id=1, source_target_pairs={{1,0},{2,1},{3,2},{5,4},{6,5},{7,6},{9,8},{10,9},{11,10},{13,12},{... | collective-permute-start | bytes 3032 | tf_op jit(solution)/shard_map/ppermute | solution.py:20
  46.6 3.0 collective-permute-start.6
  48.2 5.5 %collective-permute-start.7 = (f32[1,8,64]{2,1,0:T(8,128)S(1)}, f32[1,8,64]{2,1,0:T(8,128)S(1)}, u32[]{:S(2)}, u32[]{:S(2)}) collective-permute-start(f32[1,8,64]{2,1,0:T(8,128)S(1)} %get-tuple-element.141), channel_id=1, source_target_pairs={{16,0},{17,1},{18,2},{19,3},{20,4},{21,5},{22,6},{23,7},{24,8},{25... | collective-permute-start | bytes 6152 | tf_op jit(solution)/shard_map/ppermute | solution.py:20
  53.7 3.9 %collective-permute-start.8 = (f32[8,1,64]{2,1,0:T(1,128)S(1)}, f32[8,1,64]{2,1,0:T(1,128)S(1)}, u32[]{:S(2)}, u32[]{:S(2)}) collective-permute-start(f32[8,1,64]{2,1,0:T(1,128)S(1)} %get-tuple-element.130), channel_id=1, source_target_pairs={{0,4},{4,8},{8,12},{1,5},{5,9},{9,13},{2,6},{6,10},{10,14},{3,7},{... | collective-permute-start | bytes 6152 | tf_op jit(solution)/shard_map/ppermute | solution.py:17
  56.3 4.3 %collective-permute-start.9 = (f32[8,1,64]{2,1,0:T(1,128)S(1)}, f32[8,1,64]{2,1,0:T(1,128)S(1)}, u32[]{:S(2)}, u32[]{:S(2)}) collective-permute-start(f32[8,1,64]{2,1,0:T(1,128)S(1)} %get-tuple-element.131), channel_id=1, source_target_pairs={{4,0},{8,4},{12,8},{5,1},{9,5},{13,9},{6,2},{10,6},{14,10},{7,3},{... | collective-permute-start | bytes 6152 | tf_op jit(solution)/shard_map/ppermute | solution.py:20
  60.7 6.2 %collective-permute-start.10 = (f32[8,10,1]{2,0,1:T(8,128)S(1)}, f32[8,10,1]{2,0,1:T(8,128)S(1)}, u32[]{:S(2)}, u32[]{:S(2)}) collective-permute-start(f32[8,10,1]{2,0,1:T(8,128)S(1)} %get-tuple-element.122), channel_id=1, source_target_pairs={{0,1},{1,2},{2,3},{4,5},{5,6},{6,7},{8,9},{9,10},{10,11},{12,13},{... | collective-permute-start | bytes 968 | tf_op jit(solution)/shard_map/ppermute | solution.py:17
  65.3 5.9 %collective-permute-start.11 = (f32[8,10,1]{2,0,1:T(8,128)S(1)}, f32[8,10,1]{2,0,1:T(8,128)S(1)}, u32[]{:S(2)}, u32[]{:S(2)}) collective-permute-start(f32[8,10,1]{2,0,1:T(8,128)S(1)} %get-tuple-element.123), channel_id=1, source_target_pairs={{1,0},{2,1},{3,2},{5,4},{6,5},{7,6},{9,8},{10,9},{11,10},{13,12},{... | collective-permute-start | bytes 968 | tf_op jit(solution)/shard_map/ppermute | solution.py:20
  73.4 5.9 %collective-permute-start.13 = (f32[3,3,4,32]{3,2,1,0:T(4,128)S(1)}, f32[3,3,4,32]{3,2,1,0:T(4,128)S(1)}, u32[]{:S(2)}, u32[]{:S(2)}) collective-permute-start(f32[3,3,4,32]{3,2,1,0:T(4,128)S(1)} %pad_maximum_fusion.37), channel_id=1, source_target_pairs={{16,0},{17,1},{18,2},{19,3},{20,4},{21,5},{22,6},{23,7},{24,8},{25... | collective-permute-start | bytes 13832 | tf_op jit(solution)/shard_map/ppermute | solution.py:20
  74.7 6.0 %collective-permute-start.12 = (f32[3,3,4,32]{3,2,1,0:T(4,128)S(1)}, f32[3,3,4,32]{3,2,1,0:T(4,128)S(1)}, u32[]{:S(2)}, u32[]{:S(2)}) collective-permute-start(f32[3,3,4,32]{3,2,1,0:T(4,128)S(1)} %pad_maximum_fusion.37), channel_id=1, source_target_pairs={{0,16},{1,17},{2,18},{3,19},{4,20},{5,21},{6,22},{7,23},{8,24},{9,... | collective-permute-start | bytes 13832 | tf_op jit(solution)/shard_map/ppermute | solution.py:17
  80.7 3.0 collective-permute-start.14
  82.4 5.2 %collective-permute-start.15 = (f32[3,9,3,32]{3,2,1,0:T(4,128)S(1)}, f32[3,9,3,32]{3,2,1,0:T(4,128)S(1)}, u32[]{:S(2)}, u32[]{:S(2)}) collective-permute-start(f32[3,9,3,32]{3,2,1,0:T(4,128)S(1)} %get-tuple-element.103), channel_id=1, source_target_pairs={{4,0},{8,4},{12,8},{5,1},{9,5},{13,9},{6,2},{10,6},{14,10},{7,3},{... | collective-permute-start | bytes 31112 | tf_op jit(solution)/shard_map/ppermute | solution.py:20
  87.9 7.4 %collective-permute-start.16 = (f32[3,9,10,3]{3,2,1,0:T(8,128)S(1)}, f32[3,9,10,3]{3,2,1,0:T(8,128)S(1)}, u32[]{:S(2)}, u32[]{:S(2)}) collective-permute-start(f32[3,9,10,3]{3,2,1,0:T(8,128)S(1)} %get-tuple-element.58), channel_id=1, source_target_pairs={{0,1},{1,2},{2,3},{4,5},{5,6},{6,7},{8,9},{9,10},{10,11},{12,13},{... | collective-permute-start | bytes 9728 | tf_op jit(solution)/shard_map/ppermute | solution.py:17
  91.4 8.6 %collective-permute-start.17 = (f32[3,9,10,3]{3,2,1,0:T(8,128)S(1)}, f32[3,9,10,3]{3,2,1,0:T(8,128)S(1)}, u32[]{:S(2)}, u32[]{:S(2)}) collective-permute-start(f32[3,9,10,3]{3,2,1,0:T(8,128)S(1)} %get-tuple-element.59), channel_id=1, source_target_pairs={{1,0},{2,1},{3,2},{5,4},{6,5},{7,6},{9,8},{10,9},{11,10},{13,12},{... | collective-permute-start | bytes 9728 | tf_op jit(solution)/shard_map/ppermute | solution.py:20
  101.5 5.5 %collective-permute-start.18 = (f32[1,8,64]{2,1,0:T(8,128)S(1)}, f32[1,8,64]{2,1,0:T(8,128)S(1)}, u32[]{:S(2)}, u32[]{:S(2)}) collective-permute-start(f32[1,8,64]{2,1,0:T(8,128)S(1)} %get-tuple-element.136), channel_id=1, source_target_pairs={{0,16},{1,17},{2,18},{3,19},{4,20},{5,21},{6,22},{7,23},{8,24},{9,... | collective-permute-start | bytes 6152 | tf_op jit(solution)/shard_map/ppermute | solution.py:17
  105.8 5.5 %collective-permute-start.19 = (f32[1,8,64]{2,1,0:T(8,128)S(1)}, f32[1,8,64]{2,1,0:T(8,128)S(1)}, u32[]{:S(2)}, u32[]{:S(2)}) collective-permute-start(f32[1,8,64]{2,1,0:T(8,128)S(1)} %get-tuple-element.137), channel_id=1, source_target_pairs={{16,0},{17,1},{18,2},{19,3},{20,4},{21,5},{22,6},{23,7},{24,8},{25... | collective-permute-start | bytes 6152 | tf_op jit(solution)/shard_map/ppermute | solution.py:20
  111.3 3.3 collective-permute-start.20
  113.3 4.5 %collective-permute-start.21 = (f32[8,1,64]{2,1,0:T(1,128)S(1)}, f32[8,1,64]{2,1,0:T(1,128)S(1)}, u32[]{:S(2)}, u32[]{:S(2)}) collective-permute-start(f32[8,1,64]{2,1,0:T(1,128)S(1)} %get-tuple-element.129), channel_id=1, source_target_pairs={{4,0},{8,4},{12,8},{5,1},{9,5},{13,9},{6,2},{10,6},{14,10},{7,3},{... | collective-permute-start | bytes 6152 | tf_op jit(solution)/shard_map/ppermute | solution.py:20
  117.9 5.1 %collective-permute-start.22 = (f32[8,10,1]{2,0,1:T(8,128)S(1)}, f32[8,10,1]{2,0,1:T(8,128)S(1)}, u32[]{:S(2)}, u32[]{:S(2)}) collective-permute-start(f32[8,10,1]{2,0,1:T(8,128)S(1)} %get-tuple-element.117), channel_id=1, source_target_pairs={{0,1},{1,2},{2,3},{4,5},{5,6},{6,7},{8,9},{9,10},{10,11},{12,13},{... | collective-permute-start | bytes 968 | tf_op jit(solution)/shard_map/ppermute | solution.py:17
  121.3 5.9 %collective-permute-start.23 = (f32[8,10,1]{2,0,1:T(8,128)S(1)}, f32[8,10,1]{2,0,1:T(8,128)S(1)}, u32[]{:S(2)}, u32[]{:S(2)}) collective-permute-start(f32[8,10,1]{2,0,1:T(8,128)S(1)} %get-tuple-element.118), channel_id=1, source_target_pairs={{1,0},{2,1},{3,2},{5,4},{6,5},{7,6},{9,8},{10,9},{11,10},{13,12},{... | collective-permute-start | bytes 968 | tf_op jit(solution)/shard_map/ppermute | solution.py:20
  128.3 3.0 collective-permute-start.24
  129.9 5.5 %collective-permute-start.25 = (f32[1,16,128]{2,1,0:T(8,128)S(1)}, f32[1,16,128]{2,1,0:T(8,128)S(1)}, u32[]{:S(2)}, u32[]{:S(2)}) collective-permute-start(f32[1,16,128]{2,1,0:T(8,128)S(1)} %get-tuple-element.97), channel_id=1, source_target_pairs={{16,0},{17,1},{18,2},{19,3},{20,4},{21,5},{22,6},{23,7},{24,8},{25... | collective-permute-start | bytes 24584 | tf_op jit(solution)/shard_map/ppermute | solution.py:20
  136.9 5.5 %collective-permute-start.27 = (f32[14,1,128]{2,1,0:T(1,128)S(1)}, f32[14,1,128]{2,1,0:T(1,128)S(1)}, u32[]{:S(2)}, u32[]{:S(2)}) collective-permute-start(f32[14,1,128]{2,1,0:T(1,128)S(1)} %get-tuple-element.80), channel_id=1, source_target_pairs={{4,0},{8,4},{12,8},{5,1},{9,5},{13,9},{6,2},{10,6},{14,10},{7,3},{... | collective-permute-start | bytes 21512 | tf_op jit(solution)/shard_map/ppermute | solution.py:20
  142.5 4.7 %collective-permute-start.28 = (f32[14,18,1]{2,0,1:T(8,128)S(1)}, f32[14,18,1]{2,0,1:T(8,128)S(1)}, u32[]{:S(2)}, u32[]{:S(2)}) collective-permute-start(f32[14,18,1]{2,0,1:T(8,128)S(1)} %get-tuple-element.68), channel_id=1, source_target_pairs={{0,1},{1,2},{2,3},{4,5},{5,6},{6,7},{8,9},{9,10},{10,11},{12,13},{... | collective-permute-start | bytes 3032 | tf_op jit(solution)/shard_map/ppermute | solution.py:17
  144.5 7.5 %collective-permute-start.29 = (f32[14,18,1]{2,0,1:T(8,128)S(1)}, f32[14,18,1]{2,0,1:T(8,128)S(1)}, u32[]{:S(2)}, u32[]{:S(2)}) collective-permute-start(f32[14,18,1]{2,0,1:T(8,128)S(1)} %get-tuple-element.69), channel_id=1, source_target_pairs={{1,0},{2,1},{3,2},{5,4},{6,5},{7,6},{9,8},{10,9},{11,10},{13,12},{... | collective-permute-start | bytes 3032 | tf_op jit(solution)/shard_map/ppermute | solution.py:20
  152.8 3.0 collective-permute-start.30
  154.4 5.5 %collective-permute-start.31 = (f32[1,16,128]{2,1,0:T(8,128)S(1)}, f32[1,16,128]{2,1,0:T(8,128)S(1)}, u32[]{:S(2)}, u32[]{:S(2)}) collective-permute-start(f32[1,16,128]{2,1,0:T(8,128)S(1)} %get-tuple-element.95), channel_id=1, source_target_pairs={{16,0},{17,1},{18,2},{19,3},{20,4},{21,5},{22,6},{23,7},{24,8},{25... | collective-permute-start | bytes 24584 | tf_op jit(solution)/shard_map/ppermute | solution.py:20
  161.4 5.0 %collective-permute-start.33 = (f32[14,1,128]{2,1,0:T(1,128)S(1)}, f32[14,1,128]{2,1,0:T(1,128)S(1)}, u32[]{:S(2)}, u32[]{:S(2)}) collective-permute-start(f32[14,1,128]{2,1,0:T(1,128)S(1)} %get-tuple-element.78), channel_id=1, source_target_pairs={{4,0},{8,4},{12,8},{5,1},{9,5},{13,9},{6,2},{10,6},{14,10},{7,3},{... | collective-permute-start | bytes 21512 | tf_op jit(solution)/shard_map/ppermute | solution.py:20
  166.6 4.7 %collective-permute-start.34 = (f32[14,18,1]{2,0,1:T(8,128)S(1)}, f32[14,18,1]{2,0,1:T(8,128)S(1)}, u32[]{:S(2)}, u32[]{:S(2)}) collective-permute-start(f32[14,18,1]{2,0,1:T(8,128)S(1)} %get-tuple-element.66), channel_id=1, source_target_pairs={{0,1},{1,2},{2,3},{4,5},{5,6},{6,7},{8,9},{9,10},{10,11},{12,13},{... | collective-permute-start | bytes 3032 | tf_op jit(solution)/shard_map/ppermute | solution.py:17
  168.5 7.5 %collective-permute-start.35 = (f32[14,18,1]{2,0,1:T(8,128)S(1)}, f32[14,18,1]{2,0,1:T(8,128)S(1)}, u32[]{:S(2)}, u32[]{:S(2)}) collective-permute-start(f32[14,18,1]{2,0,1:T(8,128)S(1)} %get-tuple-element.67), channel_id=1, source_target_pairs={{1,0},{2,1},{3,2},{5,4},{6,5},{7,6},{9,8},{10,9},{11,10},{13,12},{... | collective-permute-start | bytes 3032 | tf_op jit(solution)/shard_map/ppermute | solution.py:20
  176.8 3.1 collective-permute-start.36
  178.5 5.7 %collective-permute-start.37 = (f32[1,16,128]{2,1,0:T(8,128)S(1)}, f32[1,16,128]{2,1,0:T(8,128)S(1)}, u32[]{:S(2)}, u32[]{:S(2)}) collective-permute-start(f32[1,16,128]{2,1,0:T(8,128)S(1)} %get-tuple-element.93), channel_id=1, source_target_pairs={{16,0},{17,1},{18,2},{19,3},{20,4},{21,5},{22,6},{23,7},{24,8},{25... | collective-permute-start | bytes 24584 | tf_op jit(solution)/shard_map/ppermute | solution.py:20
  185.7 5.0 %collective-permute-start.39 = (f32[14,1,128]{2,1,0:T(1,128)S(1)}, f32[14,1,128]{2,1,0:T(1,128)S(1)}, u32[]{:S(2)}, u32[]{:S(2)}) collective-permute-start(f32[14,1,128]{2,1,0:T(1,128)S(1)} %get-tuple-element.76), channel_id=1, source_target_pairs={{4,0},{8,4},{12,8},{5,1},{9,5},{13,9},{6,2},{10,6},{14,10},{7,3},{... | collective-permute-start | bytes 21512 | tf_op jit(solution)/shard_map/ppermute | solution.py:20
  190.8 4.7 %collective-permute-start.40 = (f32[14,18,1]{2,0,1:T(8,128)S(1)}, f32[14,18,1]{2,0,1:T(8,128)S(1)}, u32[]{:S(2)}, u32[]{:S(2)}) collective-permute-start(f32[14,18,1]{2,0,1:T(8,128)S(1)} %get-tuple-element.64), channel_id=1, source_target_pairs={{0,1},{1,2},{2,3},{4,5},{5,6},{6,7},{8,9},{9,10},{10,11},{12,13},{... | collective-permute-start | bytes 3032 | tf_op jit(solution)/shard_map/ppermute | solution.py:17
  192.7 7.5 %collective-permute-start.41 = (f32[14,18,1]{2,0,1:T(8,128)S(1)}, f32[14,18,1]{2,0,1:T(8,128)S(1)}, u32[]{:S(2)}, u32[]{:S(2)}) collective-permute-start(f32[14,18,1]{2,0,1:T(8,128)S(1)} %get-tuple-element.65), channel_id=1, source_target_pairs={{1,0},{2,1},{3,2},{5,4},{6,5},{7,6},{9,8},{10,9},{11,10},{13,12},{... | collective-permute-start | bytes 3032 | tf_op jit(solution)/shard_map/ppermute | solution.py:20
  213.6 5.5 %collective-permute-start.43 = (f32[1,8,64]{2,1,0:T(8,128)S(1)}, f32[1,8,64]{2,1,0:T(8,128)S(1)}, u32[]{:S(2)}, u32[]{:S(2)}) collective-permute-start(f32[1,8,64]{2,1,0:T(8,128)S(1)} %get-tuple-element.135), channel_id=1, source_target_pairs={{16,0},{17,1},{18,2},{19,3},{20,4},{21,5},{22,6},{23,7},{24,8},{25... | collective-permute-start | bytes 6152 | tf_op jit(solution)/shard_map/ppermute | solution.py:20
  220.6 5.0 %collective-permute-start.45 = (f32[8,1,64]{2,1,0:T(1,128)S(1)}, f32[8,1,64]{2,1,0:T(1,128)S(1)}, u32[]{:S(2)}, u32[]{:S(2)}) collective-permute-start(f32[8,1,64]{2,1,0:T(1,128)S(1)} %get-tuple-element.127), channel_id=1, source_target_pairs={{4,0},{8,4},{12,8},{5,1},{9,5},{13,9},{6,2},{10,6},{14,10},{7,3},{... | collective-permute-start | bytes 6152 | tf_op jit(solution)/shard_map/ppermute | solution.py:20
  225.7 3.6 collective-permute-start.46
  227.6 5.9 %collective-permute-start.47 = (f32[8,10,1]{2,0,1:T(8,128)S(1)}, f32[8,10,1]{2,0,1:T(8,128)S(1)}, u32[]{:S(2)}, u32[]{:S(2)}) collective-permute-start(f32[8,10,1]{2,0,1:T(8,128)S(1)} %get-tuple-element.113), channel_id=1, source_target_pairs={{1,0},{2,1},{3,2},{5,4},{6,5},{7,6},{9,8},{10,9},{11,10},{13,12},{... | collective-permute-start | bytes 968 | tf_op jit(solution)/shard_map/ppermute | solution.py:20
  234.7 5.9 %collective-permute-start.49 = (f32[3,3,4,32]{3,2,1,0:T(4,128)S(1)}, f32[3,3,4,32]{3,2,1,0:T(4,128)S(1)}, u32[]{:S(2)}, u32[]{:S(2)}) collective-permute-start(f32[3,3,4,32]{3,2,1,0:T(4,128)S(1)} %pad_maximum_fusion.36), channel_id=1, source_target_pairs={{16,0},{17,1},{18,2},{19,3},{20,4},{21,5},{22,6},{23,7},{24,8},{25... | collective-permute-start | bytes 13832 | tf_op jit(solution)/shard_map/ppermute | solution.py:20
  236.0 6.0 %collective-permute-start.48 = (f32[3,3,4,32]{3,2,1,0:T(4,128)S(1)}, f32[3,3,4,32]{3,2,1,0:T(4,128)S(1)}, u32[]{:S(2)}, u32[]{:S(2)}) collective-permute-start(f32[3,3,4,32]{3,2,1,0:T(4,128)S(1)} %pad_maximum_fusion.36), channel_id=1, source_target_pairs={{0,16},{1,17},{2,18},{3,19},{4,20},{5,21},{6,22},{7,23},{8,24},{9,... | collective-permute-start | bytes 13832 | tf_op jit(solution)/shard_map/ppermute | solution.py:17
  242.1 3.0 collective-permute-start.50
  243.8 5.2 %collective-permute-start.51 = (f32[3,9,3,32]{3,2,1,0:T(4,128)S(1)}, f32[3,9,3,32]{3,2,1,0:T(4,128)S(1)}, u32[]{:S(2)}, u32[]{:S(2)}) collective-permute-start(f32[3,9,3,32]{3,2,1,0:T(4,128)S(1)} %get-tuple-element.101), channel_id=1, source_target_pairs={{4,0},{8,4},{12,8},{5,1},{9,5},{13,9},{6,2},{10,6},{14,10},{7,3},{... | collective-permute-start | bytes 31112 | tf_op jit(solution)/shard_map/ppermute | solution.py:20
  249.2 5.9 %collective-permute-start.52 = (f32[3,9,10,3]{3,2,1,0:T(8,128)S(1)}, f32[3,9,10,3]{3,2,1,0:T(8,128)S(1)}, u32[]{:S(2)}, u32[]{:S(2)}) collective-permute-start(f32[3,9,10,3]{3,2,1,0:T(8,128)S(1)} %get-tuple-element.53), channel_id=1, source_target_pairs={{0,1},{1,2},{2,3},{4,5},{5,6},{6,7},{8,9},{9,10},{10,11},{12,13},{... | collective-permute-start | bytes 9728 | tf_op jit(solution)/shard_map/ppermute | solution.py:17
  251.2 8.6 %collective-permute-start.53 = (f32[3,9,10,3]{3,2,1,0:T(8,128)S(1)}, f32[3,9,10,3]{3,2,1,0:T(8,128)S(1)}, u32[]{:S(2)}, u32[]{:S(2)}) collective-permute-start(f32[3,9,10,3]{3,2,1,0:T(8,128)S(1)} %get-tuple-element.54), channel_id=1, source_target_pairs={{1,0},{2,1},{3,2},{5,4},{6,5},{7,6},{9,8},{10,9},{11,10},{13,12},{... | collective-permute-start | bytes 9728 | tf_op jit(solution)/shard_map/ppermute | solution.py:20
  261.3 5.5 %collective-permute-start.54 = (f32[1,8,64]{2,1,0:T(8,128)S(1)}, f32[1,8,64]{2,1,0:T(8,128)S(1)}, u32[]{:S(2)}, u32[]{:S(2)}) collective-permute-start(f32[1,8,64]{2,1,0:T(8,128)S(1)} %get-tuple-element.132), channel_id=1, source_target_pairs={{0,16},{1,17},{2,18},{3,19},{4,20},{5,21},{6,22},{7,23},{8,24},{9,... | collective-permute-start | bytes 6152 | tf_op jit(solution)/shard_map/ppermute | solution.py:17
  265.6 5.5 %collective-permute-start.55 = (f32[1,8,64]{2,1,0:T(8,128)S(1)}, f32[1,8,64]{2,1,0:T(8,128)S(1)}, u32[]{:S(2)}, u32[]{:S(2)}) collective-permute-start(f32[1,8,64]{2,1,0:T(8,128)S(1)} %get-tuple-element.133), channel_id=1, source_target_pairs={{16,0},{17,1},{18,2},{19,3},{20,4},{21,5},{22,6},{23,7},{24,8},{25... | collective-permute-start | bytes 6152 | tf_op jit(solution)/shard_map/ppermute | solution.py:20
  271.1 3.3 collective-permute-start.56
  273.1 4.5 %collective-permute-start.57 = (f32[8,1,64]{2,1,0:T(1,128)S(1)}, f32[8,1,64]{2,1,0:T(1,128)S(1)}, u32[]{:S(2)}, u32[]{:S(2)}) collective-permute-start(f32[8,1,64]{2,1,0:T(1,128)S(1)} %get-tuple-element.125), channel_id=1, source_target_pairs={{4,0},{8,4},{12,8},{5,1},{9,5},{13,9},{6,2},{10,6},{14,10},{7,3},{... | collective-permute-start | bytes 6152 | tf_op jit(solution)/shard_map/ppermute | solution.py:20
  277.7 3.6 collective-permute-start.58
  279.6 5.9 %collective-permute-start.59 = (f32[8,10,1]{2,0,1:T(8,128)S(1)}, f32[8,10,1]{2,0,1:T(8,128)S(1)}, u32[]{:S(2)}, u32[]{:S(2)}) collective-permute-start(f32[8,10,1]{2,0,1:T(8,128)S(1)} %get-tuple-element.108), channel_id=1, source_target_pairs={{1,0},{2,1},{3,2},{5,4},{6,5},{7,6},{9,8},{10,9},{11,10},{13,12},{... | collective-permute-start | bytes 968 | tf_op jit(solution)/shard_map/ppermute | solution.py:20
  287.1 3.0 collective-permute-start.60
  288.8 5.5 %collective-permute-start.61 = (f32[1,16,128]{2,1,0:T(8,128)S(1)}, f32[1,16,128]{2,1,0:T(8,128)S(1)}, u32[]{:S(2)}, u32[]{:S(2)}) collective-permute-start(f32[1,16,128]{2,1,0:T(8,128)S(1)} %get-tuple-element.90), channel_id=1, source_target_pairs={{16,0},{17,1},{18,2},{19,3},{20,4},{21,5},{22,6},{23,7},{24,8},{25... | collective-permute-start | bytes 24584 | tf_op jit(solution)/shard_map/ppermute | solution.py:20
  295.8 5.5 %collective-permute-start.63 = (f32[14,1,128]{2,1,0:T(1,128)S(1)}, f32[14,1,128]{2,1,0:T(1,128)S(1)}, u32[]{:S(2)}, u32[]{:S(2)}) collective-permute-start(f32[14,1,128]{2,1,0:T(1,128)S(1)} %get-tuple-element.74), channel_id=1, source_target_pairs={{4,0},{8,4},{12,8},{5,1},{9,5},{13,9},{6,2},{10,6},{14,10},{7,3},{... | collective-permute-start | bytes 21512 | tf_op jit(solution)/shard_map/ppermute | solution.py:20
  301.3 45.6 %collective-permute-start.64 = (f32[14,18,1]{2,0,1:T(8,128)S(1)}, f32[14,18,1]{2,0,1:T(8,128)S(1)}, u32[]{:S(2)}, u32[]{:S(2)}) collective-permute-start(f32[14,18,1]{2,0,1:T(8,128)S(1)} %get-tuple-element.62), channel_id=1, source_target_pairs={{0,1},{1,2},{2,3},{4,5},{5,6},{6,7},{8,9},{9,10},{10,11},{12,13},{... | collective-permute-start | bytes 3032 | tf_op jit(solution)/shard_map/ppermute | solution.py:17
  303.3 43.7 %collective-permute-start.65 = (f32[14,18,1]{2,0,1:T(8,128)S(1)}, f32[14,18,1]{2,0,1:T(8,128)S(1)}, u32[]{:S(2)}, u32[]{:S(2)}) collective-permute-start(f32[14,18,1]{2,0,1:T(8,128)S(1)} %get-tuple-element.63), channel_id=1, source_target_pairs={{1,0},{2,1},{3,2},{5,4},{6,5},{7,6},{9,8},{10,9},{11,10},{13,12},{... | collective-permute-start | bytes 3032 | tf_op jit(solution)/shard_map/ppermute | solution.py:20
  348.5 5.5 %collective-permute-start.66 = (f32[1,16,128]{2,1,0:T(8,128)S(1)}, f32[1,16,128]{2,1,0:T(8,128)S(1)}, u32[]{:S(2)}, u32[]{:S(2)}) collective-permute-start(f32[1,16,128]{2,1,0:T(8,128)S(1)} %get-tuple-element.86), channel_id=1, source_target_pairs={{0,16},{1,17},{2,18},{3,19},{4,20},{5,21},{6,22},{7,23},{8,24},{9,... | collective-permute-start | bytes 24584 | tf_op jit(solution)/shard_map/ppermute | solution.py:17
  352.6 5.5 %collective-permute-start.67 = (f32[1,16,128]{2,1,0:T(8,128)S(1)}, f32[1,16,128]{2,1,0:T(8,128)S(1)}, u32[]{:S(2)}, u32[]{:S(2)}) collective-permute-start(f32[1,16,128]{2,1,0:T(8,128)S(1)} %get-tuple-element.87), channel_id=1, source_target_pairs={{16,0},{17,1},{18,2},{19,3},{20,4},{21,5},{22,6},{23,7},{24,8},{25... | collective-permute-start | bytes 24584 | tf_op jit(solution)/shard_map/ppermute | solution.py:20
  359.5 5.4 %collective-permute-start.69 = (f32[14,1,128]{2,1,0:T(1,128)S(1)}, f32[14,1,128]{2,1,0:T(1,128)S(1)}, u32[]{:S(2)}, u32[]{:S(2)}) collective-permute-start(f32[14,1,128]{2,1,0:T(1,128)S(1)} %get-tuple-element.72), channel_id=1, source_target_pairs={{4,0},{8,4},{12,8},{5,1},{9,5},{13,9},{6,2},{10,6},{14,10},{7,3},{... | collective-permute-start | bytes 21512 | tf_op jit(solution)/shard_map/ppermute | solution.py:20
  365.0 4.6 %collective-permute-start.70 = (f32[14,18,1]{2,0,1:T(8,128)S(1)}, f32[14,18,1]{2,0,1:T(8,128)S(1)}, u32[]{:S(2)}, u32[]{:S(2)}) collective-permute-start(f32[14,18,1]{2,0,1:T(8,128)S(1)} %get-tuple-element.60), channel_id=1, source_target_pairs={{0,1},{1,2},{2,3},{4,5},{5,6},{6,7},{8,9},{9,10},{10,11},{12,13},{... | collective-permute-start | bytes 3032 | tf_op jit(solution)/shard_map/ppermute | solution.py:17
  366.8 7.5 %collective-permute-start.71 = (f32[14,18,1]{2,0,1:T(8,128)S(1)}, f32[14,18,1]{2,0,1:T(8,128)S(1)}, u32[]{:S(2)}, u32[]{:S(2)}) collective-permute-start(f32[14,18,1]{2,0,1:T(8,128)S(1)} %get-tuple-element.61), channel_id=1, source_target_pairs={{1,0},{2,1},{3,2},{5,4},{6,5},{7,6},{9,8},{10,9},{11,10},{13,12},{... | collective-permute-start | bytes 3032 | tf_op jit(solution)/shard_map/ppermute | solution.py:20
  (10 other events, 30.0 us)
where the time goes:
time: 378 us; the launch traced here: 376 us
  waiting for transfers between devices  147 us (39%)
  starting transfers between devices  133 us (35%)
  blocking collectives  41.1 us (11%)
  local copies, waits for them, and re-layouts  30 us (8%)
  other arithmetic  21 us (6%)
  between operations  3.85 us (1%)
    ppermute x36, waiting for transfers between devices, with_halo(): lax.ppermute(lax.slice_in_dim(block, 0, width, axis=dim), axis, backward)  131 us
    ppermute x36, starting transfers between devices, with_halo(): lax.ppermute(lax.slice_in_dim(block, block.shape[dim] - width, None, axis...  86.4 us
    ppermute x36, starting transfers between devices, with_halo(): lax.ppermute(lax.slice_in_dim(block, 0, width, axis=dim), axis, backward)  46.7 us
    psum x1, blocking collectives, shards(): lax.psum((jnp.sum(residual * precond), jnp.sum(image * precond)), ('gx',...  41.1 us
    reshape x5, local copies, waits for them, and re-layouts, restrict(): values.reshape(extent[0] // 2, 2, extent[1] // 2, 2, extent[2] // 2, 2)  25.2 us
    ppermute x36, waiting for transfers between devices, with_halo(): lax.ppermute(lax.slice_in_dim(block, block.shape[dim] - width, None, axis...  15.8 us
    reduce_sum x6, other arithmetic, restrict(): return 0.5 * grouped.sum(axis=(1, 3, 5))  10.3 us
  transfers between devices with their start and end apart: 72, of which 44 were waited for; matrix products, arithmetic and copies ran while one was open for 3% of the time, Pallas kernels for 0%

commit v1 on v0

v1 whole, which is shorter than its diff:
```python
import jax
import jax.numpy as jnp
from jax import lax
from jax.experimental import pallas as pl
from jax.experimental.pallas import tpu as pltpu
from jax.sharding import PartitionSpec as P

SWEEPS = 4
relaxation = 0.6
f32 = jnp.float32

HALO = 4


def roll(value, shift, axis):
    return pltpu.roll(value, shift % value.shape[axis], axis)


def iota(shape, axis):
    return lax.broadcasted_iota(jnp.int32, shape, axis)


class Shape:
    def __init__(self, nx, ny, nz, block):
        self.nx, self.ny, self.nz = nx, ny, nz
        self.bx, self.by, self.bz = block
        self.half = self.by // 2
        self.slots = nx * 4
        self.rows = self.bx * self.half
        self.x1 = nx * self.bx // 2
        self.y1 = self.half // 2
        self.slots1 = 2 * ny
        self.rows1 = self.x1 * self.y1
        self.share = 2 * self.rows1


def fine_tools(s):
    shape = (s.slots, s.bz)
    sub = iota(shape, 0)
    first_block = sub < 4
    last_block = sub >= s.slots - 4
    first_chunk = sub % 4 == 0
    last_chunk = sub % 4 == 3

    def below_x(v):
        return jnp.where(first_block, 0.0, roll(v, 4, 0))

    def above_x(v):
        return jnp.where(last_block, 0.0, roll(v, -4, 0))

    def below_y(v):
        return jnp.where(first_chunk, 0.0, roll(v, 1, 0))

    def above_y(v):
        return jnp.where(last_chunk, 0.0, roll(v, -1, 0))

    return below_x, above_x, below_y, above_y


def triple(v, low, high):
    n = len(v)
    out = []
    for i in range(0, n, 2):
        pair = v[i] + v[i + 1]
        out.append(pair + (low if i == 0 else v[i - 1]))
        out.append(pair + (high if i + 2 == n else v[i + 2]))
    return out


def plain_triple(v):
    n = len(v)
    out = []
    for i in range(n):
        total = v[i]
        if i > 0:
            total = total + v[i - 1]
        if i + 1 < n:
            total = total + v[i + 1]
        out.append(total)
    return out


def fine_block_sum(s, source, temp, consume):
    below_x, above_x, below_y, above_y = fine_tools(s)
    for par in range(2):
        for yi in range(s.half):
            v = [source[par, xi * s.half + yi] for xi in range(s.bx)]
            for xi, t in enumerate(triple(v, below_x(v[-1]), above_x(v[0]))):
                temp[par, xi * s.half + yi] = t
    for i in range(s.bx // 2):
        sums = []
        for k in range(2):
            xi = 2 * i + k
            both = []
            for par in range(2):
                v = [temp[par, xi * s.half + yi] for yi in range(s.half)]
                both.append(triple(v, below_y(v[-1]), above_y(v[0])))
            even, odd = both
            out_even, out_odd = [], []
            for e, o in zip(even, odd):
                pair = e + o
                out_even.append(pair + roll(o, 1, 1))
                out_odd.append(pair + roll(e, -1, 1))
            sums.append((out_even, out_odd))
        consume(i, sums)


def fine_restrict(s, values, i, store):
    for j in range(s.y1):
        total = None
        for k in range(2):
            for par in range(2):
                for yi in (2 * j, 2 * j + 1):
                    v = values[k][par][yi]
                    total = v if total is None else total + v
        store(i * s.y1 + j, 0.5 * total)


def share_out(s, temp, out, lead):
    count = (s.bx // 2) * s.y1
    for h in range(2):
        for b in range(s.nx):
            out[lead, pl.ds(h * s.rows1 + b * count, count), :] = temp[
                pl.ds(b * 4 + 1 + h, count, stride=s.slots), :
            ]


def split3(v):
    high = v.astype(jnp.bfloat16)
    rest = v - high.astype(f32)
    middle = rest.astype(jnp.bfloat16)
    low = (rest - middle.astype(f32)).astype(jnp.bfloat16)
    return high, middle, low


def exact_dot(v, selection):
    dot = lambda a: jnp.dot(a, selection, preferred_element_type=f32)
    high, middle, low = split3(v)
    return dot(high) + (dot(middle) + dot(low))


def first_kernel(s, place, *refs):
    n = s.nx
    own_g, own_c, x_gc = refs[0], refs[1], refs[2:1 + n]
    refs = refs[1 + n:]
    zside = refs[: 2 * n]
    refs = refs[2 * n:]
    y_a, y_b, g_out, d_out, q_out, share, natural, split_e, split_o, temp, temp1 = refs
    ix, iy, iz = place[0], place[1], place[2]
    even_y = iy % 2 == 0
    even_z = iz % 2 == 0
    L = s.bz
    tile = (s.half, L)
    lane = iota(tile, 1)
    row = iota(tile, 0)
    left = lane < L // 2

    def halo(nextlo, prevhi):
        return (
            jnp.where(left, nextlo, roll(prevhi, L // 2, 1)),
            jnp.where(left, roll(nextlo, L // 2, 1), prevhi),
        )

    for t in range(n):
        base = (ix ^ t) if n & (n - 1) == 0 else (ix + t) % n
        for xi in range(s.bx):
            for ch in range(4):
                if ch in (1, 2):
                    span = pl.ds((ch - 1) * s.half, s.half)
                    if t == 0:
                        g, c = own_g[xi, span, :], own_c[xi, span, :]
                    else:
                        g, c = x_gc[t - 1][0, xi, span, :], x_gc[t - 1][1, xi, span, :]
                    a, b = zside[2 * t][xi, span, :], zside[2 * t + 1][xi, span, :]
                    nextlo = jnp.where(even_z, a, b)
                    prevhi = jnp.where(even_z, b, a)
                    gh, chh = halo(nextlo, prevhi)
                else:
                    use_a = even_y if ch == 3 else jnp.logical_not(even_y)
                    gc = jnp.where(use_a, y_a[t, 0, xi], y_b[t, 0, xi])
                    ab = jnp.where(use_a, y_a[t, 1, xi], y_b[t, 1, xi])
                    turned = roll(gc, HALO, 0)
                    ab_turned = roll(ab, HALO, 0)
                    if ch == 3:
                        keep = row < HALO
                        g, c = gc, turned
                        a, b = ab, ab_turned
                    else:
                        keep = row >= s.half - HALO
                        g, c = turned, gc
                        a, b = ab_turned, ab
                    nextlo = jnp.where(even_z, a, b)
                    prevhi = jnp.where(even_z, b, a)
                    gh, chh = halo(nextlo, prevhi)
                    g, c = jnp.where(keep, g, 0.0), jnp.where(keep, c, 0.0)
                    gh, chh = jnp.where(keep, gh, 0.0), jnp.where(keep, chh, 0.0)
                at = ch * s.rows + xi * s.half
                natural[0, pl.ds(at, s.half), pl.ds(0, L)] = g
                natural[0, pl.ds(at, s.half), pl.ds(L, L)] = gh
                natural[1, pl.ds(at, s.half), pl.ds(0, L)] = c
                natural[1, pl.ds(at, s.half), pl.ds(L, L)] = chh
        source = iota((2 * L, 2 * L), 0)
        target = iota((2 * L, 2 * L), 1)
        wanted = jnp.where(target < L, 2 * target, 2 * (target - L) + 1)
        selection = jnp.where(source == wanted, 1.0, 0.0).astype(jnp.bfloat16)
        start = pl.multiple_of(base * (4 * s.rows), 4 * s.rows)
        for arr in range(2):
            parted = exact_dot(natural[arr], selection)
            split_e[arr, pl.ds(start, 4 * s.rows), :] = parted[:, :L]
            split_o[arr, pl.ds(start, 4 * s.rows), :] = parted[:, L:]

    shape = (s.slots, L)
    subs = iota(shape, 0) % 4
    inside = inside_columns(s, iz, shape) & inside_chunks(s, iy, subs)
    for i in range(s.bx // 2):
        values = []
        for k in range(2):
            both = []
            for par, split in enumerate((split_e, split_o)):
                line = []
                for yi in range(s.half):
                    r = (2 * i + k) * s.half + yi
                    g = split[0, pl.ds(r, s.slots, stride=s.rows), :]
                    c = split[1, pl.ds(r, s.slots, stride=s.rows), :]
                    q = 26.0 + c
                    valid = inside
                    if yi >= HALO:
                        valid = valid & (subs != 3)
                    if yi < s.half - HALO:
                        valid = valid & (subs != 0)
                    d = jnp.where(valid, relaxation / q, 0.0)
                    g_out[par, r] = g
                    q_out[par, r] = q
                    d_out[par, r] = d
                    line.append(c)
                both.append(line)
            values.append(both)

        def keep_c(at, tile1):
            temp1[pl.ds(at * s.slots, s.slots), :] = tile1

        fine_restrict(s, values, i, keep_c)
    share_out(s, temp1, share, 1)
    first_half(s, g_out, d_out, temp, temp1, share, 0)


def first_half(s, g_ref, d_ref, temps, temp1, share, lead):
    e_ref, x_ref = temps.at[0], temps.at[1]
    for par in range(2):
        for r in range(s.rows):
            e_ref[par, r] = d_ref[par, r] * g_ref[par, r]

    def consume(i, sums):
        values = []
        for k in range(2):
            both = []
            for par in range(2):
                line = []
                for yi in range(s.half):
                    r = (2 * i + k) * s.half + yi
                    line.append(
                        (1.0 - relaxation) * g_ref[par, r] - e_ref[par, r] + sums[k][par][yi]
                    )
                both.append(line)
            values.append(both)

        def keep(at, tile1):
            temp1[pl.ds(at * s.slots, s.slots), :] = tile1

        fine_restrict(s, values, i, keep)

    fine_block_sum(s, e_ref, x_ref, consume)
    share_out(s, temp1, share, lead)


def gather_shares(s, iy, shares, lead, spot):
    for t, ref in enumerate(shares):
        at = (iy ^ t) if s.ny & (s.ny - 1) == 0 else (iy + t) % s.ny
        start = pl.multiple_of(at * s.share, s.share)
        spot[pl.ds(start, s.share), :] = ref[lead, pl.ds(0, s.share), :]
    return [spot[pl.ds(r, s.slots1, stride=s.rows1), :] for r in range(s.rows1)]


def middle_sum(s, v, nx, ny, step):
    shape = v[0].shape
    sub = iota(shape, 0)
    first, last = sub == 0, sub == shape[0] - 1
    out = [None] * (nx * ny)
    for yi in range(ny):
        for xi, t in enumerate(plain_triple([v[x * ny + yi] for x in range(nx)])):
            out[xi * ny + yi] = t
    for xi in range(nx):
        line = out[xi * ny:(xi + 1) * ny]
        low = jnp.where(first, 0.0, roll(line[-1], 1, 0))
        high = jnp.where(last, 0.0, roll(line[0], -1, 0))
        out[xi * ny:(xi + 1) * ny] = triple(line, low, high)
    return [t + (roll(t, step, 1) + roll(t, -step, 1)) for t in out]


def middle_restrict(s, v):
    out = []
    for i in range(s.x1 // 2):
        for j in range(s.y1 // 2):
            t = (v[2 * i * s.y1 + 2 * j] + v[2 * i * s.y1 + 2 * j + 1]) + (
                v[(2 * i + 1) * s.y1 + 2 * j] + v[(2 * i + 1) * s.y1 + 2 * j + 1]
            )
            out.append(0.5 * (t + roll(t, -1, 1)))
    return out


def inside_columns(s, iz, shape):
    lanes = iota(shape, 1)
    below = jnp.where(iz < s.nz - 1, 3 * s.bz // 4, s.bz // 2)
    above = jnp.where(iz > 0, 3 * s.bz // 4, s.bz)
    return (lanes < below) | (lanes >= above)


def inside_chunks(s, iy, chunk):
    first = jnp.where(iy > 0, 0, 1)
    last = jnp.where(iy < s.ny - 1, 3, 2)
    return (chunk >= first) & (chunk <= last)


def middle_solve(s, g, d1, d2):
    keep = 1.0 - relaxation
    e0 = [d * t for d, t in zip(d1, g)]
    sums = middle_sum(s, e0, s.x1, s.y1, 1)
    g2 = middle_restrict(s, [keep * t - e + u for t, e, u in zip(g, e0, sums)])
    e = [d * t for d, t in zip(d2, g2)]
    for sweep in range(SWEEPS - 1):
        sums = middle_sum(s, e, s.x1 // 2, s.y1 // 2, 2)
        e = [keep * a + d * ((t - a) + u) for a, d, t, u in zip(e, d2, g2, sums)]
    spread = [a + roll(a, 1, 1) for a in e]
    e1 = [
        e0[x * s.y1 + y] + spread[(x // 2) * (s.y1 // 2) + y // 2]
        for x in range(s.x1)
        for y in range(s.y1)
    ]
    sums = middle_sum(s, e1, s.x1, s.y1, 1)
    return [keep * a + d * ((t - a) + u) for a, d, t, u in zip(e1, d1, g, sums)]


def to_fine(s, iy, e2):
    shape = (s.slots, s.bz)
    sub = iota(shape, 0)
    block = sub // 4
    chunk = sub % 4
    known = inside_chunks(s, iy, chunk)
    out = []
    per = s.bx // 2
    for x in range(per):
        for y in range(s.y1):
            total = jnp.zeros(shape, f32)
            for b in range(s.nx):
                v = e2[(b * per + x) * s.y1 + y]
                shift = (4 * b + 1 - 2 * iy) % s.slots1
                if s.slots1 < s.slots:
                    v = jnp.concatenate([v] * (s.slots // s.slots1), axis=0)
                v = pltpu.roll(v, shift, 0)[: s.slots]
                total = jnp.where(block == b, v, total)
            out.append(jnp.where(known, total, 0.0))
    return out


def second_half(s, g_ref, d_ref, q_ref, coarse, e_ref, x_ref, p_ref, image_store):
    for par in range(2):
        for xi in range(s.bx):
            for yi in range(s.half):
                r = xi * s.half + yi
                e_ref[par, r] = (
                    d_ref[par, r] * g_ref[par, r] + coarse[(xi // 2) * s.y1 + yi // 2]
                )

    def smooth(i, sums):
        for k in range(2):
            for par in range(2):
                for yi in range(s.half):
                    r = (2 * i + k) * s.half + yi
                    e = e_ref[par, r]
                    p_ref[par, r] = (1.0 - relaxation) * e + d_ref[par, r] * (
                        (g_ref[par, r] - e) + sums[k][par][yi]
                    )

    fine_block_sum(s, e_ref, x_ref, smooth)

    def apply(i, sums):
        for k in range(2):
            for par in range(2):
                for yi in range(s.half):
                    r = (2 * i + k) * s.half + yi
                    p = p_ref[par, r]
                    image_store(par, r, (q_ref[par, r] * p + p) - sums[k][par][yi])

    fine_block_sum(s, p_ref, x_ref, apply)


def second_kernel(s, place, *refs):
    shares = refs[: s.ny]
    g_ref, d_ref, q_ref, p_out, image_out, d1_out, d2_out, share = refs[s.ny:s.ny + 8]
    spot, temps, temp1 = refs[s.ny + 8:]
    iy, iz = place[1], place[2]
    g1 = gather_shares(s, iy, shares, 0, spot)
    c1 = gather_shares(s, iy, shares, 1, spot)
    shape = (s.slots1, s.bz)
    inside = inside_columns(s, iz, shape)
    inside2 = inside & (iota(shape, 1) % 2 == 0)
    d1 = [jnp.where(inside, relaxation / (26.0 + c), 0.0) for c in c1]
    d2 = [jnp.where(inside2, relaxation / (26.0 + c), 0.0) for c in middle_restrict(s, c1)]
    for r, d in enumerate(d1):
        d1_out[r] = d
    for r, d in enumerate(d2):
        d2_out[r] = d
    coarse = to_fine(s, iy, middle_solve(s, g1, d1, d2))
    e_ref, x_ref = temps.at[0], temps.at[1]

    def keep(par, r, value):
        image_out[par, r] = value

    second_half(s, g_ref, d_ref, q_ref, coarse, e_ref, x_ref, p_out, keep)
    shape = (s.slots, s.bz)
    chunk = iota(shape, 0) % 4
    own = (iota(shape, 1) < s.bz // 2) & (chunk > 0) & (chunk < 3)
    gammas = [jnp.zeros(shape, f32) for _ in range(4)]
    deltas = [jnp.zeros(shape, f32) for _ in range(4)]
    for par in range(2):
        for r in range(s.rows):
            p = p_out[par, r]
            gammas[r % 4] += g_ref[par, r] * p
            deltas[r % 4] += image_out[par, r] * p
    gamma = jnp.where(own, (gammas[0] + gammas[1]) + (gammas[2] + gammas[3]), 0.0)
    delta = jnp.where(own, (deltas[0] + deltas[1]) + (deltas[2] + deltas[3]), 0.0)
    share[0, pl.ds(s.share, s.slots), :] = gamma
    share[0, pl.ds(s.share + s.slots, s.slots), :] = delta
    first_half(s, image_out, d_ref, temps, temp1, share, 0)


def third_kernel(s, place, *refs):
    shares = refs[: s.ny]
    p_ref, g_ref, d_ref, q_ref, d1_ref, d2_ref = refs[s.ny:s.ny + 6]
    p_out, image_out, mw_out, nw_out = refs[s.ny + 6:s.ny + 10]
    spot, temps, flat, mw_ref = refs[s.ny + 10:]
    ix, iy = place[0], place[1]
    g1 = gather_shares(s, iy, shares, 0, spot)
    d1 = [d1_ref[r] for r in range(s.rows1)]
    d2 = [d2_ref[r] for r in range(s.rows1 // 4)]
    coarse = to_fine(s, iy, middle_solve(s, g1, d1, d2))
    e_ref, x_ref = temps.at[0], temps.at[1]

    def keep(par, r, value):
        flat[par, pl.ds(r * s.slots, s.slots), :] = value

    second_half(s, g_ref, d_ref, q_ref, coarse, e_ref, x_ref, mw_ref, keep)
    L = s.bz
    source = iota((L, L), 0)
    target = iota((L, L), 1)
    wanted = jnp.where(target % 2 == 0, target // 2, L // 2 + target // 2)
    selection = jnp.where(source == wanted, 1.0, 0.0).astype(jnp.bfloat16)
    left = iota((s.half, L), 1) < L // 2
    for ref, out in ((None, nw_out), (mw_ref, mw_out), (g_ref, image_out), (p_ref, p_out)):
        if ref is not None:
            for par in range(2):
                for r in range(s.rows):
                    flat[par, pl.ds(r * s.slots, s.slots), :] = ref[par, r]
        tiles = []
        for xi in range(s.bx):
            for h in range(2):
                at = xi * s.half * s.slots + ix * 4 + 1 + h
                even = flat[0, pl.ds(at, s.half, stride=s.slots), :]
                odd = flat[1, pl.ds(at, s.half, stride=s.slots), :]
                tiles.append(jnp.where(left, even, roll(odd, L // 2, 1)))
        whole = exact_dot(jnp.concatenate(tiles, axis=0), selection)
        for xi in range(s.bx):
            out[xi] = whole[xi * s.by:(xi + 1) * s.by]


def pairs(count):
    return (
        [(i, i ^ 1) for i in range(count) if (i ^ 1) < count],
        [(i, ((i + 1) ^ 1) - 1) for i in range(1, count) if ((i + 1) ^ 1) - 1 < count],
    )


def turns(count):
    if count & (count - 1) == 0:
        return [[(i ^ t, i) for i in range(count)] for t in range(1, count)]
    return [[((i + t) % count, i) for i in range(count)] for t in range(1, count)]


def shards(s, right_side, coefficient):
    L = s.bz
    ix, iy, iz = (lax.axis_index(a) for a in ("gx", "gy", "gz"))
    place = jnp.stack([ix, iy, iz]).astype(jnp.int32)
    smem = pl.BlockSpec(memory_space=pltpu.SMEM)
    vmem = pl.BlockSpec(memory_space=pltpu.VMEM)
    struct = lambda *shape: jax.ShapeDtypeStruct(shape, f32)
    params = pltpu.CompilerParams(vmem_limit_bytes=56 * 2**20)

    low = jnp.concatenate([right_side[:, :, : L // 2], coefficient[:, :, : L // 2]], axis=2)
    high = jnp.concatenate([right_side[:, :, L // 2:], coefficient[:, :, L // 2:]], axis=2)
    even_z = iz % 2 == 0
    send = (jnp.where(even_z, high, low), jnp.where(even_z, low, high))
    both = jnp.stack([right_side, coefficient])
    zpairs = pairs(s.nz)
    zside = [lax.ppermute(v, "gz", p) for v, p in zip(send, zpairs)]
    x_gc = []
    for turn in turns(s.nx):
        x_gc.append(lax.ppermute(both, "gx", turn))
        for v, p in zip(send, zpairs):
            crossed = [
                (a * s.nz + c, b * s.nz + d) for a, b in turn for c, d in p
            ]
            zside.append(lax.ppermute(v, ("gx", "gz"), crossed))

    def edge(rows):
        parts = []
        for t in range(s.nx):
            g, c = (right_side, coefficient) if t == 0 else (x_gc[t - 1][0], x_gc[t - 1][1])
            a, b = zside[2 * t], zside[2 * t + 1]
            parts.append(jnp.concatenate([g[:, rows], c[:, rows]], axis=1))
            parts.append(jnp.concatenate([a[:, rows], b[:, rows]], axis=1))
        return jnp.stack(parts).reshape(s.nx, 2, s.bx, 2 * HALO, L)

    first_rows, last_rows = edge(slice(0, HALO)), edge(slice(s.by - HALO, s.by))
    even_y = iy % 2 == 0
    ypairs = pairs(s.ny)
    y_a = lax.ppermute(jnp.where(even_y, last_rows, first_rows), "gy", ypairs[0])
    y_b = lax.ppermute(jnp.where(even_y, first_rows, last_rows), "gy", ypairs[1])

    fine = struct(2, s.rows, s.slots, L)
    fine_scratch = pltpu.VMEM((2, s.rows, s.slots, L), f32)
    temps = pltpu.VMEM((2, 2, s.rows, s.slots, L), f32)
    temp1 = pltpu.VMEM(((s.bx // 2) * s.y1 * s.slots, L), f32)
    g, d, q, share = pl.pallas_call(
        lambda *refs: first_kernel(s, *refs),
        out_shape=(fine, fine, fine, struct(2, s.share, L)),
        in_specs=[smem] + [vmem] * (2 + (s.nx - 1) + 2 * s.nx + 2),
        out_specs=(vmem,) * 4,
        scratch_shapes=[
            pltpu.VMEM((2, 4 * s.rows, 2 * L), f32),
            pltpu.VMEM((2, s.slots * s.rows, L), f32),
            pltpu.VMEM((2, s.slots * s.rows, L), f32),
            temps,
            temp1,
        ],
        compiler_params=params,
        name="widen",
    )(place, right_side, coefficient, *x_gc, *zside, y_a, y_b)

    spot = pltpu.VMEM((s.slots1 * s.rows1, L), f32)
    yturns = turns(s.ny)
    shares = [share] + [lax.ppermute(share, "gy", turn) for turn in yturns]
    p, image, d1, d2, share = pl.pallas_call(
        lambda *refs: second_kernel(s, *refs),
        out_shape=(
            fine,
            fine,
            struct(s.rows1, s.slots1, L),
            struct(s.rows1 // 4, s.slots1, L),
            struct(1, s.share + 2 * s.slots, L),
        ),
        in_specs=[smem] + [vmem] * (s.ny + 3),
        out_specs=(vmem,) * 5,
        scratch_shapes=[spot, temps, temp1],
        compiler_params=params,
        name="cycle",
    )(place, *shares, g, d, q)

    shares = [share] + [lax.ppermute(share, "gy", turn) for turn in yturns]
    sums = sum(v[0, s.share:] for v in shares)
    sums = sum([lax.ppermute(sums, "gz", turn) for turn in turns(s.nz)], sums)
    nat = struct(s.bx, s.by, L)
    p, image, mw, nw = pl.pallas_call(
        lambda *refs: third_kernel(s, *refs),
        out_shape=(nat,) * 4,
        in_specs=[smem] + [vmem] * (s.ny + 6),
        out_specs=(vmem,) * 4,
        scratch_shapes=[
            spot,
            temps,
            pltpu.VMEM((2, s.rows * s.slots, L), f32),
            fine_scratch,
        ],
        compiler_params=params,
        name="again",
    )(place, *shares, p, image, d, q, d1, d2)

    alpha = jnp.sum(sums[: s.slots]) / jnp.sum(sums[s.slots:])
    return (alpha * p, right_side - alpha * image, p - alpha * mw, image - alpha * nw)


def solution(mesh):
    spec = P("gx", "gy", "gz")
    count = [mesh.shape[a] for a in ("gx", "gy", "gz")]

    def body(right_side, coefficient):
        s = Shape(*count, right_side.shape)
        assert s.bx % 4 == 0 and s.by % 16 == 0 and s.bz % 128 == 0
        return shards(s, right_side, coefficient)

    return jax.shard_map(
        body, mesh=mesh, in_specs=(spec, spec), out_specs=(spec,) * 4, check_vma=False
    )
```

time: 378 us -> 64.7 us (0.17)
  waiting for transfers between devices: 147 us -> 11.8 us
  starting transfers between devices: 133 us -> 25.4 us
  blocking collectives: 41.1 us -> 0 us
  local copies, waits for them, and re-layouts: 30 us -> 5.78 us
  other arithmetic: 21 us -> 4.66 us
  Pallas kernels: 0 us -> 14.5 us
    ppermute x72 -> x16, waiting for transfers between devices: 147 us -> 11.8 us  [the longest x6 8.5 us: shards(): shares = [share] + [lax.ppermute(share, 'gy', turn) for turn in yturns]]
    ppermute x72 -> x16, starting transfers between devices: 133 us -> 25.4 us  [the longest x2 9.19 us: shards(): zside.append(lax.ppermute(v, ('gx', 'gz'), crossed))]
    psum x1 -> x0, blocking collectives: 41.1 us -> none  [shards(): lax.psum((jnp.sum(residual * precond), jnp.sum(image * precond)), ('gx',...]
    reshape x13 -> x0, local copies, waits for them, and re-layouts: 26.3 us -> none  [the longest x5 25.2 us: restrict(): values.reshape(extent[0] // 2, 2, extent[1] // 2, 2, extent[2] // 2, 2)]
    pallas_call x0 -> x3, Pallas kernels: none -> 14.5 us  [the longest x1 4.93 us: shards(): pl.pallas_call(lambda *refs: second_kernel(s, *refs), out_shape=(fine, fi...]
    reduce_sum x7 -> x1, other arithmetic: 10.9 us -> 0.67 us  [shards(): alpha = jnp.sum(sums[:s.slots]) / jnp.sum(sums[s.slots:])]
    unnamed x16 -> x36, local copies, waits for them, and re-layouts: 0.25 us -> 4.54 us
  transfers between devices with their start and end apart: 72 -> 16, of which waited for: 44 -> 7; matrix products, arithmetic and copies ran while one was open for 3% -> 1% of each run, Pallas kernels for 0% -> 7%
where the time goes in v1:
time: 64.7 us; the launch traced here: 64.3 us
  starting transfers between devices  25.4 us (39%)
  Pallas kernels  14.5 us (22%)
  waiting for transfers between devices  11.8 us (18%)
  local copies, waits for them, and re-layouts  5.78 us (9%)
  other arithmetic  4.66 us (7%)
  between operations  2.16 us (3%)
    ppermute x2, starting transfers between devices, shards(): zside.append(lax.ppermute(v, ('gx', 'gz'), crossed))  9.19 us
    ppermute x6, starting transfers between devices, shards(): shares = [share] + [lax.ppermute(share, 'gy', turn) for turn in yturns]  8.85 us
    ppermute x6, waiting for transfers between devices, shards(): shares = [share] + [lax.ppermute(share, 'gy', turn) for turn in yturns]  8.5 us
    pallas_call x1, Pallas kernels, shards(): pl.pallas_call(lambda *refs: second_kernel(s, *refs), out_shape=(fine, fi...  4.93 us
    pallas_call x1, Pallas kernels, shards(): pl.pallas_call(lambda *refs: first_kernel(s, *refs), out_shape=(fine, fin...  4.87 us
    pallas_call x1, Pallas kernels, shards(): pl.pallas_call(lambda *refs: third_kernel(s, *refs), out_shape=(nat,) * 4...  4.74 us
    unnamed x36, local copies, waits for them, and re-layouts  4.54 us
    ppermute x3, starting transfers between devices, shards(): sums = sum([lax.ppermute(sums, 'gz', turn) for turn in turns(s.nz)], sums)  4.39 us
  transfers between devices with their start and end apart: 16, of which 7 were waited for; matrix products, arithmetic and copies ran while one was open for 1% of the time, Pallas kernels for 7%

profile of v1, /device:TPU:0, one launch (start us, length us, event | category | flops | bytes accessed | tf_op | source)
XLA Modules:
  0.0 64.3 jit_solution(2082405625709401936)
XLA Ops:
  0.6 1.1 %fusion.11 = (f32[12,16,64]{2,1,0:T(8,128)S(1)}, f32[12,16,64]{2,1,0:T(8,128)S(1)}, f32[12,16,64]{2,1,0:T(8,128)S(1)}, f32[12,16,64]{2,1,0:T(8,128)S(1)}) fusion(f32[12,16,128]{2,1,0:T(8,128)} %refs_1_.1, f32[12,16,128]{2,1,0:T(8,128)} %refs_2_.1), kind=kLoop, calls=%fused_computation.39 | loop fusion | bytes 393216 | tf_op jit(solution)/shard_map/slice | solution.py:499
  1.8 0.0 copy-start
  1.8 0.0 copy-start.2
  1.8 0.1 broadcast_select_fusion
  1.9 0.7 %collective-permute-start.4 = (f32[12,16,128]{2,1,0:T(8,128)S(1)}, f32[12,16,128]{2,1,0:T(8,128)S(1)}, u32[]{:S(2)}, u32[]{:S(2)}) collective-permute-start(f32[12,16,128]{2,1,0:T(8,128)S(1)} %get-tuple-element.34), channel_id=1, source_target_pairs={{17,2},{18,1},{1,18},{2,17},{21,6},{22,5},{5,22},{6,21},{25,10},{2... | collective-permute-start | bytes 294920 | tf_op jit(solution)/shard_map/ppermute | solution.py:512
  2.6 0.7 %collective-permute-start.2 = (f32[12,16,128]{2,1,0:T(8,128)S(1)}, f32[12,16,128]{2,1,0:T(8,128)S(1)}, u32[]{:S(2)}, u32[]{:S(2)}) collective-permute-start(f32[12,16,128]{2,1,0:T(8,128)S(1)} %get-tuple-element.34), channel_id=1, source_target_pairs={{1,2},{2,1},{5,6},{6,5},{9,10},{10,9},{13,14},{14,13},{17,18},{18,... | collective-permute-start | bytes 294920 | tf_op jit(solution)/shard_map/ppermute | solution.py:504
  3.3 8.5 %collective-permute-start.3 = (f32[12,16,128]{2,1,0:T(8,128)S(1)}, f32[12,16,128]{2,1,0:T(8,128)S(1)}, u32[]{:S(2)}, u32[]{:S(2)}) collective-permute-start(f32[12,16,128]{2,1,0:T(8,128)S(1)} %get-tuple-element.35), channel_id=1, source_target_pairs={{16,1},{17,0},{18,3},{19,2},{0,17},{1,16},{2,19},{3,18},{20,5},{21... | collective-permute-start | bytes 294920 | tf_op jit(solution)/shard_map/ppermute | solution.py:512
  11.8 0.1 collective-permute-start.1
  11.9 0.0 copy-done
  11.9 0.0 copy-done.2
  12.0 1.5 %collective-permute-start = (f32[2,12,16,128]{3,2,1,0:T(8,128)S(1)}, f32[2,12,16,128]{3,2,1,0:T(8,128)S(1)}, u32[]{:S(2)}, u32[]{:S(2)}) collective-permute-start(f32[2,12,16,128]{3,2,1,0:T(8,128)S(1)} %pad_maximum_fusion), channel_id=1, source_target_pairs={{16,0},{0,16},{17,1},{1,17},{18,2},{2,18},{19,3},{3,19},{20,4},{4,... | collective-permute-start | bytes 589832 | tf_op jit(solution)/shard_map/ppermute | solution.py:507
  13.5 0.0 collective-permute-done.4.refs_7_
  13.5 0.0 copy-start.4
  13.5 1.0 %collective-permute-done.3.refs_6_ = f32[12,16,128]{2,1,0:T(8,128)S(1)} collective-permute-done((f32[12,16,128]{2,1,0:T(8,128)S(1)}, f32[12,16,128]{2,1,0:T(8,128)S(1)}, u32[]{:S(2)}, u32[]{:S(2)}) %collective-permute-start.3) | collective-permute-done | bytes 98336 | tf_op jit(solution)/shard_map/ppermute | solution.py:512
  14.5 0.0 copy-done.4
  14.6 0.6 copy-done.6
  15.1 0.0 collective-permute-done.2.refs_5_
  15.2 0.6 copy-done.5
  15.8 0.8 %collective-permute-done.1.refs_4_ = f32[12,16,128]{2,1,0:T(8,128)S(1)} collective-permute-done((f32[12,16,128]{2,1,0:T(8,128)S(1)}, f32[12,16,128]{2,1,0:T(8,128)S(1)}, u32[]{:S(2)}, u32[]{:S(2)}) %collective-permute-start.1) | collective-permute-done | bytes 98336 | tf_op jit(solution)/shard_map/ppermute | solution.py:504
  16.6 0.6 copy-done.7
  17.2 1.4 %collective-permute-done.refs_3_ = f32[2,12,16,128]{3,2,1,0:T(8,128)S(1)} collective-permute-done((f32[2,12,16,128]{3,2,1,0:T(8,128)S(1)}, f32[2,12,16,128]{3,2,1,0:T(8,128)S(1)}, u32[]{:S(2)}, u32[]{:S(2)}) %collective-permute-start) | collective-permute-done | bytes 196640 | tf_op jit(solution)/shard_map/ppermute | solution.py:507
  18.7 0.7 %copy-done.3 = f32[2,12,16,128]{3,2,1,0:T(8,128)} copy-done((f32[2,12,16,128]{3,2,1,0:T(8,128)}, f32[2,12,16,128]{3,2,1,0:T(8,128)S(1)}, u32[]{:S(2)}) %copy-start.3) | copy-done | bytes 196632
  19.4 0.1 collective-permute-start.5
  19.5 0.7 %collective-permute-start.6 = (f32[2,2,12,8,128]{4,3,2,1,0:T(8,128)S(1)}, f32[2,2,12,8,128]{4,3,2,1,0:T(8,128)S(1)}, u32[]{:S(2)}, u32[]{:S(2)}) collective-permute-start(f32[2,2,12,8,128]{4,3,2,1,0:T(8,128)S(1)} %bitcast.31), channel_id=1, source_target_pairs={{4,8},{8,4},{5,9},{9,5},{6,10},{10,6},{7,11},{11,7},{20,24},{24,20... | collective-permute-start | bytes 589832 | tf_op jit(solution)/shard_map/ppermute | solution.py:527
  20.2 0.6 pad_add_fusion.refs_0_
  20.8 0.1 collective-permute-done.5.refs_8_
  20.9 0.0 collective-permute-done.6.refs_9_
  20.9 0.7 %copy-done.8 = f32[2,2,12,8,128]{4,3,2,1,0:T(8,128)} copy-done((f32[2,2,12,8,128]{4,3,2,1,0:T(8,128)}, f32[2,2,12,8,128]{4,3,2,1,0:T(8,128)S(1)}, u32[]{:S(2)}) %copy-start.8) | copy-done | bytes 196632
  21.6 0.7 %copy-done.9 = f32[2,2,12,8,128]{4,3,2,1,0:T(8,128)} copy-done((f32[2,2,12,8,128]{4,3,2,1,0:T(8,128)}, f32[2,2,12,8,128]{4,3,2,1,0:T(8,128)S(1)}, u32[]{:S(2)}) %copy-start.9) | copy-done | bytes 196632
  22.3 4.9 %widen.1 = (f32[2,96,8,128]{3,2,1,0:T(8,128)}, f32[2,96,8,128]{3,2,1,0:T(8,128)}, f32[2,96,8,128]{3,2,1,0:T(8,128)}, f32[2,96,128]{2,1,0:T(8,128)}) custom-call(s32[3]{0:T(128)} %pad_add_fusion.refs_0_, f32[12,16,128]{2,1,0:T(8,128)} %refs_1_.1, f32[12,16,128]{2,1,0:T(8,128)} %refs_2_.1, f32[2,12,16,128]{3,2,1,0:T(8,128)} %copy-done.3, ...), custom_call_target="tpu_custom_call" | custom-call | tf_op jit(solution)/shard_map/widen/pallas_call | solution.py:533
  27.2 1.5 %collective-permute-start.9 = (f32[2,96,128]{2,1,0:T(8,128)}, f32[2,96,128]{2,1,0:T(8,128)S(1)}, u32[]{:S(2)}, u32[]{:S(2)}) collective-permute-start(f32[2,96,128]{2,1,0:T(8,128)} %get-tuple-element.17.refs_1_), channel_id=1, source_target_pairs={{12,0},{8,4},{4,8},{0,12},{13,1},{9,5},{5,9},{1,13},{14,2},{10,6},... | collective-permute-start | bytes 294920 | tf_op jit(solution)/shard_map/ppermute | solution.py:551
  28.6 5.5 %collective-permute-start.8 = (f32[2,96,128]{2,1,0:T(8,128)}, f32[2,96,128]{2,1,0:T(8,128)S(1)}, u32[]{:S(2)}, u32[]{:S(2)}) collective-permute-start(f32[2,96,128]{2,1,0:T(8,128)} %get-tuple-element.17.refs_1_), channel_id=1, source_target_pairs={{8,0},{12,4},{0,8},{4,12},{9,1},{13,5},{1,9},{5,13},{10,2},{14,6},... | collective-permute-start | bytes 294920 | tf_op jit(solution)/shard_map/ppermute | solution.py:551
  34.2 0.0 collective-permute-start.7
  34.2 0.0 collective-permute-done.9.refs_4_
  34.2 4.9 %collective-permute-done.8.refs_3_ = f32[2,96,128]{2,1,0:T(8,128)S(1)} collective-permute-done((f32[2,96,128]{2,1,0:T(8,128)}, f32[2,96,128]{2,1,0:T(8,128)S(1)}, u32[]{:S(2)}, u32[]{:S(2)}) %collective-permute-start.8) | collective-permute-done | bytes 98336 | tf_op jit(solution)/shard_map/ppermute | solution.py:551
  39.1 0.0 collective-permute-done.7.refs_2_
  39.1 0.0 copy-done.10
  39.1 0.6 copy-done.11
  39.7 0.0 copy-done.12
  39.7 4.9 %cycle.1 = (f32[2,96,8,128]{3,2,1,0:T(8,128)}, f32[2,96,8,128]{3,2,1,0:T(8,128)}, f32[48,8,128]{2,1,0:T(8,128)}, f32[12,8,128]{2,1,0:T(8,128)}, f32[1,112,128]{2,1,0:T(8,128)}) custom-call(s32[3]{0:T(128)} %pad_add_fusion.refs_0_, f32[2,96,128]{2,1,0:T(8,128)} %get-tuple-element.17.refs_1_, f32[2,96,128]{2,1,0:T(8,128)} %copy-done.12, ...), custom_call_target="tpu_custom_call" | custom-call | tf_op jit(solution)/shard_map/cycle/pallas_call | solution.py:552
  44.7 0.5 collective-permute-start.12
  45.1 0.8 %collective-permute-start.11 = (f32[1,112,128]{2,1,0:T(8,128)}, f32[1,112,128]{2,1,0:T(8,128)S(1)}, u32[]{:S(2)}, u32[]{:S(2)}) collective-permute-start(f32[1,112,128]{2,1,0:T(8,128)} %get-tuple-element.21.refs_1_), channel_id=1, source_target_pairs={{8,0},{12,4},{0,8},{4,12},{9,1},{13,5},{1,9},{5,13},{10,2},{14,6},... | collective-permute-start | bytes 172040 | tf_op jit(solution)/shard_map/ppermute | solution.py:568
  45.9 0.6 collective-permute-start.10
  46.5 2.4 %collective-permute-done.12.refs_4_ = f32[1,112,128]{2,1,0:T(8,128)S(1)} collective-permute-done((f32[1,112,128]{2,1,0:T(8,128)}, f32[1,112,128]{2,1,0:T(8,128)S(1)}, u32[]{:S(2)}, u32[]{:S(2)}) %collective-permute-start.12) | collective-permute-done | bytes 57376 | tf_op jit(solution)/shard_map/ppermute | solution.py:568
  48.9 1.2 %collective-permute-done.11.refs_3_ = f32[1,112,128]{2,1,0:T(8,128)S(1)} collective-permute-done((f32[1,112,128]{2,1,0:T(8,128)}, f32[1,112,128]{2,1,0:T(8,128)S(1)}, u32[]{:S(2)}, u32[]{:S(2)}) %collective-permute-start.11) | collective-permute-done | bytes 57376 | tf_op jit(solution)/shard_map/ppermute | solution.py:568
  50.1 0.0 collective-permute-done.10.refs_2_
  50.1 0.7 %fusion.2 = f32[16,128]{1,0:T(8,128)S(1)} fusion(f32[1,112,128]{2,1,0:T(8,128)S(1)} %collective-permute-done.12.refs_4_, f32[1,112,128]{2,1,0:T(8,128)S(1)} %collective-permute-done.11.refs_3_, f32[1,112,128]{2,1,0:T(8,128)S(1)} %collective-permute-done.10.refs_2_, f32[1,112,128]{2,1,0:T(8,128)} %get-tuple-element.21.refs_1_), kind=kLoop, calls=%fused_computation.24 | loop fusion | flops 6144 | bytes 40960 | tf_op jit(solution)/shard_map/add | solution.py:569
  50.9 2.5 %collective-permute-start.15 = (f32[16,128]{1,0:T(8,128)S(1)}, f32[16,128]{1,0:T(8,128)S(1)}, u32[]{:S(2)}, u32[]{:S(2)}) collective-permute-start(f32[16,128]{1,0:T(8,128)S(1)} %fusion.2), channel_id=1, source_target_pairs={{3,0},{2,1},{1,2},{0,3},{7,4},{6,5},{5,6},{4,7},{11,8},{10,9},{9,1... | collective-permute-start | bytes 24584 | tf_op jit(solution)/shard_map/ppermute | solution.py:570
  53.3 1.3 %collective-permute-start.14 = (f32[16,128]{1,0:T(8,128)S(1)}, f32[16,128]{1,0:T(8,128)S(1)}, u32[]{:S(2)}, u32[]{:S(2)}) collective-permute-start(f32[16,128]{1,0:T(8,128)S(1)} %fusion.2), channel_id=1, source_target_pairs={{2,0},{3,1},{0,2},{1,3},{6,4},{7,5},{4,6},{5,7},{10,8},{11,9},{8,1... | collective-permute-start | bytes 24584 | tf_op jit(solution)/shard_map/ppermute | solution.py:570
  54.6 0.6 collective-permute-start.13
  55.2 0.0 copy-done.15
  55.2 0.0 copy-done.16
  55.3 0.0 copy-done.17
  55.3 4.7 %again.1 = (f32[12,16,128]{2,1,0:T(8,128)}, f32[12,16,128]{2,1,0:T(8,128)}, f32[12,16,128]{2,1,0:T(8,128)}, f32[12,16,128]{2,1,0:T(8,128)}) custom-call(s32[3]{0:T(128)} %pad_add_fusion.refs_0_, f32[1,112,128]{2,1,0:T(8,128)} %get-tuple-element.21.refs_1_, f32[1,112,128]{2,1,0:T(8,128)} %copy-done.17, f32[1,112,128]{2,1,0:T(8,128)} %copy-done.16, ...), custom_call_target="tpu_custom_call" | custom-call | tf_op jit(solution)/shard_map/again/pallas_call | solution.py:572
  60.0 0.0 collective-permute-done.15
  60.0 0.0 collective-permute-done.14
  60.0 0.0 collective-permute-done.13
  60.0 0.7 %slice_reduce_fusion = (f32[]{:T(128)}, f32[]{:T(128)}) fusion(f32[16,128]{1,0:T(8,128)S(1)} %add_add_fusion), kind=kLoop, calls=%fused_computation.28 | loop fusion | flops 2046 | bytes 8200 | tf_op jit(solution)/shard_map/reduce_sum | solution.py:587
  61.9 0.0 copy-done.1
  61.9 0.0 copy-start.13
  62.0 0.0 copy-start.14
  62.0 1.7 %multiply_subtract_fusion = (f32[12,16,128]{2,1,0:T(8,128)}, f32[12,16,128]{2,1,0:T(8,128)}) fusion(f32[12,16,128]{2,1,0:T(8,128)} %get-tuple-element.27, f32[12,16,128]{2,1,0:T(8,128)} %get-tuple-element.29, f32[]{:T(128)S(6)} %div.3, f32[12,16,128]{2,1,0:T(8,128)S(1)} %copy-done.1), kind=kLoop, calls=%fused_computation.9 | loop fusion | flops 98304 | bytes 491524 | tf_op jit(solution)/shard_map/sub | solution.py:588
  63.6 0.0 copy-done.13
  63.7 0.7 %multiply_subtract_fusion.1 = (f32[12,16,128]{2,1,0:T(8,128)}, f32[12,16,128]{2,1,0:T(8,128)}) fusion(f32[12,16,128]{2,1,0:T(8,128)S(1)} %copy-done.13, f32[12,16,128]{2,1,0:T(8,128)S(1)} %copy-done.14, f32[]{:T(128)S(6)} %div.3), kind=kLoop, calls=%fused_computation.10 | loop fusion | flops 73728 | bytes 393220 | tf_op jit(solution)/shard_map/sub | solution.py:588
  (32 shorter events, 0.3 us)
Async XLA Ops:
  1.8 10.1 %copy-start = (f32[12,16,128]{2,1,0:T(8,128)S(1)}, f32[12,16,128]{2,1,0:T(8,128)}, u32[]{:S(2)}) copy-start(f32[12,16,128]{2,1,0:T(8,128)} %refs_1_.1) | copy-start | bytes 294916
  1.8 10.1 %copy-start.2 = (f32[12,16,128]{2,1,0:T(8,128)S(1)}, f32[12,16,128]{2,1,0:T(8,128)}, u32[]{:S(2)}) copy-start(f32[12,16,128]{2,1,0:T(8,128)} %refs_2_.1) | copy-start | bytes 294916
  1.9 11.5 %collective-permute-start.4 = (f32[12,16,128]{2,1,0:T(8,128)S(1)}, f32[12,16,128]{2,1,0:T(8,128)S(1)}, u32[]{:S(2)}, u32[]{:S(2)}) collective-permute-start(f32[12,16,128]{2,1,0:T(8,128)S(1)} %get-tuple-element.34), channel_id=1, source_target_pairs={{17,2},{18,1},{1,18},{2,17},{21,6},{22,5},{5,22},{6,21},{25,10},{2... | collective-permute-start | bytes 294920 | tf_op jit(solution)/shard_map/ppermute | solution.py:512
  2.6 12.5 %collective-permute-start.2 = (f32[12,16,128]{2,1,0:T(8,128)S(1)}, f32[12,16,128]{2,1,0:T(8,128)S(1)}, u32[]{:S(2)}, u32[]{:S(2)}) collective-permute-start(f32[12,16,128]{2,1,0:T(8,128)S(1)} %get-tuple-element.34), channel_id=1, source_target_pairs={{1,2},{2,1},{5,6},{6,5},{9,10},{10,9},{13,14},{14,13},{17,18},{18,... | collective-permute-start | bytes 294920 | tf_op jit(solution)/shard_map/ppermute | solution.py:504
  3.3 11.2 %collective-permute-start.3 = (f32[12,16,128]{2,1,0:T(8,128)S(1)}, f32[12,16,128]{2,1,0:T(8,128)S(1)}, u32[]{:S(2)}, u32[]{:S(2)}) collective-permute-start(f32[12,16,128]{2,1,0:T(8,128)S(1)} %get-tuple-element.35), channel_id=1, source_target_pairs={{16,1},{17,0},{18,3},{19,2},{0,17},{1,16},{2,19},{3,18},{20,5},{21... | collective-permute-start | bytes 294920 | tf_op jit(solution)/shard_map/ppermute | solution.py:512
  11.8 4.7 %collective-permute-start.1 = (f32[12,16,128]{2,1,0:T(8,128)S(1)}, f32[12,16,128]{2,1,0:T(8,128)S(1)}, u32[]{:S(2)}, u32[]{:S(2)}) collective-permute-start(f32[12,16,128]{2,1,0:T(8,128)S(1)} %get-tuple-element.35), channel_id=1, source_target_pairs={{0,1},{1,0},{2,3},{3,2},{4,5},{5,4},{6,7},{7,6},{8,9},{9,8},{10,11... | collective-permute-start | bytes 294920 | tf_op jit(solution)/shard_map/ppermute | solution.py:504
  12.0 6.7 %collective-permute-start = (f32[2,12,16,128]{3,2,1,0:T(8,128)S(1)}, f32[2,12,16,128]{3,2,1,0:T(8,128)S(1)}, u32[]{:S(2)}, u32[]{:S(2)}) collective-permute-start(f32[2,12,16,128]{3,2,1,0:T(8,128)S(1)} %pad_maximum_fusion), channel_id=1, source_target_pairs={{16,0},{0,16},{17,1},{1,17},{18,2},{2,18},{19,3},{3,19},{20,4},{4,... | collective-permute-start | bytes 589832 | tf_op jit(solution)/shard_map/ppermute | solution.py:507
  13.5 1.0 %copy-start.4 = (f32[12,16,128]{2,1,0:T(8,128)}, f32[12,16,128]{2,1,0:T(8,128)S(1)}, u32[]{:S(2)}) copy-start(f32[12,16,128]{2,1,0:T(8,128)S(1)} %collective-permute-done.4.refs_7_) | copy-start | bytes 294916
  14.5 0.6 copy-start.6
  15.2 0.6 copy-start.5
  16.6 0.6 copy-start.7
  18.6 0.7 %copy-start.3 = (f32[2,12,16,128]{3,2,1,0:T(8,128)}, f32[2,12,16,128]{3,2,1,0:T(8,128)S(1)}, u32[]{:S(2)}) copy-start(f32[2,12,16,128]{3,2,1,0:T(8,128)S(1)} %collective-permute-done.refs_3_) | copy-start | bytes 589828
  19.4 1.5 %collective-permute-start.5 = (f32[2,2,12,8,128]{4,3,2,1,0:T(8,128)S(1)}, f32[2,2,12,8,128]{4,3,2,1,0:T(8,128)S(1)}, u32[]{:S(2)}, u32[]{:S(2)}) collective-permute-start(f32[2,2,12,8,128]{4,3,2,1,0:T(8,128)S(1)} %bitcast.32), channel_id=1, source_target_pairs={{0,4},{4,0},{8,12},{12,8},{1,5},{5,1},{9,13},{13,9},{2,6},{6,2},{1... | collective-permute-start | bytes 589832 | tf_op jit(solution)/shard_map/ppermute | solution.py:526
  19.5 1.4 %collective-permute-start.6 = (f32[2,2,12,8,128]{4,3,2,1,0:T(8,128)S(1)}, f32[2,2,12,8,128]{4,3,2,1,0:T(8,128)S(1)}, u32[]{:S(2)}, u32[]{:S(2)}) collective-permute-start(f32[2,2,12,8,128]{4,3,2,1,0:T(8,128)S(1)} %bitcast.31), channel_id=1, source_target_pairs={{4,8},{8,4},{5,9},{9,5},{6,10},{10,6},{7,11},{11,7},{20,24},{24,20... | collective-permute-start | bytes 589832 | tf_op jit(solution)/shard_map/ppermute | solution.py:527
  20.9 0.7 %copy-start.8 = (f32[2,2,12,8,128]{4,3,2,1,0:T(8,128)}, f32[2,2,12,8,128]{4,3,2,1,0:T(8,128)S(1)}, u32[]{:S(2)}) copy-start(f32[2,2,12,8,128]{4,3,2,1,0:T(8,128)S(1)} %collective-permute-done.5.refs_8_) | copy-start | bytes 589828
  21.6 0.7 %copy-start.9 = (f32[2,2,12,8,128]{4,3,2,1,0:T(8,128)}, f32[2,2,12,8,128]{4,3,2,1,0:T(8,128)S(1)}, u32[]{:S(2)}) copy-start(f32[2,2,12,8,128]{4,3,2,1,0:T(8,128)S(1)} %collective-permute-done.6.refs_9_) | copy-start | bytes 589828
  27.2 7.0 %collective-permute-start.9 = (f32[2,96,128]{2,1,0:T(8,128)}, f32[2,96,128]{2,1,0:T(8,128)S(1)}, u32[]{:S(2)}, u32[]{:S(2)}) collective-permute-start(f32[2,96,128]{2,1,0:T(8,128)} %get-tuple-element.17.refs_1_), channel_id=1, source_target_pairs={{12,0},{8,4},{4,8},{0,12},{13,1},{9,5},{5,9},{1,13},{14,2},{10,6},... | collective-permute-start | bytes 294920 | tf_op jit(solution)/shard_map/ppermute | solution.py:551
  28.6 10.4 %collective-permute-start.8 = (f32[2,96,128]{2,1,0:T(8,128)}, f32[2,96,128]{2,1,0:T(8,128)S(1)}, u32[]{:S(2)}, u32[]{:S(2)}) collective-permute-start(f32[2,96,128]{2,1,0:T(8,128)} %get-tuple-element.17.refs_1_), channel_id=1, source_target_pairs={{8,0},{12,4},{0,8},{4,12},{9,1},{13,5},{1,9},{5,13},{10,2},{14,6},... | collective-permute-start | bytes 294920 | tf_op jit(solution)/shard_map/ppermute | solution.py:551
  34.2 4.9 %collective-permute-start.7 = (f32[2,96,128]{2,1,0:T(8,128)}, f32[2,96,128]{2,1,0:T(8,128)S(1)}, u32[]{:S(2)}, u32[]{:S(2)}) collective-permute-start(f32[2,96,128]{2,1,0:T(8,128)} %get-tuple-element.17.refs_1_), channel_id=1, source_target_pairs={{4,0},{0,4},{12,8},{8,12},{5,1},{1,5},{13,9},{9,13},{6,2},{2,6},{1... | collective-permute-start | bytes 294920 | tf_op jit(solution)/shard_map/ppermute | solution.py:551
  34.2 4.9 %copy-start.10 = (f32[2,96,128]{2,1,0:T(8,128)}, f32[2,96,128]{2,1,0:T(8,128)S(1)}, u32[]{:S(2)}) copy-start(f32[2,96,128]{2,1,0:T(8,128)S(1)} %collective-permute-done.9.refs_4_) | copy-start | bytes 294916
  39.1 0.6 copy-start.11
  39.1 0.7 %copy-start.12 = (f32[2,96,128]{2,1,0:T(8,128)}, f32[2,96,128]{2,1,0:T(8,128)S(1)}, u32[]{:S(2)}) copy-start(f32[2,96,128]{2,1,0:T(8,128)S(1)} %collective-permute-done.7.refs_2_) | copy-start | bytes 294916
  44.7 4.2 %collective-permute-start.12 = (f32[1,112,128]{2,1,0:T(8,128)}, f32[1,112,128]{2,1,0:T(8,128)S(1)}, u32[]{:S(2)}, u32[]{:S(2)}) collective-permute-start(f32[1,112,128]{2,1,0:T(8,128)} %get-tuple-element.21.refs_1_), channel_id=1, source_target_pairs={{12,0},{8,4},{4,8},{0,12},{13,1},{9,5},{5,9},{1,13},{14,2},{10,6},... | collective-permute-start | bytes 172040 | tf_op jit(solution)/shard_map/ppermute | solution.py:568
  45.1 5.0 %collective-permute-start.11 = (f32[1,112,128]{2,1,0:T(8,128)}, f32[1,112,128]{2,1,0:T(8,128)S(1)}, u32[]{:S(2)}, u32[]{:S(2)}) collective-permute-start(f32[1,112,128]{2,1,0:T(8,128)} %get-tuple-element.21.refs_1_), channel_id=1, source_target_pairs={{8,0},{12,4},{0,8},{4,12},{9,1},{13,5},{1,9},{5,13},{10,2},{14,6},... | collective-permute-start | bytes 172040 | tf_op jit(solution)/shard_map/ppermute | solution.py:568
  45.9 4.2 %collective-permute-start.10 = (f32[1,112,128]{2,1,0:T(8,128)}, f32[1,112,128]{2,1,0:T(8,128)S(1)}, u32[]{:S(2)}, u32[]{:S(2)}) collective-permute-start(f32[1,112,128]{2,1,0:T(8,128)} %get-tuple-element.21.refs_1_), channel_id=1, source_target_pairs={{4,0},{0,4},{12,8},{8,12},{5,1},{1,5},{13,9},{9,13},{6,2},{2,6},{1... | collective-permute-start | bytes 172040 | tf_op jit(solution)/shard_map/ppermute | solution.py:568
  48.9 6.3 %copy-start.15 = (f32[1,112,128]{2,1,0:T(8,128)}, f32[1,112,128]{2,1,0:T(8,128)S(1)}, u32[]{:S(2)}) copy-start(f32[1,112,128]{2,1,0:T(8,128)S(1)} %collective-permute-done.12.refs_4_) | copy-start | bytes 172036
  50.1 5.1 %copy-start.16 = (f32[1,112,128]{2,1,0:T(8,128)}, f32[1,112,128]{2,1,0:T(8,128)S(1)}, u32[]{:S(2)}) copy-start(f32[1,112,128]{2,1,0:T(8,128)S(1)} %collective-permute-done.11.refs_3_) | copy-start | bytes 172036
  50.1 5.1 %copy-start.17 = (f32[1,112,128]{2,1,0:T(8,128)}, f32[1,112,128]{2,1,0:T(8,128)S(1)}, u32[]{:S(2)}) copy-start(f32[1,112,128]{2,1,0:T(8,128)S(1)} %collective-permute-done.10.refs_2_) | copy-start | bytes 172036
  50.9 9.1 %collective-permute-start.15 = (f32[16,128]{1,0:T(8,128)S(1)}, f32[16,128]{1,0:T(8,128)S(1)}, u32[]{:S(2)}, u32[]{:S(2)}) collective-permute-start(f32[16,128]{1,0:T(8,128)S(1)} %fusion.2), channel_id=1, source_target_pairs={{3,0},{2,1},{1,2},{0,3},{7,4},{6,5},{5,6},{4,7},{11,8},{10,9},{9,1... | collective-permute-start | bytes 24584 | tf_op jit(solution)/shard_map/ppermute | solution.py:570
  53.3 6.7 %collective-permute-start.14 = (f32[16,128]{1,0:T(8,128)S(1)}, f32[16,128]{1,0:T(8,128)S(1)}, u32[]{:S(2)}, u32[]{:S(2)}) collective-permute-start(f32[16,128]{1,0:T(8,128)S(1)} %fusion.2), channel_id=1, source_target_pairs={{2,0},{3,1},{0,2},{1,3},{6,4},{7,5},{4,6},{5,7},{10,8},{11,9},{8,1... | collective-permute-start | bytes 24584 | tf_op jit(solution)/shard_map/ppermute | solution.py:570
  54.6 5.4 %collective-permute-start.13 = (f32[16,128]{1,0:T(8,128)S(1)}, f32[16,128]{1,0:T(8,128)S(1)}, u32[]{:S(2)}, u32[]{:S(2)}) collective-permute-start(f32[16,128]{1,0:T(8,128)S(1)} %fusion.2), channel_id=1, source_target_pairs={{1,0},{0,1},{3,2},{2,3},{5,4},{4,5},{7,6},{6,7},{9,8},{8,9},{11,10... | collective-permute-start | bytes 24584 | tf_op jit(solution)/shard_map/ppermute | solution.py:570
  55.3 6.7 %copy-start.1 = (f32[12,16,128]{2,1,0:T(8,128)S(1)}, f32[12,16,128]{2,1,0:T(8,128)}, u32[]{:S(2)}) copy-start(f32[12,16,128]{2,1,0:T(8,128)} %refs_1_.1) | copy-start | bytes 294916
  61.9 1.7 %copy-start.13 = (f32[12,16,128]{2,1,0:T(8,128)S(1)}, f32[12,16,128]{2,1,0:T(8,128)}, u32[]{:S(2)}) copy-start(f32[12,16,128]{2,1,0:T(8,128)} %get-tuple-element.26) | copy-start | bytes 294916
  62.0 1.7 %copy-start.14 = (f32[12,16,128]{2,1,0:T(8,128)S(1)}, f32[12,16,128]{2,1,0:T(8,128)}, u32[]{:S(2)}) copy-start(f32[12,16,128]{2,1,0:T(8,128)} %get-tuple-element.28) | copy-start | bytes 294916

commit v2 on v1

--- a/solution.py
+++ b/solution.py
@@ -436,9 +436,11 @@
 
 def third_kernel(s, place, *refs):
     shares = refs[: s.ny]
-    p_ref, g_ref, d_ref, q_ref, d1_ref, d2_ref = refs[s.ny:s.ny + 6]
-    p_out, image_out, mw_out, nw_out = refs[s.ny + 6:s.ny + 10]
-    spot, temps, flat, mw_ref = refs[s.ny + 10:]
+    sums = refs[s.ny:s.ny + s.nz]
+    refs = refs[s.ny + s.nz:]
+    right, p_ref, g_ref, d_ref, q_ref, d1_ref, d2_ref = refs[:7]
+    outs = refs[7:11]
+    spot, temps, flat, mw_ref = refs[11:]
     ix, iy = place[0], place[1]
     g1 = gather_shares(s, iy, shares, 0, spot)
     d1 = [d1_ref[r] for r in range(s.rows1)]
@@ -456,7 +458,14 @@
     wanted = jnp.where(target % 2 == 0, target // 2, L // 2 + target // 2)
     selection = jnp.where(source == wanted, 1.0, 0.0).astype(jnp.bfloat16)
     left = iota((s.half, L), 1) < L // 2
-    for ref, out in ((None, nw_out), (mw_ref, mw_out), (g_ref, image_out), (p_ref, p_out)):
+    total = sums[0][...]
+    for v in sums[1:]:
+        total = total + v[...]
+    gamma = jnp.sum(total[: s.slots], keepdims=True)
+    delta = jnp.sum(total[s.slots:], keepdims=True)
+    alpha = gamma / delta
+    natural = []
+    for ref in (None, mw_ref, g_ref, p_ref):
         if ref is not None:
             for par in range(2):
                 for r in range(s.rows):
@@ -468,9 +477,14 @@
                 even = flat[0, pl.ds(at, s.half, stride=s.slots), :]
                 odd = flat[1, pl.ds(at, s.half, stride=s.slots), :]
                 tiles.append(jnp.where(left, even, roll(odd, L // 2, 1)))
-        whole = exact_dot(jnp.concatenate(tiles, axis=0), selection)
-        for xi in range(s.bx):
-            out[xi] = whole[xi * s.by:(xi + 1) * s.by]
+        natural.append(exact_dot(jnp.concatenate(tiles, axis=0), selection))
+    nw, mw, image, p = natural
+    for xi in range(s.bx):
+        at = slice(xi * s.by, (xi + 1) * s.by)
+        outs[0][xi] = alpha * p[at]
+        outs[1][xi] = right[xi] - alpha * image[at]
+        outs[2][xi] = p[at] - alpha * mw[at]
+        outs[3][xi] = image[at] - alpha * nw[at]
 
 
 def pairs(count):
@@ -493,7 +507,7 @@
     smem = pl.BlockSpec(memory_space=pltpu.SMEM)
     vmem = pl.BlockSpec(memory_space=pltpu.VMEM)
     struct = lambda *shape: jax.ShapeDtypeStruct(shape, f32)
-    params = pltpu.CompilerParams(vmem_limit_bytes=56 * 2**20)
+    params = pltpu.CompilerParams(vmem_limit_bytes=16 * 4 * 2 * s.rows * s.slots * L)
 
     low = jnp.concatenate([right_side[:, :, : L // 2], coefficient[:, :, : L // 2]], axis=2)
     high = jnp.concatenate([right_side[:, :, L // 2:], coefficient[:, :, L // 2:]], axis=2)
@@ -567,12 +581,11 @@
 
     shares = [share] + [lax.ppermute(share, "gy", turn) for turn in yturns]
     sums = sum(v[0, s.share:] for v in shares)
-    sums = sum([lax.ppermute(sums, "gz", turn) for turn in turns(s.nz)], sums)
-    nat = struct(s.bx, s.by, L)
-    p, image, mw, nw = pl.pallas_call(
+    sums = [sums] + [lax.ppermute(sums, "gz", turn) for turn in turns(s.nz)]
+    return pl.pallas_call(
         lambda *refs: third_kernel(s, *refs),
-        out_shape=(nat,) * 4,
-        in_specs=[smem] + [vmem] * (s.ny + 6),
+        out_shape=(struct(s.bx, s.by, L),) * 4,
+        in_specs=[smem] + [vmem] * (s.ny + s.nz + 7),
         out_specs=(vmem,) * 4,
         scratch_shapes=[
             spot,
@@ -582,10 +595,7 @@
         ],
         compiler_params=params,
         name="again",
-    )(place, *shares, p, image, d, q, d1, d2)
-
-    alpha = jnp.sum(sums[: s.slots]) / jnp.sum(sums[s.slots:])
-    return (alpha * p, right_side - alpha * image, p - alpha * mw, image - alpha * nw)
+    )(place, *shares, *sums, right_side, p, image, d, q, d1, d2)
 
 
 def solution(mesh):

time: 64.7 us -> 55 us (0.85)
  Pallas kernels: 14.5 us -> 9.13 us
  local copies, waits for them, and re-layouts: 5.78 us -> 1.26 us
  waiting for transfers between devices: 11.8 us -> 16.3 us
  other arithmetic: 4.66 us -> 0.36 us
  starting transfers between devices: 25.4 us -> 26.9 us
  between operations: 2.16 us -> 0.88 us
    unnamed x36 -> x4, local copies, waits for them, and re-layouts: 4.54 us -> 0.01 us
    ppermute x3, waiting for transfers between devices: 0.01 us -> 3.03 us  [shards(): sums = [sums] + [lax.ppermute(sums, 'gz', turn) for turn in turns(s.nz)]]
    sub x2 -> x0, other arithmetic: 2.37 us -> none  [the longest x1 1.68 us: shards(): image - alpha * nw]
    pallas_call x1, Pallas kernels: 4.93 us -> 2.82 us  [shards(): pl.pallas_call(lambda *refs: second_kernel(s, *refs), out_shape=(fine, fi...]
    pallas_call x1, Pallas kernels: 4.87 us -> 2.84 us  [shards(): pl.pallas_call(lambda *refs: first_kernel(s, *refs), out_shape=(fine, fin...]
    ppermute x6, starting transfers between devices: 8.85 us -> 10.3 us  [shards(): shares = [share] + [lax.ppermute(share, 'gy', turn) for turn in yturns]]
    pallas_call x1, Pallas kernels: 4.74 us -> 3.47 us  [shards(): pl.pallas_call(lambda *refs: third_kernel(s, *refs), out_shape=(struct(s....]
    ppermute x2, waiting for transfers between devices: 0.76 us -> 1.96 us  [shards(): zside = [lax.ppermute(v, 'gz', p) for v, p in zip(send, zpairs)]]
  transfers between devices with their start and end apart: 16 -> 16, of which waited for: 7 -> 10; matrix products, arithmetic and copies ran while one was open for 1% -> 0% of each run, Pallas kernels for 7% -> 0%
where the time goes in v2:
time: 55 us; the launch traced here: 54.8 us
  starting transfers between devices  26.9 us (49%)
  waiting for transfers between devices  16.3 us (30%)
  Pallas kernels  9.13 us (17%)
  local copies, waits for them, and re-layouts  1.26 us (2%)
  between operations  0.88 us (2%)
    ppermute x6, starting transfers between devices, shards(): shares = [share] + [lax.ppermute(share, 'gy', turn) for turn in yturns]  10.3 us
    ppermute x2, starting transfers between devices, shards(): zside.append(lax.ppermute(v, ('gx', 'gz'), crossed))  9.19 us
    ppermute x6, waiting for transfers between devices, shards(): shares = [share] + [lax.ppermute(share, 'gy', turn) for turn in yturns]  7.62 us
    ppermute x3, starting transfers between devices, shards(): sums = [sums] + [lax.ppermute(sums, 'gz', turn) for turn in turns(s.nz)]  4.45 us
    pallas_call x1, Pallas kernels, shards(): pl.pallas_call(lambda *refs: third_kernel(s, *refs), out_shape=(struct(s....  3.47 us
    ppermute x3, waiting for transfers between devices, shards(): sums = [sums] + [lax.ppermute(sums, 'gz', turn) for turn in turns(s.nz)]  3.03 us
    pallas_call x1, Pallas kernels, shards(): pl.pallas_call(lambda *refs: first_kernel(s, *refs), out_shape=(fine, fin...  2.84 us
    pallas_call x1, Pallas kernels, shards(): pl.pallas_call(lambda *refs: second_kernel(s, *refs), out_shape=(fine, fi...  2.82 us
  transfers between devices with their start and end apart: 16, of which 10 were waited for; matrix products, arithmetic and copies ran while one was open for 0% of the time, Pallas kernels for 0%

profile of v2, /device:TPU:0, one launch (start us, length us, event | category | flops | bytes accessed | tf_op | source)
XLA Modules:
  0.0 54.8 jit_solution(5097423406794080822)
XLA Ops:
  0.6 1.1 %fusion.11 = (f32[12,16,64]{2,1,0:T(8,128)S(1)}, f32[12,16,64]{2,1,0:T(8,128)S(1)}, f32[12,16,64]{2,1,0:T(8,128)S(1)}, f32[12,16,64]{2,1,0:T(8,128)S(1)}) fusion(f32[12,16,128]{2,1,0:T(8,128)} %refs_9_.1, f32[12,16,128]{2,1,0:T(8,128)} %refs_2_.1), kind=kLoop, calls=%fused_computation.32 | loop fusion | bytes 393216 | tf_op jit(solution)/shard_map/slice | solution.py:513
  1.8 0.0 copy-start
  1.8 0.0 copy-start.1
  1.8 0.1 broadcast_select_fusion
  1.9 0.7 %collective-permute-start.4 = (f32[12,16,128]{2,1,0:T(8,128)S(1)}, f32[12,16,128]{2,1,0:T(8,128)S(1)}, u32[]{:S(2)}, u32[]{:S(2)}) collective-permute-start(f32[12,16,128]{2,1,0:T(8,128)S(1)} %get-tuple-element.24), channel_id=1, source_target_pairs={{17,2},{18,1},{1,18},{2,17},{21,6},{22,5},{5,22},{6,21},{25,10},{2... | collective-permute-start | bytes 294920 | tf_op jit(solution)/shard_map/ppermute | solution.py:526
  2.6 0.7 %collective-permute-start.2 = (f32[12,16,128]{2,1,0:T(8,128)S(1)}, f32[12,16,128]{2,1,0:T(8,128)S(1)}, u32[]{:S(2)}, u32[]{:S(2)}) collective-permute-start(f32[12,16,128]{2,1,0:T(8,128)S(1)} %get-tuple-element.24), channel_id=1, source_target_pairs={{1,2},{2,1},{5,6},{6,5},{9,10},{10,9},{13,14},{14,13},{17,18},{18,... | collective-permute-start | bytes 294920 | tf_op jit(solution)/shard_map/ppermute | solution.py:518
  3.3 8.5 %collective-permute-start.3 = (f32[12,16,128]{2,1,0:T(8,128)S(1)}, f32[12,16,128]{2,1,0:T(8,128)S(1)}, u32[]{:S(2)}, u32[]{:S(2)}) collective-permute-start(f32[12,16,128]{2,1,0:T(8,128)S(1)} %get-tuple-element.25), channel_id=1, source_target_pairs={{16,1},{17,0},{18,3},{19,2},{0,17},{1,16},{2,19},{3,18},{20,5},{21... | collective-permute-start | bytes 294920 | tf_op jit(solution)/shard_map/ppermute | solution.py:526
  11.8 0.1 collective-permute-start.1
  11.9 0.0 copy-done
  11.9 0.0 copy-done.1
  12.0 1.5 %collective-permute-start = (f32[2,12,16,128]{3,2,1,0:T(8,128)S(1)}, f32[2,12,16,128]{3,2,1,0:T(8,128)S(1)}, u32[]{:S(2)}, u32[]{:S(2)}) collective-permute-start(f32[2,12,16,128]{3,2,1,0:T(8,128)S(1)} %pad_maximum_fusion), channel_id=1, source_target_pairs={{16,0},{0,16},{17,1},{1,17},{18,2},{2,18},{19,3},{3,19},{20,4},{4,... | collective-permute-start | bytes 589832 | tf_op jit(solution)/shard_map/ppermute | solution.py:521
  13.5 0.0 collective-permute-done.4.refs_7_
  13.5 1.0 %collective-permute-done.3.refs_6_ = f32[12,16,128]{2,1,0:T(8,128)S(1)} collective-permute-done((f32[12,16,128]{2,1,0:T(8,128)S(1)}, f32[12,16,128]{2,1,0:T(8,128)S(1)}, u32[]{:S(2)}, u32[]{:S(2)}) %collective-permute-start.3) | collective-permute-done | bytes 98336 | tf_op jit(solution)/shard_map/ppermute | solution.py:526
  14.5 0.0 collective-permute-done.2.refs_5_
  14.6 2.0 %collective-permute-done.1.refs_4_ = f32[12,16,128]{2,1,0:T(8,128)S(1)} collective-permute-done((f32[12,16,128]{2,1,0:T(8,128)S(1)}, f32[12,16,128]{2,1,0:T(8,128)S(1)}, u32[]{:S(2)}, u32[]{:S(2)}) %collective-permute-start.1) | collective-permute-done | bytes 98336 | tf_op jit(solution)/shard_map/ppermute | solution.py:518
  16.6 2.0 %collective-permute-done.refs_3_ = f32[2,12,16,128]{3,2,1,0:T(8,128)S(1)} collective-permute-done((f32[2,12,16,128]{3,2,1,0:T(8,128)S(1)}, f32[2,12,16,128]{3,2,1,0:T(8,128)S(1)}, u32[]{:S(2)}, u32[]{:S(2)}) %collective-permute-start) | collective-permute-done | bytes 196640 | tf_op jit(solution)/shard_map/ppermute | solution.py:521
  18.8 0.1 collective-permute-start.5
  18.8 0.7 %collective-permute-start.6 = (f32[2,2,12,8,128]{4,3,2,1,0:T(8,128)S(1)}, f32[2,2,12,8,128]{4,3,2,1,0:T(8,128)S(1)}, u32[]{:S(2)}, u32[]{:S(2)}) collective-permute-start(f32[2,2,12,8,128]{4,3,2,1,0:T(8,128)S(1)} %bitcast.31), channel_id=1, source_target_pairs={{4,8},{8,4},{5,9},{9,5},{6,10},{10,6},{7,11},{11,7},{20,24},{24,20... | collective-permute-start | bytes 589832 | tf_op jit(solution)/shard_map/ppermute | solution.py:541
  19.5 0.1 pad_add_fusion.refs_0_
  19.6 0.7 %collective-permute-done.5.refs_8_ = f32[2,2,12,8,128]{4,3,2,1,0:T(8,128)S(1)} collective-permute-done((f32[2,2,12,8,128]{4,3,2,1,0:T(8,128)S(1)}, f32[2,2,12,8,128]{4,3,2,1,0:T(8,128)S(1)}, u32[]{:S(2)}, u32[]{:S(2)}) %collective-permute-start.5) | collective-permute-done | bytes 196640 | tf_op jit(solution)/shard_map/ppermute | solution.py:540
  20.3 0.0 collective-permute-done.6.refs_9_
  20.3 2.8 %widen.1 = (f32[2,96,8,128]{3,2,1,0:T(8,128)S(1)}, f32[2,96,8,128]{3,2,1,0:T(8,128)S(1)}, f32[2,96,8,128]{3,2,1,0:T(8,128)S(1)}, f32[2,96,128]{2,1,0:T(8,128)S(1)}) custom-call(s32[3]{0:T(128)S(1)} %pad_add_fusion.refs_0_, f32[12,16,128]{2,1,0:T(8,128)S(1)} %copy-done, f32[12,16,128]{2,1,0:T(8,128)S(1)} %copy-done.1, ...), custom_call_target="tpu_custom_call" | custom-call | tf_op jit(solution)/shard_map/widen/pallas_call | solution.py:547
  23.1 1.3 %collective-permute-start.9 = (f32[2,96,128]{2,1,0:T(8,128)S(1)}, f32[2,96,128]{2,1,0:T(8,128)S(1)}, u32[]{:S(2)}, u32[]{:S(2)}) collective-permute-start(f32[2,96,128]{2,1,0:T(8,128)S(1)} %get-tuple-element.13.refs_1_), channel_id=1, source_target_pairs={{12,0},{8,4},{4,8},{0,12},{13,1},{9,5},{5,9},{1,13},{14,2},{10,6},... | collective-permute-start | bytes 294920 | tf_op jit(solution)/shard_map/ppermute | solution.py:565
  24.4 7.0 %collective-permute-start.8 = (f32[2,96,128]{2,1,0:T(8,128)S(1)}, f32[2,96,128]{2,1,0:T(8,128)S(1)}, u32[]{:S(2)}, u32[]{:S(2)}) collective-permute-start(f32[2,96,128]{2,1,0:T(8,128)S(1)} %get-tuple-element.13.refs_1_), channel_id=1, source_target_pairs={{8,0},{12,4},{0,8},{4,12},{9,1},{13,5},{1,9},{5,13},{10,2},{14,6},... | collective-permute-start | bytes 294920 | tf_op jit(solution)/shard_map/ppermute | solution.py:565
  31.5 0.0 collective-permute-start.7
  31.5 0.0 collective-permute-done.9.refs_4_
  31.5 4.6 %collective-permute-done.8.refs_3_ = f32[2,96,128]{2,1,0:T(8,128)S(1)} collective-permute-done((f32[2,96,128]{2,1,0:T(8,128)S(1)}, f32[2,96,128]{2,1,0:T(8,128)S(1)}, u32[]{:S(2)}, u32[]{:S(2)}) %collective-permute-start.8) | collective-permute-done | bytes 98336 | tf_op jit(solution)/shard_map/ppermute | solution.py:565
  36.1 0.0 collective-permute-done.7.refs_2_
  36.1 2.8 %cycle.1 = (f32[2,96,8,128]{3,2,1,0:T(8,128)S(1)}, f32[2,96,8,128]{3,2,1,0:T(8,128)S(1)}, f32[48,8,128]{2,1,0:T(8,128)S(1)}, f32[12,8,128]{2,1,0:T(8,128)S(1)}, f32[1,112,128]{2,1,0:T(8,128)S(1)}) custom-call(s32[3]{0:T(128)S(1)} %pad_add_fusion.refs_0_, f32[2,96,128]{2,1,0:T(8,128)S(1)} %get-tuple-element.13.refs_1_, ...), custom_call_target="tpu_custom_call" | custom-call | tf_op jit(solution)/shard_map/cycle/pallas_call | solution.py:566
  39.0 0.1 collective-permute-start.12
  39.0 0.4 collective-permute-start.11
  39.4 1.5 %collective-permute-start.10 = (f32[1,112,128]{2,1,0:T(8,128)S(1)}, f32[1,112,128]{2,1,0:T(8,128)S(1)}, u32[]{:S(2)}, u32[]{:S(2)}) collective-permute-start(f32[1,112,128]{2,1,0:T(8,128)S(1)} %get-tuple-element.17.refs_1_), channel_id=1, source_target_pairs={{4,0},{0,4},{12,8},{8,12},{5,1},{1,5},{13,9},{9,13},{6,2},{2,6},{1... | collective-permute-start | bytes 172040 | tf_op jit(solution)/shard_map/ppermute | solution.py:582
  40.9 1.7 %collective-permute-done.12.refs_4_ = f32[1,112,128]{2,1,0:T(8,128)S(1)} collective-permute-done((f32[1,112,128]{2,1,0:T(8,128)S(1)}, f32[1,112,128]{2,1,0:T(8,128)S(1)}, u32[]{:S(2)}, u32[]{:S(2)}) %collective-permute-start.12) | collective-permute-done | bytes 57376 | tf_op jit(solution)/shard_map/ppermute | solution.py:582
  42.6 1.2 %collective-permute-done.11.refs_3_ = f32[1,112,128]{2,1,0:T(8,128)S(1)} collective-permute-done((f32[1,112,128]{2,1,0:T(8,128)S(1)}, f32[1,112,128]{2,1,0:T(8,128)S(1)}, u32[]{:S(2)}, u32[]{:S(2)}) %collective-permute-start.11) | collective-permute-done | bytes 57376 | tf_op jit(solution)/shard_map/ppermute | solution.py:582
  43.9 0.0 collective-permute-done.10.refs_2_
  43.9 2.5 %collective-permute-start.15 = (f32[16,128]{1,0:T(8,128)S(1)}, f32[16,128]{1,0:T(8,128)S(1)}, u32[]{:S(2)}, u32[]{:S(2)}) collective-permute-start(f32[16,128]{1,0:T(8,128)S(1)} %fusion.2.refs_5_), channel_id=1, source_target_pairs={{3,0},{2,1},{1,2},{0,3},{7,4},{6,5},{5,6},{4,7},{11,8},{10,9},{9,1... | collective-permute-start | bytes 24584 | tf_op jit(solution)/shard_map/ppermute | solution.py:584
  46.4 1.3 %collective-permute-start.14 = (f32[16,128]{1,0:T(8,128)S(1)}, f32[16,128]{1,0:T(8,128)S(1)}, u32[]{:S(2)}, u32[]{:S(2)}) collective-permute-start(f32[16,128]{1,0:T(8,128)S(1)} %fusion.2.refs_5_), channel_id=1, source_target_pairs={{2,0},{3,1},{0,2},{1,3},{6,4},{7,5},{4,6},{5,7},{10,8},{11,9},{8,1... | collective-permute-start | bytes 24584 | tf_op jit(solution)/shard_map/ppermute | solution.py:584
  47.7 0.6 %collective-permute-start.13 = (f32[16,128]{1,0:T(8,128)S(1)}, f32[16,128]{1,0:T(8,128)S(1)}, u32[]{:S(2)}, u32[]{:S(2)}) collective-permute-start(f32[16,128]{1,0:T(8,128)S(1)} %fusion.2.refs_5_), channel_id=1, source_target_pairs={{1,0},{0,1},{3,2},{2,3},{5,4},{4,5},{7,6},{6,7},{9,8},{8,9},{11,10... | collective-permute-start | bytes 24584 | tf_op jit(solution)/shard_map/ppermute | solution.py:584
  48.3 1.1 %collective-permute-done.15.refs_8_ = f32[16,128]{1,0:T(8,128)S(1)} collective-permute-done((f32[16,128]{1,0:T(8,128)S(1)}, f32[16,128]{1,0:T(8,128)S(1)}, u32[]{:S(2)}, u32[]{:S(2)}) %collective-permute-start.15) | collective-permute-done | bytes 8224 | tf_op jit(solution)/shard_map/ppermute | solution.py:584
  49.4 1.5 %collective-permute-done.14.refs_7_ = f32[16,128]{1,0:T(8,128)S(1)} collective-permute-done((f32[16,128]{1,0:T(8,128)S(1)}, f32[16,128]{1,0:T(8,128)S(1)}, u32[]{:S(2)}, u32[]{:S(2)}) %collective-permute-start.14) | collective-permute-done | bytes 8224 | tf_op jit(solution)/shard_map/ppermute | solution.py:584
  51.0 0.4 collective-permute-done.13.refs_6_
  51.4 3.5 %again.1 = (f32[12,16,128]{2,1,0:T(8,128)}, f32[12,16,128]{2,1,0:T(8,128)}, f32[12,16,128]{2,1,0:T(8,128)}, f32[12,16,128]{2,1,0:T(8,128)}) custom-call(s32[3]{0:T(128)S(1)} %pad_add_fusion.refs_0_, f32[1,112,128]{2,1,0:T(8,128)S(1)} %get-tuple-element.17.refs_1_, f32[1,112,128]{2,1,0:T(8,128)S(1)} %collective-permute-done.10.refs_2_, ...), custom_call_target="tpu_custom_call" | custom-call | tf_op jit(solution)/shard_map/again/pallas_call | solution.py:585
  (18 shorter events, 0.3 us)
Async XLA Ops:
  1.8 10.1 %copy-start = (f32[12,16,128]{2,1,0:T(8,128)S(1)}, f32[12,16,128]{2,1,0:T(8,128)}, u32[]{:S(2)}) copy-start(f32[12,16,128]{2,1,0:T(8,128)} %refs_9_.1) | copy-start | bytes 294916
  1.8 10.1 %copy-start.1 = (f32[12,16,128]{2,1,0:T(8,128)S(1)}, f32[12,16,128]{2,1,0:T(8,128)}, u32[]{:S(2)}) copy-start(f32[12,16,128]{2,1,0:T(8,128)} %refs_2_.1) | copy-start | bytes 294916
  1.9 11.5 %collective-permute-start.4 = (f32[12,16,128]{2,1,0:T(8,128)S(1)}, f32[12,16,128]{2,1,0:T(8,128)S(1)}, u32[]{:S(2)}, u32[]{:S(2)}) collective-permute-start(f32[12,16,128]{2,1,0:T(8,128)S(1)} %get-tuple-element.24), channel_id=1, source_target_pairs={{17,2},{18,1},{1,18},{2,17},{21,6},{22,5},{5,22},{6,21},{25,10},{2... | collective-permute-start | bytes 294920 | tf_op jit(solution)/shard_map/ppermute | solution.py:526
  2.6 11.9 %collective-permute-start.2 = (f32[12,16,128]{2,1,0:T(8,128)S(1)}, f32[12,16,128]{2,1,0:T(8,128)S(1)}, u32[]{:S(2)}, u32[]{:S(2)}) collective-permute-start(f32[12,16,128]{2,1,0:T(8,128)S(1)} %get-tuple-element.24), channel_id=1, source_target_pairs={{1,2},{2,1},{5,6},{6,5},{9,10},{10,9},{13,14},{14,13},{17,18},{18,... | collective-permute-start | bytes 294920 | tf_op jit(solution)/shard_map/ppermute | solution.py:518
  3.3 11.2 %collective-permute-start.3 = (f32[12,16,128]{2,1,0:T(8,128)S(1)}, f32[12,16,128]{2,1,0:T(8,128)S(1)}, u32[]{:S(2)}, u32[]{:S(2)}) collective-permute-start(f32[12,16,128]{2,1,0:T(8,128)S(1)} %get-tuple-element.25), channel_id=1, source_target_pairs={{16,1},{17,0},{18,3},{19,2},{0,17},{1,16},{2,19},{3,18},{20,5},{21... | collective-permute-start | bytes 294920 | tf_op jit(solution)/shard_map/ppermute | solution.py:526
  11.8 4.7 %collective-permute-start.1 = (f32[12,16,128]{2,1,0:T(8,128)S(1)}, f32[12,16,128]{2,1,0:T(8,128)S(1)}, u32[]{:S(2)}, u32[]{:S(2)}) collective-permute-start(f32[12,16,128]{2,1,0:T(8,128)S(1)} %get-tuple-element.25), channel_id=1, source_target_pairs={{0,1},{1,0},{2,3},{3,2},{4,5},{5,4},{6,7},{7,6},{8,9},{9,8},{10,11... | collective-permute-start | bytes 294920 | tf_op jit(solution)/shard_map/ppermute | solution.py:518
  12.0 6.7 %collective-permute-start = (f32[2,12,16,128]{3,2,1,0:T(8,128)S(1)}, f32[2,12,16,128]{3,2,1,0:T(8,128)S(1)}, u32[]{:S(2)}, u32[]{:S(2)}) collective-permute-start(f32[2,12,16,128]{3,2,1,0:T(8,128)S(1)} %pad_maximum_fusion), channel_id=1, source_target_pairs={{16,0},{0,16},{17,1},{1,17},{18,2},{2,18},{19,3},{3,19},{20,4},{4,... | collective-permute-start | bytes 589832 | tf_op jit(solution)/shard_map/ppermute | solution.py:521
  18.8 1.5 %collective-permute-start.5 = (f32[2,2,12,8,128]{4,3,2,1,0:T(8,128)S(1)}, f32[2,2,12,8,128]{4,3,2,1,0:T(8,128)S(1)}, u32[]{:S(2)}, u32[]{:S(2)}) collective-permute-start(f32[2,2,12,8,128]{4,3,2,1,0:T(8,128)S(1)} %bitcast.32), channel_id=1, source_target_pairs={{0,4},{4,0},{8,12},{12,8},{1,5},{5,1},{9,13},{13,9},{2,6},{6,2},{1... | collective-permute-start | bytes 589832 | tf_op jit(solution)/shard_map/ppermute | solution.py:540
  18.8 1.4 %collective-permute-start.6 = (f32[2,2,12,8,128]{4,3,2,1,0:T(8,128)S(1)}, f32[2,2,12,8,128]{4,3,2,1,0:T(8,128)S(1)}, u32[]{:S(2)}, u32[]{:S(2)}) collective-permute-start(f32[2,2,12,8,128]{4,3,2,1,0:T(8,128)S(1)} %bitcast.31), channel_id=1, source_target_pairs={{4,8},{8,4},{5,9},{9,5},{6,10},{10,6},{7,11},{11,7},{20,24},{24,20... | collective-permute-start | bytes 589832 | tf_op jit(solution)/shard_map/ppermute | solution.py:541
  23.1 8.4 %collective-permute-start.9 = (f32[2,96,128]{2,1,0:T(8,128)S(1)}, f32[2,96,128]{2,1,0:T(8,128)S(1)}, u32[]{:S(2)}, u32[]{:S(2)}) collective-permute-start(f32[2,96,128]{2,1,0:T(8,128)S(1)} %get-tuple-element.13.refs_1_), channel_id=1, source_target_pairs={{12,0},{8,4},{4,8},{0,12},{13,1},{9,5},{5,9},{1,13},{14,2},{10,6},... | collective-permute-start | bytes 294920 | tf_op jit(solution)/shard_map/ppermute | solution.py:565
  24.4 11.7 %collective-permute-start.8 = (f32[2,96,128]{2,1,0:T(8,128)S(1)}, f32[2,96,128]{2,1,0:T(8,128)S(1)}, u32[]{:S(2)}, u32[]{:S(2)}) collective-permute-start(f32[2,96,128]{2,1,0:T(8,128)S(1)} %get-tuple-element.13.refs_1_), channel_id=1, source_target_pairs={{8,0},{12,4},{0,8},{4,12},{9,1},{13,5},{1,9},{5,13},{10,2},{14,6},... | collective-permute-start | bytes 294920 | tf_op jit(solution)/shard_map/ppermute | solution.py:565
  31.5 4.7 %collective-permute-start.7 = (f32[2,96,128]{2,1,0:T(8,128)S(1)}, f32[2,96,128]{2,1,0:T(8,128)S(1)}, u32[]{:S(2)}, u32[]{:S(2)}) collective-permute-start(f32[2,96,128]{2,1,0:T(8,128)S(1)} %get-tuple-element.13.refs_1_), channel_id=1, source_target_pairs={{4,0},{0,4},{12,8},{8,12},{5,1},{1,5},{13,9},{9,13},{6,2},{2,6},{1... | collective-permute-start | bytes 294920 | tf_op jit(solution)/shard_map/ppermute | solution.py:565
  39.0 3.7 %collective-permute-start.12 = (f32[1,112,128]{2,1,0:T(8,128)S(1)}, f32[1,112,128]{2,1,0:T(8,128)S(1)}, u32[]{:S(2)}, u32[]{:S(2)}) collective-permute-start(f32[1,112,128]{2,1,0:T(8,128)S(1)} %get-tuple-element.17.refs_1_), channel_id=1, source_target_pairs={{12,0},{8,4},{4,8},{0,12},{13,1},{9,5},{5,9},{1,13},{14,2},{10,6},... | collective-permute-start | bytes 172040 | tf_op jit(solution)/shard_map/ppermute | solution.py:582
  39.0 4.8 %collective-permute-start.11 = (f32[1,112,128]{2,1,0:T(8,128)S(1)}, f32[1,112,128]{2,1,0:T(8,128)S(1)}, u32[]{:S(2)}, u32[]{:S(2)}) collective-permute-start(f32[1,112,128]{2,1,0:T(8,128)S(1)} %get-tuple-element.17.refs_1_), channel_id=1, source_target_pairs={{8,0},{12,4},{0,8},{4,12},{9,1},{13,5},{1,9},{5,13},{10,2},{14,6},... | collective-permute-start | bytes 172040 | tf_op jit(solution)/shard_map/ppermute | solution.py:582
  39.4 4.4 %collective-permute-start.10 = (f32[1,112,128]{2,1,0:T(8,128)S(1)}, f32[1,112,128]{2,1,0:T(8,128)S(1)}, u32[]{:S(2)}, u32[]{:S(2)}) collective-permute-start(f32[1,112,128]{2,1,0:T(8,128)S(1)} %get-tuple-element.17.refs_1_), channel_id=1, source_target_pairs={{4,0},{0,4},{12,8},{8,12},{5,1},{1,5},{13,9},{9,13},{6,2},{2,6},{1... | collective-permute-start | bytes 172040 | tf_op jit(solution)/shard_map/ppermute | solution.py:582
  43.9 5.5 %collective-permute-start.15 = (f32[16,128]{1,0:T(8,128)S(1)}, f32[16,128]{1,0:T(8,128)S(1)}, u32[]{:S(2)}, u32[]{:S(2)}) collective-permute-start(f32[16,128]{1,0:T(8,128)S(1)} %fusion.2.refs_5_), channel_id=1, source_target_pairs={{3,0},{2,1},{1,2},{0,3},{7,4},{6,5},{5,6},{4,7},{11,8},{10,9},{9,1... | collective-permute-start | bytes 24584 | tf_op jit(solution)/shard_map/ppermute | solution.py:584
  46.4 4.5 %collective-permute-start.14 = (f32[16,128]{1,0:T(8,128)S(1)}, f32[16,128]{1,0:T(8,128)S(1)}, u32[]{:S(2)}, u32[]{:S(2)}) collective-permute-start(f32[16,128]{1,0:T(8,128)S(1)} %fusion.2.refs_5_), channel_id=1, source_target_pairs={{2,0},{3,1},{0,2},{1,3},{6,4},{7,5},{4,6},{5,7},{10,8},{11,9},{8,1... | collective-permute-start | bytes 24584 | tf_op jit(solution)/shard_map/ppermute | solution.py:584
  47.7 3.7 %collective-permute-start.13 = (f32[16,128]{1,0:T(8,128)S(1)}, f32[16,128]{1,0:T(8,128)S(1)}, u32[]{:S(2)}, u32[]{:S(2)}) collective-permute-start(f32[16,128]{1,0:T(8,128)S(1)} %fusion.2.refs_5_), channel_id=1, source_target_pairs={{1,0},{0,1},{3,2},{2,3},{5,4},{4,5},{7,6},{6,7},{9,8},{8,9},{11,10... | collective-permute-start | bytes 24584 | tf_op jit(solution)/shard_map/ppermute | solution.py:584

commit v3 on v1

--- a/solution.py
+++ b/solution.py
@@ -14,6 +14,10 @@
 
 def roll(value, shift, axis):
     return pltpu.roll(value, shift % value.shape[axis], axis)
+
+
+def position():
+    return tuple(lax.axis_index(a) for a in ("gx", "gy", "gz"))
 
 
 def iota(shape, axis):
@@ -139,14 +143,14 @@
     return dot(high) + (dot(middle) + dot(low))
 
 
-def first_kernel(s, place, *refs):
+def first_kernel(s, *refs):
     n = s.nx
     own_g, own_c, x_gc = refs[0], refs[1], refs[2:1 + n]
     refs = refs[1 + n:]
-    zside = refs[: 2 * n]
-    refs = refs[2 * n:]
+    zside = refs[:n]
+    refs = refs[n:]
     y_a, y_b, g_out, d_out, q_out, share, natural, split_e, split_o, temp, temp1 = refs
-    ix, iy, iz = place[0], place[1], place[2]
+    ix, iy, iz = position()
     even_y = iy % 2 == 0
     even_z = iz % 2 == 0
     L = s.bz
@@ -171,7 +175,7 @@
                         g, c = own_g[xi, span, :], own_c[xi, span, :]
                     else:
                         g, c = x_gc[t - 1][0, xi, span, :], x_gc[t - 1][1, xi, span, :]
-                    a, b = zside[2 * t][xi, span, :], zside[2 * t + 1][xi, span, :]
+                    a, b = zside[t][0, xi, span, :], zside[t][1, xi, span, :]
                     nextlo = jnp.where(even_z, a, b)
                     prevhi = jnp.where(even_z, b, a)
                     gh, chh = halo(nextlo, prevhi)
@@ -394,11 +398,11 @@
     fine_block_sum(s, p_ref, x_ref, apply)
 
 
-def second_kernel(s, place, *refs):
+def second_kernel(s, *refs):
     shares = refs[: s.ny]
     g_ref, d_ref, q_ref, p_out, image_out, d1_out, d2_out, share = refs[s.ny:s.ny + 8]
     spot, temps, temp1 = refs[s.ny + 8:]
-    iy, iz = place[1], place[2]
+    ix, iy, iz = position()
     g1 = gather_shares(s, iy, shares, 0, spot)
     c1 = gather_shares(s, iy, shares, 1, spot)
     shape = (s.slots1, s.bz)
@@ -434,12 +438,11 @@
     first_half(s, image_out, d_ref, temps, temp1, share, 0)
 
 
-def third_kernel(s, place, *refs):
+def third_kernel(s, *refs):
     shares = refs[: s.ny]
-    p_ref, g_ref, d_ref, q_ref, d1_ref, d2_ref = refs[s.ny:s.ny + 6]
-    p_out, image_out, mw_out, nw_out = refs[s.ny + 6:s.ny + 10]
-    spot, temps, flat, mw_ref = refs[s.ny + 10:]
-    ix, iy = place[0], place[1]
+    p_ref, g_ref, d_ref, q_ref, d1_ref, d2_ref, out = refs[s.ny:s.ny + 7]
+    spot, temps, flat, mw_ref = refs[s.ny + 7:]
+    ix, iy, iz = position()
     g1 = gather_shares(s, iy, shares, 0, spot)
     d1 = [d1_ref[r] for r in range(s.rows1)]
     d2 = [d2_ref[r] for r in range(s.rows1 // 4)]
@@ -456,7 +459,7 @@
     wanted = jnp.where(target % 2 == 0, target // 2, L // 2 + target // 2)
     selection = jnp.where(source == wanted, 1.0, 0.0).astype(jnp.bfloat16)
     left = iota((s.half, L), 1) < L // 2
-    for ref, out in ((None, nw_out), (mw_ref, mw_out), (g_ref, image_out), (p_ref, p_out)):
+    for k, ref in enumerate((None, mw_ref, g_ref, p_ref)):
         if ref is not None:
             for par in range(2):
                 for r in range(s.rows):
@@ -468,9 +471,25 @@
                 even = flat[0, pl.ds(at, s.half, stride=s.slots), :]
                 odd = flat[1, pl.ds(at, s.half, stride=s.slots), :]
                 tiles.append(jnp.where(left, even, roll(odd, L // 2, 1)))
-        whole = exact_dot(jnp.concatenate(tiles, axis=0), selection)
-        for xi in range(s.bx):
-            out[xi] = whole[xi * s.by:(xi + 1) * s.by]
+        out[k] = exact_dot(jnp.concatenate(tiles, axis=0), selection)
+
+
+def last_kernel(s, *refs):
+    right, natural = refs[s.nz:s.nz + 2]
+    outs = refs[s.nz + 2:]
+    total = refs[0][...]
+    for v in refs[1:s.nz]:
+        total = total + v[...]
+    gamma = jnp.sum(total[: s.slots], keepdims=True)
+    delta = jnp.sum(total[s.slots:], keepdims=True)
+    alpha = gamma / delta
+    for xi in range(s.bx):
+        at = pl.ds(xi * s.by, s.by)
+        nw, mw, image, p = (natural[k, at, :] for k in range(4))
+        outs[0][xi] = alpha * p
+        outs[1][xi] = right[xi] - alpha * image
+        outs[2][xi] = p - alpha * mw
+        outs[3][xi] = image - alpha * nw
 
 
 def pairs(count):
@@ -486,14 +505,25 @@
     return [[((i + t) % count, i) for i in range(count)] for t in range(1, count)]
 
 
+def gather(block, axis, count):
+    if count & (count - 1):
+        return [block] + [lax.ppermute(block, axis, turn) for turn in turns(count)]
+    found = {0: block}
+    step = count // 2
+    while step:
+        turn = [(i, i ^ step) for i in range(count)]
+        for t in list(found):
+            found[t ^ step] = lax.ppermute(found[t], axis, turn)
+        step //= 2
+    return [found[t] for t in range(count)]
+
+
 def shards(s, right_side, coefficient):
     L = s.bz
-    ix, iy, iz = (lax.axis_index(a) for a in ("gx", "gy", "gz"))
-    place = jnp.stack([ix, iy, iz]).astype(jnp.int32)
-    smem = pl.BlockSpec(memory_space=pltpu.SMEM)
+    ix, iy, iz = position()
     vmem = pl.BlockSpec(memory_space=pltpu.VMEM)
     struct = lambda *shape: jax.ShapeDtypeStruct(shape, f32)
-    params = pltpu.CompilerParams(vmem_limit_bytes=56 * 2**20)
+    params = pltpu.CompilerParams(vmem_limit_bytes=16 * 4 * 2 * s.rows * s.slots * L)
 
     low = jnp.concatenate([right_side[:, :, : L // 2], coefficient[:, :, : L // 2]], axis=2)
     high = jnp.concatenate([right_side[:, :, L // 2:], coefficient[:, :, L // 2:]], axis=2)
@@ -501,21 +531,17 @@
     send = (jnp.where(even_z, high, low), jnp.where(even_z, low, high))
     both = jnp.stack([right_side, coefficient])
     zpairs = pairs(s.nz)
-    zside = [lax.ppermute(v, "gz", p) for v, p in zip(send, zpairs)]
+    zside = [jnp.stack([lax.ppermute(v, "gz", p) for v, p in zip(send, zpairs)])]
     x_gc = []
     for turn in turns(s.nx):
         x_gc.append(lax.ppermute(both, "gx", turn))
-        for v, p in zip(send, zpairs):
-            crossed = [
-                (a * s.nz + c, b * s.nz + d) for a, b in turn for c, d in p
-            ]
-            zside.append(lax.ppermute(v, ("gx", "gz"), crossed))
+        zside.append(lax.ppermute(zside[0], "gx", turn))
 
     def edge(rows):
         parts = []
         for t in range(s.nx):
             g, c = (right_side, coefficient) if t == 0 else (x_gc[t - 1][0], x_gc[t - 1][1])
-            a, b = zside[2 * t], zside[2 * t + 1]
+            a, b = zside[t][0], zside[t][1]
             parts.append(jnp.concatenate([g[:, rows], c[:, rows]], axis=1))
             parts.append(jnp.concatenate([a[:, rows], b[:, rows]], axis=1))
         return jnp.stack(parts).reshape(s.nx, 2, s.bx, 2 * HALO, L)
@@ -533,7 +559,7 @@
     g, d, q, share = pl.pallas_call(
         lambda *refs: first_kernel(s, *refs),
         out_shape=(fine, fine, fine, struct(2, s.share, L)),
-        in_specs=[smem] + [vmem] * (2 + (s.nx - 1) + 2 * s.nx + 2),
+        in_specs=[vmem] * (2 + (s.nx - 1) + s.nx + 2),
         out_specs=(vmem,) * 4,
         scratch_shapes=[
             pltpu.VMEM((2, 4 * s.rows, 2 * L), f32),
@@ -544,11 +570,10 @@
         ],
         compiler_params=params,
         name="widen",
-    )(place, right_side, coefficient, *x_gc, *zside, y_a, y_b)
+    )(right_side, coefficient, *x_gc, *zside, y_a, y_b)
 
     spot = pltpu.VMEM((s.slots1 * s.rows1, L), f32)
-    yturns = turns(s.ny)
-    shares = [share] + [lax.ppermute(share, "gy", turn) for turn in yturns]
+    shares = gather(share, "gy", s.ny)
     p, image, d1, d2, share = pl.pallas_call(
         lambda *refs: second_kernel(s, *refs),
         out_shape=(
@@ -558,22 +583,21 @@
             struct(s.rows1 // 4, s.slots1, L),
             struct(1, s.share + 2 * s.slots, L),
         ),
-        in_specs=[smem] + [vmem] * (s.ny + 3),
+        in_specs=[vmem] * (s.ny + 3),
         out_specs=(vmem,) * 5,
         scratch_shapes=[spot, temps, temp1],
         compiler_params=params,
         name="cycle",
-    )(place, *shares, g, d, q)
-
-    shares = [share] + [lax.ppermute(share, "gy", turn) for turn in yturns]
+    )(*shares, g, d, q)
+
+    shares = gather(share, "gy", s.ny)
     sums = sum(v[0, s.share:] for v in shares)
-    sums = sum([lax.ppermute(sums, "gz", turn) for turn in turns(s.nz)], sums)
-    nat = struct(s.bx, s.by, L)
-    p, image, mw, nw = pl.pallas_call(
+    sums = [sums] + [lax.ppermute(sums, "gz", turn) for turn in turns(s.nz)]
+    natural = pl.pallas_call(
         lambda *refs: third_kernel(s, *refs),
-        out_shape=(nat,) * 4,
-        in_specs=[smem] + [vmem] * (s.ny + 6),
-        out_specs=(vmem,) * 4,
+        out_shape=struct(4, s.bx * s.by, L),
+        in_specs=[vmem] * (s.ny + 6),
+        out_specs=vmem,
         scratch_shapes=[
             spot,
             temps,
@@ -582,10 +606,15 @@
         ],
         compiler_params=params,
         name="again",
-    )(place, *shares, p, image, d, q, d1, d2)
-
-    alpha = jnp.sum(sums[: s.slots]) / jnp.sum(sums[s.slots:])
-    return (alpha * p, right_side - alpha * image, p - alpha * mw, image - alpha * nw)
+    )(*shares, p, image, d, q, d1, d2)
+    return pl.pallas_call(
+        lambda *refs: last_kernel(s, *refs),
+        out_shape=(struct(s.bx, s.by, L),) * 4,
+        in_specs=[vmem] * (s.nz + 2),
+        out_specs=(vmem,) * 4,
+        compiler_params=params,
+        name="update",
+    )(*sums, right_side, natural)
 
 
 def solution(mesh):

time: 64.7 us -> 49.9 us (0.77)
  Pallas kernels: 14.5 us -> 7.58 us
  waiting for transfers between devices: 11.8 us -> 18.6 us
  local copies, waits for them, and re-layouts: 5.78 us -> 0.23 us
  starting transfers between devices: 25.4 us -> 21.2 us
  other arithmetic: 4.66 us -> 1.29 us
  between operations: 2.16 us -> 0.89 us
    ppermute x13 -> x12, waiting for transfers between devices: 10.2 us -> 17.8 us  [the longest x6 9.24 us: gather(): found[t ^ step] = lax.ppermute(found[t], axis, turn)]
    ppermute x13 -> x12, starting transfers between devices: 23.2 us -> 17.4 us  [the longest x6 8.32 us: gather(): found[t ^ step] = lax.ppermute(found[t], axis, turn)]
    unnamed x36 -> x4, local copies, waits for them, and re-layouts: 4.54 us -> 0.01 us
    pallas_call x1, Pallas kernels: 4.93 us -> 2.17 us  [shards(): pl.pallas_call(lambda *refs: second_kernel(s, *refs), out_shape=(fine, fi...]
    pallas_call x1, Pallas kernels: 4.87 us -> 2.26 us  [shards(): pl.pallas_call(lambda *refs: first_kernel(s, *refs), out_shape=(fine, fin...]
    sub x2 -> x0, other arithmetic: 2.37 us -> none  [the longest x1 1.68 us: shards(): image - alpha * nw]
    pallas_call x1 -> x2, Pallas kernels: 4.74 us -> 3.14 us  [the longest x1 2.26 us: shards(): pl.pallas_call(lambda *refs: third_kernel(s, *refs), out_shape=struct(4,...]
    ppermute x1, starting transfers between devices: 1.46 us -> 3.03 us  [shards(): x_gc.append(lax.ppermute(both, 'gx', turn))]
  transfers between devices with their start and end apart: 16 -> 15, of which waited for: 7 -> 8; matrix products, arithmetic and copies ran while one was open for 1% -> 1% of each run, Pallas kernels for 7% -> 5%
where the time goes in v3:
time: 49.9 us; the launch traced here: 49.7 us
  starting transfers between devices  21.2 us (42%)
  waiting for transfers between devices  18.6 us (37%)
  Pallas kernels  7.58 us (15%)
  other arithmetic  1.29 us (3%)
  between operations  0.89 us (2%)
    ppermute x6, waiting for transfers between devices, gather(): found[t ^ step] = lax.ppermute(found[t], axis, turn)  9.24 us
    ppermute x6, starting transfers between devices, gather(): found[t ^ step] = lax.ppermute(found[t], axis, turn)  8.32 us
    ppermute x3, starting transfers between devices, shards(): sums = [sums] + [lax.ppermute(sums, 'gz', turn) for turn in turns(s.nz)]  6.61 us
    ppermute x1, waiting for transfers between devices, shards(): zside.append(lax.ppermute(zside[0], 'gx', turn))  5.39 us
    ppermute x1, starting transfers between devices, shards(): x_gc.append(lax.ppermute(both, 'gx', turn))  3.03 us
    ppermute x2, starting transfers between devices, shards(): lax.ppermute(v, 'gz', p)  2.3 us
    ppermute x2, waiting for transfers between devices, shards(): lax.ppermute(v, 'gz', p)  2.29 us
    pallas_call x1, Pallas kernels, shards(): pl.pallas_call(lambda *refs: first_kernel(s, *refs), out_shape=(fine, fin...  2.26 us
  transfers between devices with their start and end apart: 15, of which 8 were waited for; matrix products, arithmetic and copies ran while one was open for 1% of the time, Pallas kernels for 5%

profile of v3, /device:TPU:0, one launch (start us, length us, event | category | flops | bytes accessed | tf_op | source)
XLA Modules:
  0.0 49.7 jit_solution(7507740691906159050)
XLA Ops:
  0.6 0.0 copy-start
  0.6 0.0 copy-start.1
  0.7 1.0 %pad_maximum_fusion = f32[2,12,16,128]{3,2,1,0:T(8,128)S(1)} fusion(f32[1,12,16,128]{3,2,1,0:T(8,128)} %bitcast.33, f32[1,12,16,128]{3,2,1,0:T(8,128)} %bitcast.32), kind=kLoop, calls=%fused_computation | loop fusion | flops 49152 | bytes 393216 | tf_op jit(solution)/shard_map/stack | solution.py:532
  1.6 3.0 %collective-permute-start = (f32[2,12,16,128]{3,2,1,0:T(8,128)S(1)}, f32[2,12,16,128]{3,2,1,0:T(8,128)S(1)}, u32[]{:S(2)}, u32[]{:S(2)}) collective-permute-start(f32[2,12,16,128]{3,2,1,0:T(8,128)S(1)} %pad_maximum_fusion), channel_id=1, source_target_pairs={{16,0},{0,16},{17,1},{1,17},{18,2},{2,18},{19,3},{3,19},{20,4},{4,... | collective-permute-start | bytes 589832 | tf_op jit(solution)/shard_map/ppermute | solution.py:537
  4.7 0.0 copy-done
  4.7 0.0 copy-done.1
  4.7 0.1 fusion.11
  4.8 0.1 broadcast_select_fusion.1
  4.9 1.6 %collective-permute-start.1 = (f32[12,16,128]{2,1,0:T(8,128)S(1)}, f32[12,16,128]{2,1,0:T(8,128)S(1)}, u32[]{:S(2)}, u32[]{:S(2)}) collective-permute-start(f32[12,16,128]{2,1,0:T(8,128)S(1)} %get-tuple-element.24), channel_id=1, source_target_pairs={{0,1},{1,0},{2,3},{3,2},{4,5},{5,4},{6,7},{7,6},{8,9},{9,8},{10,11... | collective-permute-start | bytes 294920 | tf_op jit(solution)/shard_map/ppermute | solution.py:534
  6.6 0.7 %collective-permute-start.2 = (f32[12,16,128]{2,1,0:T(8,128)S(1)}, f32[12,16,128]{2,1,0:T(8,128)S(1)}, u32[]{:S(2)}, u32[]{:S(2)}) collective-permute-start(f32[12,16,128]{2,1,0:T(8,128)S(1)} %get-tuple-element.25), channel_id=1, source_target_pairs={{1,2},{2,1},{5,6},{6,5},{9,10},{10,9},{13,14},{14,13},{17,18},{18,... | collective-permute-start | bytes 294920 | tf_op jit(solution)/shard_map/ppermute | solution.py:534
  7.3 2.3 %collective-permute-done.1 = f32[12,16,128]{2,1,0:T(8,128)S(1)} collective-permute-done((f32[12,16,128]{2,1,0:T(8,128)S(1)}, f32[12,16,128]{2,1,0:T(8,128)S(1)}, u32[]{:S(2)}, u32[]{:S(2)}) %collective-permute-start.1) | collective-permute-done | bytes 98336 | tf_op jit(solution)/shard_map/ppermute | solution.py:534
  9.6 0.0 collective-permute-done.2
  9.6 0.2 collective-permute-start.3
  9.9 0.0 collective-permute-done.refs_2_
  10.0 5.4 %collective-permute-done.3.refs_4_ = f32[2,12,16,128]{3,2,1,0:T(8,128)S(1)} collective-permute-done((f32[2,12,16,128]{3,2,1,0:T(8,128)S(1)}, f32[2,12,16,128]{3,2,1,0:T(8,128)S(1)}, u32[]{:S(2)}, u32[]{:S(2)}) %collective-permute-start.3) | collective-permute-done | bytes 196640 | tf_op jit(solution)/shard_map/ppermute | solution.py:538
  15.5 0.1 collective-permute-start.4
  15.6 0.7 %collective-permute-start.5 = (f32[2,2,12,8,128]{4,3,2,1,0:T(8,128)S(1)}, f32[2,2,12,8,128]{4,3,2,1,0:T(8,128)S(1)}, u32[]{:S(2)}, u32[]{:S(2)}) collective-permute-start(f32[2,2,12,8,128]{4,3,2,1,0:T(8,128)S(1)} %bitcast.36), channel_id=1, source_target_pairs={{4,8},{8,4},{5,9},{9,5},{6,10},{10,6},{7,11},{11,7},{20,24},{24,20... | collective-permute-start | bytes 589832 | tf_op jit(solution)/shard_map/ppermute | solution.py:553
  16.3 0.7 %collective-permute-done.4.refs_5_ = f32[2,2,12,8,128]{4,3,2,1,0:T(8,128)S(1)} collective-permute-done((f32[2,2,12,8,128]{4,3,2,1,0:T(8,128)S(1)}, f32[2,2,12,8,128]{4,3,2,1,0:T(8,128)S(1)}, u32[]{:S(2)}, u32[]{:S(2)}) %collective-permute-start.4) | collective-permute-done | bytes 196640 | tf_op jit(solution)/shard_map/ppermute | solution.py:552
  17.0 0.0 collective-permute-done.5.refs_6_
  17.0 2.3 %widen.1 = (f32[2,96,8,128]{3,2,1,0:T(8,128)S(1)}, f32[2,96,8,128]{3,2,1,0:T(8,128)S(1)}, f32[2,96,8,128]{3,2,1,0:T(8,128)S(1)}, f32[2,96,128]{2,1,0:T(8,128)S(1)}) custom-call(f32[12,16,128]{2,1,0:T(8,128)S(1)} %copy-done, f32[12,16,128]{2,1,0:T(8,128)S(1)} %copy-done.1, f32[2,12,16,128]{3,2,1,0:T(8,128)S(1)} %collective-permute-done.refs_2_, ...), custom_call_target="tpu_custom_call" | custom-call | tf_op jit(solution)/shard_map/widen/pallas_call | solution.py:559
  19.3 7.1 %collective-permute-start.7 = (f32[2,96,128]{2,1,0:T(8,128)S(1)}, f32[2,96,128]{2,1,0:T(8,128)S(1)}, u32[]{:S(2)}, u32[]{:S(2)}) collective-permute-start(f32[2,96,128]{2,1,0:T(8,128)S(1)} %get-tuple-element.13.refs_0_), channel_id=1, source_target_pairs={{0,8},{4,12},{8,0},{12,4},{1,9},{5,13},{9,1},{13,5},{2,10},{6,14},... | collective-permute-start | bytes 294920 | tf_op jit(solution)/shard_map/ppermute | solution.py:516
  26.4 0.0 collective-permute-start.6
  26.4 3.6 %collective-permute-done.7.refs_2_ = f32[2,96,128]{2,1,0:T(8,128)S(1)} collective-permute-done((f32[2,96,128]{2,1,0:T(8,128)S(1)}, f32[2,96,128]{2,1,0:T(8,128)S(1)}, u32[]{:S(2)}, u32[]{:S(2)}) %collective-permute-start.7) | collective-permute-done | bytes 98336 | tf_op jit(solution)/shard_map/ppermute | solution.py:516
  30.1 0.1 collective-permute-start.8
  30.2 0.0 collective-permute-done.6.refs_1_
  30.2 1.2 %collective-permute-done.8.refs_3_ = f32[2,96,128]{2,1,0:T(8,128)S(1)} collective-permute-done((f32[2,96,128]{2,1,0:T(8,128)S(1)}, f32[2,96,128]{2,1,0:T(8,128)S(1)}, u32[]{:S(2)}, u32[]{:S(2)}) %collective-permute-start.8) | collective-permute-done | bytes 98336 | tf_op jit(solution)/shard_map/ppermute | solution.py:516
  31.4 2.2 %cycle.1 = (f32[2,96,8,128]{3,2,1,0:T(8,128)S(1)}, f32[2,96,8,128]{3,2,1,0:T(8,128)S(1)}, f32[48,8,128]{2,1,0:T(8,128)S(1)}, f32[12,8,128]{2,1,0:T(8,128)S(1)}, f32[1,112,128]{2,1,0:T(8,128)S(1)}) custom-call(f32[2,96,128]{2,1,0:T(8,128)S(1)} %get-tuple-element.13.refs_0_, f32[2,96,128]{2,1,0:T(8,128)S(1)} %collective-permute-done.6.refs_1_, ...), custom_call_target="tpu_custom_call" | custom-call | tf_op jit(solution)/shard_map/cycle/pallas_call | solution.py:577
  33.6 1.1 %collective-permute-start.10 = (f32[1,112,128]{2,1,0:T(8,128)S(1)}, f32[1,112,128]{2,1,0:T(8,128)S(1)}, u32[]{:S(2)}, u32[]{:S(2)}) collective-permute-start(f32[1,112,128]{2,1,0:T(8,128)S(1)} %get-tuple-element.17.refs_0_), channel_id=1, source_target_pairs={{0,8},{4,12},{8,0},{12,4},{1,9},{5,13},{9,1},{13,5},{2,10},{6,14},... | collective-permute-start | bytes 172040 | tf_op jit(solution)/shard_map/ppermute | solution.py:516
  34.6 0.0 collective-permute-start.9
  34.6 3.2 %collective-permute-done.10.refs_2_ = f32[1,112,128]{2,1,0:T(8,128)S(1)} collective-permute-done((f32[1,112,128]{2,1,0:T(8,128)S(1)}, f32[1,112,128]{2,1,0:T(8,128)S(1)}, u32[]{:S(2)}, u32[]{:S(2)}) %collective-permute-start.10) | collective-permute-done | bytes 57376 | tf_op jit(solution)/shard_map/ppermute | solution.py:516
  37.8 0.0 collective-permute-start.11
  37.8 0.0 collective-permute-done.9.refs_1_
  37.8 1.2 %collective-permute-done.11.refs_3_ = f32[1,112,128]{2,1,0:T(8,128)S(1)} collective-permute-done((f32[1,112,128]{2,1,0:T(8,128)S(1)}, f32[1,112,128]{2,1,0:T(8,128)S(1)}, u32[]{:S(2)}, u32[]{:S(2)}) %collective-permute-start.11) | collective-permute-done | bytes 57376 | tf_op jit(solution)/shard_map/ppermute | solution.py:516
  39.0 3.6 %collective-permute-start.14 = (f32[16,128]{1,0:T(8,128)S(1)}, f32[16,128]{1,0:T(8,128)S(1)}, u32[]{:S(2)}, u32[]{:S(2)}) collective-permute-start(f32[16,128]{1,0:T(8,128)S(1)} %fusion.2.refs_0_), channel_id=1, source_target_pairs={{3,0},{2,1},{1,2},{0,3},{7,4},{6,5},{5,6},{4,7},{11,8},{10,9},{9,1... | collective-permute-start | bytes 24584 | tf_op jit(solution)/shard_map/ppermute | solution.py:595
  42.6 2.5 %collective-permute-start.13 = (f32[16,128]{1,0:T(8,128)S(1)}, f32[16,128]{1,0:T(8,128)S(1)}, u32[]{:S(2)}, u32[]{:S(2)}) collective-permute-start(f32[16,128]{1,0:T(8,128)S(1)} %fusion.2.refs_0_), channel_id=1, source_target_pairs={{2,0},{3,1},{0,2},{1,3},{6,4},{7,5},{4,6},{5,7},{10,8},{11,9},{8,1... | collective-permute-start | bytes 24584 | tf_op jit(solution)/shard_map/ppermute | solution.py:595
  45.2 0.5 collective-permute-start.12
  45.7 2.3 %again.1.refs_5_ = f32[4,192,128]{2,1,0:T(8,128)S(1)} custom-call(f32[1,112,128]{2,1,0:T(8,128)S(1)} %get-tuple-element.17.refs_0_, f32[1,112,128]{2,1,0:T(8,128)S(1)} %collective-permute-done.9.refs_1_, f32[1,112,128]{2,1,0:T(8,128)S(1)} %collective-permute-done.10.refs_2_, f32[1,112,128]{2,1,0:T(8,128)S(1)} %collective-permute-done.11.refs_3_, ...), custom_call_target="tpu_custom_call" | custom-call | tf_op jit(solution)/shard_map/again/pallas_call | solution.py:596
  47.9 0.0 collective-permute-done.14.refs_3_
  47.9 0.0 collective-permute-done.13.refs_2_
  47.9 0.9 %collective-permute-done.12.refs_1_ = f32[16,128]{1,0:T(8,128)S(1)} collective-permute-done((f32[16,128]{1,0:T(8,128)S(1)}, f32[16,128]{1,0:T(8,128)S(1)}, u32[]{:S(2)}, u32[]{:S(2)}) %collective-permute-start.12) | collective-permute-done | bytes 8224 | tf_op jit(solution)/shard_map/ppermute | solution.py:595
  48.8 0.9 %update.1 = (f32[12,16,128]{2,1,0:T(8,128)}, f32[12,16,128]{2,1,0:T(8,128)}, f32[12,16,128]{2,1,0:T(8,128)}, f32[12,16,128]{2,1,0:T(8,128)}) custom-call(f32[16,128]{1,0:T(8,128)S(1)} %fusion.2.refs_0_, f32[16,128]{1,0:T(8,128)S(1)} %collective-permute-done.12.refs_1_, f32[16,128]{1,0:T(8,128)S(1)} %collective-permute-done.13.refs_2_, ...), custom_call_target="tpu_custom_call" | custom-call | tf_op jit(solution)/shard_map/update/pallas_call | solution.py:610
  (19 shorter events, 0.3 us)
Async XLA Ops:
  0.6 4.0 %copy-start = (f32[12,16,128]{2,1,0:T(8,128)S(1)}, f32[12,16,128]{2,1,0:T(8,128)}, u32[]{:S(2)}) copy-start(f32[12,16,128]{2,1,0:T(8,128)} %refs_4_.1) | copy-start | bytes 294916
  0.6 4.0 %copy-start.1 = (f32[12,16,128]{2,1,0:T(8,128)S(1)}, f32[12,16,128]{2,1,0:T(8,128)}, u32[]{:S(2)}) copy-start(f32[12,16,128]{2,1,0:T(8,128)} %refs_1_.1) | copy-start | bytes 294916
  1.6 8.2 %collective-permute-start = (f32[2,12,16,128]{3,2,1,0:T(8,128)S(1)}, f32[2,12,16,128]{3,2,1,0:T(8,128)S(1)}, u32[]{:S(2)}, u32[]{:S(2)}) collective-permute-start(f32[2,12,16,128]{3,2,1,0:T(8,128)S(1)} %pad_maximum_fusion), channel_id=1, source_target_pairs={{16,0},{0,16},{17,1},{1,17},{18,2},{2,18},{19,3},{3,19},{20,4},{4,... | collective-permute-start | bytes 589832 | tf_op jit(solution)/shard_map/ppermute | solution.py:537
  4.9 4.7 %collective-permute-start.1 = (f32[12,16,128]{2,1,0:T(8,128)S(1)}, f32[12,16,128]{2,1,0:T(8,128)S(1)}, u32[]{:S(2)}, u32[]{:S(2)}) collective-permute-start(f32[12,16,128]{2,1,0:T(8,128)S(1)} %get-tuple-element.24), channel_id=1, source_target_pairs={{0,1},{1,0},{2,3},{3,2},{4,5},{5,4},{6,7},{7,6},{8,9},{9,8},{10,11... | collective-permute-start | bytes 294920 | tf_op jit(solution)/shard_map/ppermute | solution.py:534
  6.6 3.0 %collective-permute-start.2 = (f32[12,16,128]{2,1,0:T(8,128)S(1)}, f32[12,16,128]{2,1,0:T(8,128)S(1)}, u32[]{:S(2)}, u32[]{:S(2)}) collective-permute-start(f32[12,16,128]{2,1,0:T(8,128)S(1)} %get-tuple-element.25), channel_id=1, source_target_pairs={{1,2},{2,1},{5,6},{6,5},{9,10},{10,9},{13,14},{14,13},{17,18},{18,... | collective-permute-start | bytes 294920 | tf_op jit(solution)/shard_map/ppermute | solution.py:534
  9.6 5.7 %collective-permute-start.3 = (f32[2,12,16,128]{3,2,1,0:T(8,128)S(1)}, f32[2,12,16,128]{3,2,1,0:T(8,128)S(1)}, u32[]{:S(2)}, u32[]{:S(2)}) collective-permute-start(f32[2,12,16,128]{3,2,1,0:T(8,128)S(1)} %pad_maximum_fusion.1.refs_3_), channel_id=1, source_target_pairs={{16,0},{0,16},{17,1},{1,17},{18,2},{2,18},{19,3},{3,19},{20,4},{4,... | collective-permute-start | bytes 589832 | tf_op jit(solution)/shard_map/ppermute | solution.py:538
  15.5 1.5 %collective-permute-start.4 = (f32[2,2,12,8,128]{4,3,2,1,0:T(8,128)S(1)}, f32[2,2,12,8,128]{4,3,2,1,0:T(8,128)S(1)}, u32[]{:S(2)}, u32[]{:S(2)}) collective-permute-start(f32[2,2,12,8,128]{4,3,2,1,0:T(8,128)S(1)} %bitcast.37), channel_id=1, source_target_pairs={{0,4},{4,0},{8,12},{12,8},{1,5},{5,1},{9,13},{13,9},{2,6},{6,2},{1... | collective-permute-start | bytes 589832 | tf_op jit(solution)/shard_map/ppermute | solution.py:552
  15.6 1.4 %collective-permute-start.5 = (f32[2,2,12,8,128]{4,3,2,1,0:T(8,128)S(1)}, f32[2,2,12,8,128]{4,3,2,1,0:T(8,128)S(1)}, u32[]{:S(2)}, u32[]{:S(2)}) collective-permute-start(f32[2,2,12,8,128]{4,3,2,1,0:T(8,128)S(1)} %bitcast.36), channel_id=1, source_target_pairs={{4,8},{8,4},{5,9},{9,5},{6,10},{10,6},{7,11},{11,7},{20,24},{24,20... | collective-permute-start | bytes 589832 | tf_op jit(solution)/shard_map/ppermute | solution.py:553
  19.3 10.8 %collective-permute-start.7 = (f32[2,96,128]{2,1,0:T(8,128)S(1)}, f32[2,96,128]{2,1,0:T(8,128)S(1)}, u32[]{:S(2)}, u32[]{:S(2)}) collective-permute-start(f32[2,96,128]{2,1,0:T(8,128)S(1)} %get-tuple-element.13.refs_0_), channel_id=1, source_target_pairs={{0,8},{4,12},{8,0},{12,4},{1,9},{5,13},{9,1},{13,5},{2,10},{6,14},... | collective-permute-start | bytes 294920 | tf_op jit(solution)/shard_map/ppermute | solution.py:516
  26.4 3.8 %collective-permute-start.6 = (f32[2,96,128]{2,1,0:T(8,128)S(1)}, f32[2,96,128]{2,1,0:T(8,128)S(1)}, u32[]{:S(2)}, u32[]{:S(2)}) collective-permute-start(f32[2,96,128]{2,1,0:T(8,128)S(1)} %get-tuple-element.13.refs_0_), channel_id=1, source_target_pairs={{0,4},{4,0},{8,12},{12,8},{1,5},{5,1},{9,13},{13,9},{2,6},{6,2},{1... | collective-permute-start | bytes 294920 | tf_op jit(solution)/shard_map/ppermute | solution.py:516
  30.1 1.3 %collective-permute-start.8 = (f32[2,96,128]{2,1,0:T(8,128)S(1)}, f32[2,96,128]{2,1,0:T(8,128)S(1)}, u32[]{:S(2)}, u32[]{:S(2)}) collective-permute-start(f32[2,96,128]{2,1,0:T(8,128)S(1)} %collective-permute-done.7.refs_2_), channel_id=1, source_target_pairs={{0,4},{4,0},{8,12},{12,8},{1,5},{5,1},{9,13},{13,9},{2,6},{6,2},{1... | collective-permute-start | bytes 294920 | tf_op jit(solution)/shard_map/ppermute | solution.py:516
  33.6 4.2 %collective-permute-start.10 = (f32[1,112,128]{2,1,0:T(8,128)S(1)}, f32[1,112,128]{2,1,0:T(8,128)S(1)}, u32[]{:S(2)}, u32[]{:S(2)}) collective-permute-start(f32[1,112,128]{2,1,0:T(8,128)S(1)} %get-tuple-element.17.refs_0_), channel_id=1, source_target_pairs={{0,8},{4,12},{8,0},{12,4},{1,9},{5,13},{9,1},{13,5},{2,10},{6,14},... | collective-permute-start | bytes 172040 | tf_op jit(solution)/shard_map/ppermute | solution.py:516
  34.6 3.2 %collective-permute-start.9 = (f32[1,112,128]{2,1,0:T(8,128)S(1)}, f32[1,112,128]{2,1,0:T(8,128)S(1)}, u32[]{:S(2)}, u32[]{:S(2)}) collective-permute-start(f32[1,112,128]{2,1,0:T(8,128)S(1)} %get-tuple-element.17.refs_0_), channel_id=1, source_target_pairs={{0,4},{4,0},{8,12},{12,8},{1,5},{5,1},{9,13},{13,9},{2,6},{6,2},{1... | collective-permute-start | bytes 172040 | tf_op jit(solution)/shard_map/ppermute | solution.py:516
  37.8 1.2 %collective-permute-start.11 = (f32[1,112,128]{2,1,0:T(8,128)S(1)}, f32[1,112,128]{2,1,0:T(8,128)S(1)}, u32[]{:S(2)}, u32[]{:S(2)}) collective-permute-start(f32[1,112,128]{2,1,0:T(8,128)S(1)} %collective-permute-done.10.refs_2_), channel_id=1, source_target_pairs={{0,4},{4,0},{8,12},{12,8},{1,5},{5,1},{9,13},{13,9},{2,6},{6,2},{1... | collective-permute-start | bytes 172040 | tf_op jit(solution)/shard_map/ppermute | solution.py:516
  39.0 8.9 %collective-permute-start.14 = (f32[16,128]{1,0:T(8,128)S(1)}, f32[16,128]{1,0:T(8,128)S(1)}, u32[]{:S(2)}, u32[]{:S(2)}) collective-permute-start(f32[16,128]{1,0:T(8,128)S(1)} %fusion.2.refs_0_), channel_id=1, source_target_pairs={{3,0},{2,1},{1,2},{0,3},{7,4},{6,5},{5,6},{4,7},{11,8},{10,9},{9,1... | collective-permute-start | bytes 24584 | tf_op jit(solution)/shard_map/ppermute | solution.py:595
  42.6 5.3 %collective-permute-start.13 = (f32[16,128]{1,0:T(8,128)S(1)}, f32[16,128]{1,0:T(8,128)S(1)}, u32[]{:S(2)}, u32[]{:S(2)}) collective-permute-start(f32[16,128]{1,0:T(8,128)S(1)} %fusion.2.refs_0_), channel_id=1, source_target_pairs={{2,0},{3,1},{0,2},{1,3},{6,4},{7,5},{4,6},{5,7},{10,8},{11,9},{8,1... | collective-permute-start | bytes 24584 | tf_op jit(solution)/shard_map/ppermute | solution.py:595
  45.2 3.7 %collective-permute-start.12 = (f32[16,128]{1,0:T(8,128)S(1)}, f32[16,128]{1,0:T(8,128)S(1)}, u32[]{:S(2)}, u32[]{:S(2)}) collective-permute-start(f32[16,128]{1,0:T(8,128)S(1)} %fusion.2.refs_0_), channel_id=1, source_target_pairs={{1,0},{0,1},{3,2},{2,3},{5,4},{4,5},{7,6},{6,7},{9,8},{8,9},{11,10... | collective-permute-start | bytes 24584 | tf_op jit(solution)/shard_map/ppermute | solution.py:595

commit v4 on v3

--- a/solution.py
+++ b/solution.py
@@ -5,11 +5,13 @@
 from jax.experimental.pallas import tpu as pltpu
 from jax.sharding import PartitionSpec as P
 
+
 SWEEPS = 4
 relaxation = 0.6
 f32 = jnp.float32
 
 HALO = 4
+COLUMNS = 40
 
 
 def roll(value, shift, axis):
@@ -36,6 +38,8 @@
         self.slots1 = 2 * ny
         self.rows1 = self.x1 * self.y1
         self.share = 2 * self.rows1
+        self.group = self.bz // COLUMNS
+        self.packs = -(-self.bx // self.group)
 
 
 def fine_tools(s):
@@ -120,15 +124,6 @@
         store(i * s.y1 + j, 0.5 * total)
 
 
-def share_out(s, temp, out, lead):
-    count = (s.bx // 2) * s.y1
-    for h in range(2):
-        for b in range(s.nx):
-            out[lead, pl.ds(h * s.rows1 + b * count, count), :] = temp[
-                pl.ds(b * 4 + 1 + h, count, stride=s.slots), :
-            ]
-
-
 def split3(v):
     high = v.astype(jnp.bfloat16)
     rest = v - high.astype(f32)
@@ -143,112 +138,145 @@
     return dot(high) + (dot(middle) + dot(low))
 
 
+def share_out(s, temp, out):
+    count = (s.bx // 2) * s.y1
+    for h in range(2):
+        for b in range(s.nx):
+            out[pl.ds(h * s.rows1 + b * count, count), :] = temp[
+                pl.ds(b * 4 + 1 + h, count, stride=s.slots), :
+            ]
+
+
+def pack_kernel(s, both, send_a, send_b):
+    iz = position()[2]
+    even = iz % 2 == 0
+    shape = (s.by, s.bz)
+    lane = iota(shape, 1)
+    for arr in range(2):
+        for pack in range(s.packs):
+            first = jnp.zeros(shape, f32)
+            last = jnp.zeros(shape, f32)
+            for m in range(min(s.group, s.bx - pack * s.group)):
+                xi = pack * s.group + m
+                v = both[arr, xi]
+                here = (lane >= m * COLUMNS) & (lane < (m + 1) * COLUMNS)
+                first = jnp.where(here, roll(v, m * COLUMNS, 1) if m else v, first)
+                last = jnp.where(here, roll(v, (m + 1) * COLUMNS, 1), last)
+            send_a[arr, pack] = jnp.where(even, last, first)
+            send_b[arr, pack] = jnp.where(even, first, last)
+
+
+def column_tools(s, rows):
+    even_z = position()[2] % 2 == 0
+    lane = iota((rows, s.bz), 1)
+    front = lane < COLUMNS
+    back = lane >= s.bz - COLUMNS
+
+    def halo(xi, a, b):
+        at = (xi % s.group) * COLUMNS
+        following = jnp.where(even_z, a, b)
+        previous = jnp.where(even_z, b, a)
+        following = roll(following, -at, 1) if at else following
+        previous = roll(previous, s.bz - COLUMNS - at, 1)
+        return jnp.where(front, following, jnp.where(back, previous, 0.0))
+
+    shape = (2 * s.bz, 2 * s.bz)
+    source, target = iota(shape, 0), iota(shape, 1)
+    wanted = jnp.where(target < s.bz, 2 * target, 2 * (target - s.bz) + 1)
+    selection = jnp.where(source == wanted, 1.0, 0.0).astype(jnp.bfloat16)
+    return halo, selection
+
+
+def block_of(s, ix, t):
+    return (ix ^ t) if s.nx & (s.nx - 1) == 0 else (ix + t) % s.nx
+
+
+def own_kernel(s, *refs):
+    n = s.nx
+    blocks, sides = refs[:n], refs[n:2 * n]
+    split, share, natural, temp = refs[2 * n:]
+    ix = position()[0]
+    L = s.bz
+    halo, selection = column_tools(s, s.half)
+    count = (s.bx // 2) * s.y1
+    for t in range(n):
+        b = block_of(s, ix, t)
+        for arr in range(2):
+            for h in range(2):
+                span = pl.ds(h * s.half, s.half)
+                for xi in range(s.bx):
+                    at = pl.ds(h * s.rows + xi * s.half, s.half)
+                    a = sides[t][0, arr, xi // s.group, span, :]
+                    z = sides[t][1, arr, xi // s.group, span, :]
+                    natural[at, pl.ds(0, L)] = blocks[t][arr, xi, span, :]
+                    natural[at, pl.ds(L, L)] = halo(xi, a, z)
+            parted = exact_dot(natural[...], selection)
+            start = pl.multiple_of((b * 4 + 1) * s.rows, s.rows)
+            for par in range(2):
+                split[arr, par, pl.ds(start, 2 * s.rows), :] = parted[:, par * L:(par + 1) * L]
+            if arr == 0:
+                continue
+            for h in range(2):
+                for i in range(s.bx // 2):
+                    at = h * s.rows + 2 * i * s.half
+                    low, high = parted[at:at + s.half], parted[at + s.half:at + 2 * s.half]
+                    total = (low[:, :L] + low[:, L:]) + (high[:, :L] + high[:, L:])
+                    temp[pl.ds(i * s.half, s.half), :] = 0.5 * (total + roll(total, -1, 0))
+                to = pl.multiple_of(h * s.rows1 + b * count, count)
+                share[pl.ds(to, count), :] = temp[pl.ds(0, count, stride=2), :]
+
+
 def first_kernel(s, *refs):
-    n = s.nx
-    own_g, own_c, x_gc = refs[0], refs[1], refs[2:1 + n]
-    refs = refs[1 + n:]
-    zside = refs[:n]
-    refs = refs[n:]
-    y_a, y_b, g_out, d_out, q_out, share, natural, split_e, split_o, temp, temp1 = refs
+    blocks_a, blocks_b, sides_a, sides_b, _ = refs[:5]
+    split, g_out, d_out, q_out, share, natural, temp, temp1 = refs[5:]
     ix, iy, iz = position()
     even_y = iy % 2 == 0
-    even_z = iz % 2 == 0
     L = s.bz
-    tile = (s.half, L)
-    lane = iota(tile, 1)
-    row = iota(tile, 0)
-    left = lane < L // 2
-
-    def halo(nextlo, prevhi):
-        return (
-            jnp.where(left, nextlo, roll(prevhi, L // 2, 1)),
-            jnp.where(left, roll(nextlo, L // 2, 1), prevhi),
-        )
-
-    for t in range(n):
-        base = (ix ^ t) if n & (n - 1) == 0 else (ix + t) % n
-        for xi in range(s.bx):
-            for ch in range(4):
-                if ch in (1, 2):
-                    span = pl.ds((ch - 1) * s.half, s.half)
-                    if t == 0:
-                        g, c = own_g[xi, span, :], own_c[xi, span, :]
-                    else:
-                        g, c = x_gc[t - 1][0, xi, span, :], x_gc[t - 1][1, xi, span, :]
-                    a, b = zside[t][0, xi, span, :], zside[t][1, xi, span, :]
-                    nextlo = jnp.where(even_z, a, b)
-                    prevhi = jnp.where(even_z, b, a)
-                    gh, chh = halo(nextlo, prevhi)
-                else:
-                    use_a = even_y if ch == 3 else jnp.logical_not(even_y)
-                    gc = jnp.where(use_a, y_a[t, 0, xi], y_b[t, 0, xi])
-                    ab = jnp.where(use_a, y_a[t, 1, xi], y_b[t, 1, xi])
-                    turned = roll(gc, HALO, 0)
-                    ab_turned = roll(ab, HALO, 0)
-                    if ch == 3:
-                        keep = row < HALO
-                        g, c = gc, turned
-                        a, b = ab, ab_turned
-                    else:
-                        keep = row >= s.half - HALO
-                        g, c = turned, gc
-                        a, b = ab_turned, ab
-                    nextlo = jnp.where(even_z, a, b)
-                    prevhi = jnp.where(even_z, b, a)
-                    gh, chh = halo(nextlo, prevhi)
-                    g, c = jnp.where(keep, g, 0.0), jnp.where(keep, c, 0.0)
-                    gh, chh = jnp.where(keep, gh, 0.0), jnp.where(keep, chh, 0.0)
-                at = ch * s.rows + xi * s.half
-                natural[0, pl.ds(at, s.half), pl.ds(0, L)] = g
-                natural[0, pl.ds(at, s.half), pl.ds(L, L)] = gh
-                natural[1, pl.ds(at, s.half), pl.ds(0, L)] = c
-                natural[1, pl.ds(at, s.half), pl.ds(L, L)] = chh
-        source = iota((2 * L, 2 * L), 0)
-        target = iota((2 * L, 2 * L), 1)
-        wanted = jnp.where(target < L, 2 * target, 2 * (target - L) + 1)
-        selection = jnp.where(source == wanted, 1.0, 0.0).astype(jnp.bfloat16)
-        start = pl.multiple_of(base * (4 * s.rows), 4 * s.rows)
-        for arr in range(2):
-            parted = exact_dot(natural[arr], selection)
-            split_e[arr, pl.ds(start, 4 * s.rows), :] = parted[:, :L]
-            split_o[arr, pl.ds(start, 4 * s.rows), :] = parted[:, L:]
+    halo, selection = column_tools(s, 2 * HALO)
+    row = iota((s.half, L), 0)
+    for ch in (0, 3):
+        use_a = even_y if ch == 3 else jnp.logical_not(even_y)
+        for t in range(s.nx):
+            for xi in range(s.bx):
+                at = pl.ds((t * s.bx + xi) * 2 * HALO, 2 * HALO)
+                pack = xi // s.group
+                a = jnp.where(use_a, sides_a[t, 0, pack], sides_b[t, 0, pack])
+                z = jnp.where(use_a, sides_a[t, 1, pack], sides_b[t, 1, pack])
+                natural[at, pl.ds(0, L)] = jnp.where(use_a, blocks_a[t, xi], blocks_b[t, xi])
+                natural[at, pl.ds(L, L)] = halo(xi, a, z)
+        parted = exact_dot(natural[...], selection)
+        for t in range(s.nx):
+            b = block_of(s, ix, t)
+            for xi in range(s.bx):
+                at = (t * s.bx + xi) * 2 * HALO
+                to = pl.multiple_of((b * 4 + ch) * s.rows + xi * s.half, s.half)
+                for par in range(2):
+                    v = parted[at:at + 2 * HALO, par * L:(par + 1) * L]
+                    turned = roll(v, HALO, 0)
+                    g, c = (v, turned) if ch == 3 else (turned, v)
+                    split[0, par, pl.ds(to, s.half), :] = g
+                    split[1, par, pl.ds(to, s.half), :] = c
 
     shape = (s.slots, L)
     subs = iota(shape, 0) % 4
     inside = inside_columns(s, iz, shape) & inside_chunks(s, iy, subs)
-    for i in range(s.bx // 2):
-        values = []
-        for k in range(2):
-            both = []
-            for par, split in enumerate((split_e, split_o)):
-                line = []
-                for yi in range(s.half):
-                    r = (2 * i + k) * s.half + yi
-                    g = split[0, pl.ds(r, s.slots, stride=s.rows), :]
-                    c = split[1, pl.ds(r, s.slots, stride=s.rows), :]
-                    q = 26.0 + c
-                    valid = inside
-                    if yi >= HALO:
-                        valid = valid & (subs != 3)
-                    if yi < s.half - HALO:
-                        valid = valid & (subs != 0)
-                    d = jnp.where(valid, relaxation / q, 0.0)
-                    g_out[par, r] = g
-                    q_out[par, r] = q
-                    d_out[par, r] = d
-                    line.append(c)
-                both.append(line)
-            values.append(both)
-
-        def keep_c(at, tile1):
-            temp1[pl.ds(at * s.slots, s.slots), :] = tile1
-
-        fine_restrict(s, values, i, keep_c)
-    share_out(s, temp1, share, 1)
-    first_half(s, g_out, d_out, temp, temp1, share, 0)
-
-
-def first_half(s, g_ref, d_ref, temps, temp1, share, lead):
+    for par in range(2):
+        for r in range(s.rows):
+            yi = r % s.half
+            q = 26.0 + split[1, par, pl.ds(r, s.slots, stride=s.rows), :]
+            valid = inside
+            if yi >= HALO:
+                valid = valid & (subs != 3)
+            if yi < s.half - HALO:
+                valid = valid & (subs != 0)
+            g = split[0, par, pl.ds(r, s.slots, stride=s.rows), :]
+            g_out[par, r] = jnp.where(valid, g, 0.0)
+            q_out[par, r] = q
+            d_out[par, r] = jnp.where(valid, relaxation / q, 0.0)
+    first_half(s, g_out, d_out, temp, temp1, share)
+
+
+def first_half(s, g_ref, d_ref, temps, temp1, share):
     e_ref, x_ref = temps.at[0], temps.at[1]
     for par in range(2):
         for r in range(s.rows):
@@ -274,18 +302,18 @@
         fine_restrict(s, values, i, keep)
 
     fine_block_sum(s, e_ref, x_ref, consume)
-    share_out(s, temp1, share, lead)
-
-
-def gather_shares(s, iy, shares, lead, spot):
+    share_out(s, temp1, share)
+
+
+def gather_shares(s, iy, shares, spot):
     for t, ref in enumerate(shares):
         at = (iy ^ t) if s.ny & (s.ny - 1) == 0 else (iy + t) % s.ny
         start = pl.multiple_of(at * s.share, s.share)
-        spot[pl.ds(start, s.share), :] = ref[lead, pl.ds(0, s.share), :]
+        spot[pl.ds(start, s.share), :] = ref[pl.ds(0, s.share), :]
     return [spot[pl.ds(r, s.slots1, stride=s.rows1), :] for r in range(s.rows1)]
 
 
-def middle_sum(s, v, nx, ny, step):
+def middle_sum(v, nx, ny, step):
     shape = v[0].shape
     sub = iota(shape, 0)
     first, last = sub == 0, sub == shape[0] - 1
@@ -314,8 +342,8 @@
 
 def inside_columns(s, iz, shape):
     lanes = iota(shape, 1)
-    below = jnp.where(iz < s.nz - 1, 3 * s.bz // 4, s.bz // 2)
-    above = jnp.where(iz > 0, 3 * s.bz // 4, s.bz)
+    below = jnp.where(iz < s.nz - 1, (s.bz + COLUMNS) // 2, s.bz // 2)
+    above = jnp.where(iz > 0, s.bz - COLUMNS // 2, s.bz)
     return (lanes < below) | (lanes >= above)
 
 
@@ -328,11 +356,11 @@
 def middle_solve(s, g, d1, d2):
     keep = 1.0 - relaxation
     e0 = [d * t for d, t in zip(d1, g)]
-    sums = middle_sum(s, e0, s.x1, s.y1, 1)
+    sums = middle_sum(e0, s.x1, s.y1, 1)
     g2 = middle_restrict(s, [keep * t - e + u for t, e, u in zip(g, e0, sums)])
     e = [d * t for d, t in zip(d2, g2)]
-    for sweep in range(SWEEPS - 1):
-        sums = middle_sum(s, e, s.x1 // 2, s.y1 // 2, 2)
+    for _ in range(SWEEPS - 1):
+        sums = middle_sum(e, s.x1 // 2, s.y1 // 2, 2)
         e = [keep * a + d * ((t - a) + u) for a, d, t, u in zip(e, d2, g2, sums)]
     spread = [a + roll(a, 1, 1) for a in e]
     e1 = [
@@ -340,7 +368,7 @@
         for x in range(s.x1)
         for y in range(s.y1)
     ]
-    sums = middle_sum(s, e1, s.x1, s.y1, 1)
+    sums = middle_sum(e1, s.x1, s.y1, 1)
     return [keep * a + d * ((t - a) + u) for a, d, t, u in zip(e1, d1, g, sums)]
 
 
@@ -399,12 +427,13 @@
 
 
 def second_kernel(s, *refs):
-    shares = refs[: s.ny]
-    g_ref, d_ref, q_ref, p_out, image_out, d1_out, d2_out, share = refs[s.ny:s.ny + 8]
-    spot, temps, temp1 = refs[s.ny + 8:]
-    ix, iy, iz = position()
-    g1 = gather_shares(s, iy, shares, 0, spot)
-    c1 = gather_shares(s, iy, shares, 1, spot)
+    shares, shares_c = refs[: s.ny], refs[s.ny:2 * s.ny]
+    refs = refs[2 * s.ny:]
+    g_ref, d_ref, q_ref, p_out, image_out, d1_out, d2_out, share = refs[:8]
+    spot, temps, temp1 = refs[8:]
+    _, iy, iz = position()
+    g1 = gather_shares(s, iy, shares, spot)
+    c1 = gather_shares(s, iy, shares_c, spot)
     shape = (s.slots1, s.bz)
     inside = inside_columns(s, iz, shape)
     inside2 = inside & (iota(shape, 1) % 2 == 0)
@@ -433,17 +462,17 @@
             deltas[r % 4] += image_out[par, r] * p
     gamma = jnp.where(own, (gammas[0] + gammas[1]) + (gammas[2] + gammas[3]), 0.0)
     delta = jnp.where(own, (deltas[0] + deltas[1]) + (deltas[2] + deltas[3]), 0.0)
-    share[0, pl.ds(s.share, s.slots), :] = gamma
-    share[0, pl.ds(s.share + s.slots, s.slots), :] = delta
-    first_half(s, image_out, d_ref, temps, temp1, share, 0)
+    share[pl.ds(s.share, s.slots), :] = gamma
+    share[pl.ds(s.share + s.slots, s.slots), :] = delta
+    first_half(s, image_out, d_ref, temps, temp1, share)
 
 
 def third_kernel(s, *refs):
     shares = refs[: s.ny]
     p_ref, g_ref, d_ref, q_ref, d1_ref, d2_ref, out = refs[s.ny:s.ny + 7]
     spot, temps, flat, mw_ref = refs[s.ny + 7:]
-    ix, iy, iz = position()
-    g1 = gather_shares(s, iy, shares, 0, spot)
+    ix, iy, _ = position()
+    g1 = gather_shares(s, iy, shares, spot)
     d1 = [d1_ref[r] for r in range(s.rows1)]
     d2 = [d2_ref[r] for r in range(s.rows1 // 4)]
     coarse = to_fine(s, iy, middle_solve(s, g1, d1, d2))
@@ -492,11 +521,19 @@
         outs[3][xi] = image - alpha * nw
 
 
-def pairs(count):
-    return (
-        [(i, i ^ 1) for i in range(count) if (i ^ 1) < count],
-        [(i, ((i + 1) ^ 1) - 1) for i in range(1, count) if ((i + 1) ^ 1) - 1 < count],
-    )
+def pairs(count, closed=False):
+    even = [(i, i + 1) for i in range(0, count - 1, 2)]
+    odd = [(i, (i + 1) % count) for i in range(1, count if closed and count > 2 else count - 1, 2)]
+    return [[p for i, j in swaps for p in ((i, j), (j, i))] for swaps in (even, odd)]
+
+
+def filled(others, count, swaps):
+    idle = set(range(count)) - {i for i, _ in swaps}
+    if others % 2:
+        idle = set()
+    return [
+        (other * count + i, other * count + j) for other in range(others) for i, j in swaps
+    ] + [(other * count + i, (other ^ 1) * count + i) for other in range(others) for i in sorted(idle)]
 
 
 def turns(count):
@@ -520,57 +557,80 @@
 
 def shards(s, right_side, coefficient):
     L = s.bz
-    ix, iy, iz = position()
     vmem = pl.BlockSpec(memory_space=pltpu.VMEM)
     struct = lambda *shape: jax.ShapeDtypeStruct(shape, f32)
     params = pltpu.CompilerParams(vmem_limit_bytes=16 * 4 * 2 * s.rows * s.slots * L)
 
-    low = jnp.concatenate([right_side[:, :, : L // 2], coefficient[:, :, : L // 2]], axis=2)
-    high = jnp.concatenate([right_side[:, :, L // 2:], coefficient[:, :, L // 2:]], axis=2)
-    even_z = iz % 2 == 0
-    send = (jnp.where(even_z, high, low), jnp.where(even_z, low, high))
+    pack = struct(2, s.packs, s.by, L)
     both = jnp.stack([right_side, coefficient])
-    zpairs = pairs(s.nz)
-    zside = [jnp.stack([lax.ppermute(v, "gz", p) for v, p in zip(send, zpairs)])]
-    x_gc = []
-    for turn in turns(s.nx):
-        x_gc.append(lax.ppermute(both, "gx", turn))
-        zside.append(lax.ppermute(zside[0], "gx", turn))
-
-    def edge(rows):
-        parts = []
-        for t in range(s.nx):
-            g, c = (right_side, coefficient) if t == 0 else (x_gc[t - 1][0], x_gc[t - 1][1])
-            a, b = zside[t][0], zside[t][1]
-            parts.append(jnp.concatenate([g[:, rows], c[:, rows]], axis=1))
-            parts.append(jnp.concatenate([a[:, rows], b[:, rows]], axis=1))
-        return jnp.stack(parts).reshape(s.nx, 2, s.bx, 2 * HALO, L)
-
-    first_rows, last_rows = edge(slice(0, HALO)), edge(slice(s.by - HALO, s.by))
-    even_y = iy % 2 == 0
-    ypairs = pairs(s.ny)
-    y_a = lax.ppermute(jnp.where(even_y, last_rows, first_rows), "gy", ypairs[0])
-    y_b = lax.ppermute(jnp.where(even_y, first_rows, last_rows), "gy", ypairs[1])
+    send_a, send_b = pl.pallas_call(
+        lambda *refs: pack_kernel(s, *refs),
+        out_shape=(pack, pack),
+        in_specs=[vmem],
+        out_specs=(vmem,) * 2,
+        compiler_params=params,
+        name="pack",
+    )(both)
+    blocks = [both] + [lax.ppermute(both, "gx", turn) for turn in turns(s.nx)]
+    received = [
+        lax.ppermute(v, ("gy", "gz"), filled(s.ny, s.nz, p))
+        for v, p in zip((send_a, send_b), pairs(s.nz))
+    ]
+    side = jnp.stack(received)
+    sides = [side] + [lax.ppermute(side, "gx", turn) for turn in turns(s.nx)]
+
+    even_y = position()[1] % 2 == 0
+    first_rows, last_rows = slice(0, HALO), slice(s.by - HALO, s.by)
+
+    def swap_rows(values):
+        edges = [
+            jnp.concatenate([values[0][..., rows, :], values[1][..., rows, :]], axis=-2)
+            for rows in (first_rows, last_rows)
+        ]
+        a, b = pairs(s.ny, s.ny % 2 == 0)
+        return (
+            lax.ppermute(jnp.where(even_y, edges[1], edges[0]), "gy", a),
+            lax.ppermute(jnp.where(even_y, edges[0], edges[1]), "gy", b),
+        )
+
+    stacked = jnp.stack(blocks, axis=1)
+    blocks_a, blocks_b = swap_rows((stacked[0], stacked[1]))
+    stacked = jnp.stack(sides)
+    sides_a, sides_b = swap_rows((stacked[:, :, 0], stacked[:, :, 1]))
 
     fine = struct(2, s.rows, s.slots, L)
     fine_scratch = pltpu.VMEM((2, s.rows, s.slots, L), f32)
     temps = pltpu.VMEM((2, 2, s.rows, s.slots, L), f32)
     temp1 = pltpu.VMEM(((s.bx // 2) * s.y1 * s.slots, L), f32)
-    g, d, q, share = pl.pallas_call(
+    split_shape = struct(2, 2, s.slots * s.rows, L)
+    share_shape = struct(s.share, L)
+    split, share = pl.pallas_call(
+        lambda *refs: own_kernel(s, *refs),
+        out_shape=(split_shape, share_shape),
+        in_specs=[vmem] * (2 * s.nx),
+        out_specs=(vmem,) * 2,
+        scratch_shapes=[
+            pltpu.VMEM((2 * s.rows, 2 * L), f32),
+            pltpu.VMEM((s.bx // 2 * s.half, L), f32),
+        ],
+        compiler_params=params,
+        name="own",
+    )(*blocks, *sides)
+    shares_c = gather(share, "gy", s.ny)
+    _, g, d, q, share = pl.pallas_call(
         lambda *refs: first_kernel(s, *refs),
-        out_shape=(fine, fine, fine, struct(2, s.share, L)),
-        in_specs=[vmem] * (2 + (s.nx - 1) + s.nx + 2),
-        out_specs=(vmem,) * 4,
+        out_shape=(split_shape, fine, fine, fine, share_shape),
+        in_specs=[vmem] * 5,
+        out_specs=(vmem,) * 5,
+        input_output_aliases={4: 0},
         scratch_shapes=[
-            pltpu.VMEM((2, 4 * s.rows, 2 * L), f32),
-            pltpu.VMEM((2, s.slots * s.rows, L), f32),
-            pltpu.VMEM((2, s.slots * s.rows, L), f32),
+            pltpu.VMEM((s.nx * s.bx * 2 * HALO, 2 * L), f32),
             temps,
             temp1,
         ],
         compiler_params=params,
         name="widen",
-    )(right_side, coefficient, *x_gc, *zside, y_a, y_b)
+    )(blocks_a, blocks_b, sides_a, sides_b, split)
 
     spot = pltpu.VMEM((s.slots1 * s.rows1, L), f32)
     shares = gather(share, "gy", s.ny)
@@ -581,18 +641,18 @@
             fine,
             struct(s.rows1, s.slots1, L),
             struct(s.rows1 // 4, s.slots1, L),
-            struct(1, s.share + 2 * s.slots, L),
+            struct(s.share + 2 * s.slots, L),
         ),
-        in_specs=[vmem] * (s.ny + 3),
+        in_specs=[vmem] * (2 * s.ny + 3),
         out_specs=(vmem,) * 5,
         scratch_shapes=[spot, temps, temp1],
         compiler_params=params,
         name="cycle",
-    )(*shares, g, d, q)
+    )(*shares, *shares_c, g, d, q)
 
     shares = gather(share, "gy", s.ny)
-    sums = sum(v[0, s.share:] for v in shares)
-    sums = [sums] + [lax.ppermute(sums, "gz", turn) for turn in turns(s.nz)]
+    part = sum(v[s.share:] for v in shares)
+    sums = [part] + [lax.ppermute(part, "gz", turn) for turn in turns(s.nz)]
     natural = pl.pallas_call(
         lambda *refs: third_kernel(s, *refs),
         out_shape=struct(4, s.bx * s.by, L),

time: 49.9 us -> 48 us (0.962)
  starting transfers between devices: 21.2 us -> 18.9 us
  waiting for transfers between devices: 18.6 us -> 19.2 us
    ppermute x9 -> x11, waiting for transfers between devices: 9.31 us -> 12.5 us  [the longest x1 4.34 us: shards(): sides = [side] + [lax.ppermute(side, 'gx', turn) for turn in turns(s.nx)]]
    ppermute x6 -> x9, waiting for transfers between devices: 9.24 us -> 6.68 us  [gather(): found[t ^ step] = lax.ppermute(found[t], axis, turn)]
    ppermute x6 -> x9, starting transfers between devices: 8.32 us -> 5.87 us  [gather(): found[t ^ step] = lax.ppermute(found[t], axis, turn)]
    pallas_call x1 -> x3, Pallas kernels: 2.26 us -> 2.53 us  [the longest x1 1.8 us: shards(): pl.pallas_call(lambda *refs: first_kernel(s, *refs), out_shape=(split_sha...]
    ppermute x9 -> x11, starting transfers between devices: 12.8 us -> 13 us  [the longest x3 5.45 us: shards(): sums = [part] + [lax.ppermute(part, 'gz', turn) for turn in turns(s.nz)]]
    another operation x9 -> x2, other arithmetic: 1.12 us -> 0.99 us  [the longest x1 0.97 us: shards(): stacked = jnp.stack(blocks, axis=1)]
  transfers between devices with their start and end apart: 15 -> 20, of which waited for: 8 -> 9; matrix products, arithmetic and copies ran while one was open for 1% -> 0% of each run, Pallas kernels for 5% -> 10%
where the time goes in v4:
time: 48 us; the launch traced here: 47.8 us
  waiting for transfers between devices  19.2 us (40%)
  starting transfers between devices  18.9 us (39%)
  Pallas kernels  7.77 us (16%)
  other arithmetic  1.11 us (2%)
  between operations  0.77 us (2%)
    ppermute x9, waiting for transfers between devices, gather(): found[t ^ step] = lax.ppermute(found[t], axis, turn)  6.68 us
    ppermute x9, starting transfers between devices, gather(): found[t ^ step] = lax.ppermute(found[t], axis, turn)  5.87 us
    ppermute x3, starting transfers between devices, shards(): sums = [part] + [lax.ppermute(part, 'gz', turn) for turn in turns(s.nz)]  5.45 us
    ppermute x1, waiting for transfers between devices, shards(): sides = [side] + [lax.ppermute(side, 'gx', turn) for turn in turns(s.nx)]  4.34 us
    ppermute x2, starting transfers between devices, shards(): lax.ppermute(v, ('gy', 'gz'), filled(s.ny, s.nz, p))  3.12 us
    ppermute x1, waiting for transfers between devices, shards(): blocks = [both] + [lax.ppermute(both, 'gx', turn) for turn in turns(s.nx)]  2.35 us
    ppermute x2, waiting for transfers between devices, shards(): lax.ppermute(v, ('gy', 'gz'), filled(s.ny, s.nz, p))  2.24 us
    pallas_call x1, Pallas kernels, shards(): pl.pallas_call(lambda *refs: third_kernel(s, *refs), out_shape=struct(4,...  2.23 us
  transfers between devices with their start and end apart: 20, of which 9 were waited for; matrix products, arithmetic and copies ran while one was open for 0% of the time, Pallas kernels for 10%

profile of v4, /device:TPU:0, one launch (start us, length us, event | category | flops | bytes accessed | tf_op | source)
XLA Modules:
  0.0 47.8 jit_solution(9542841402878122023)
XLA Ops:
  0.6 1.0 %fusion.11 = (f32[2,1,12,16,128]{4,3,2,1,0:T(8,128)S(1)}, f32[2,12,16,128]{3,2,1,0:T(8,128)S(1)}) fusion(f32[1,12,16,128]{3,2,1,0:T(8,128)} %bitcast.25, f32[1,12,16,128]{3,2,1,0:T(8,128)} %bitcast.23), kind=kLoop, calls=%fused_computation.26 | loop fusion | flops 49152 | bytes 589824 | tf_op jit(solution)/shard_map/stack | solution.py:596
  1.6 0.1 pack.1
  1.8 3.1 %collective-permute-start.3 = (f32[2,4,16,128]{3,2,1,0:T(8,128)S(1)}, f32[2,4,16,128]{3,2,1,0:T(8,128)S(1)}, u32[]{:S(2)}, u32[]{:S(2)}) collective-permute-start(f32[2,4,16,128]{3,2,1,0:T(8,128)S(1)} %get-tuple-element.17), channel_id=1, source_target_pairs={{0,1},{1,0},{2,3},{3,2},{4,5},{5,4},{6,7},{7,6},{8,9},{9,8},{10,11... | collective-permute-start | bytes 196616 | tf_op jit(solution)/shard_map/ppermute | solution.py:576
  4.9 0.0 collective-permute-start.4
  4.9 2.2 %collective-permute-done.3 = f32[2,4,16,128]{3,2,1,0:T(8,128)S(1)} collective-permute-done((f32[2,4,16,128]{3,2,1,0:T(8,128)S(1)}, f32[2,4,16,128]{3,2,1,0:T(8,128)S(1)}, u32[]{:S(2)}, u32[]{:S(2)}) %collective-permute-start.3) | collective-permute-done | bytes 65568 | tf_op jit(solution)/shard_map/ppermute | solution.py:576
  7.1 0.0 collective-permute-done.4
  7.1 2.0 %collective-permute-start.5 = (f32[2,2,4,16,128]{4,3,2,0,1:T(8,128)S(1)}, f32[2,2,4,16,128]{4,3,2,0,1:T(8,128)S(1)}, u32[]{:S(2)}, u32[]{:S(2)}) collective-permute-start(f32[2,2,4,16,128]{4,3,2,0,1:T(8,128)S(1)} %get-tuple-element.49), channel_id=1, source_target_pairs={{16,0},{0,16},{17,1},{1,17},{18,2},{2,18},{19,3},{3,19},{20,4},{4,... | collective-permute-start | bytes 393224 | tf_op jit(solution)/shard_map/ppermute | solution.py:580
  9.2 0.1 collective-permute-start
  9.2 4.3 %collective-permute-done.5 = f32[2,2,4,16,128]{4,3,2,0,1:T(8,128)S(1)} collective-permute-done((f32[2,2,4,16,128]{4,3,2,0,1:T(8,128)S(1)}, f32[2,2,4,16,128]{4,3,2,0,1:T(8,128)S(1)}, u32[]{:S(2)}, u32[]{:S(2)}) %collective-permute-start.5) | collective-permute-done | bytes 131104 | tf_op jit(solution)/shard_map/ppermute | solution.py:580
  13.6 2.4 %collective-permute-done.refs_1_ = f32[2,12,16,128]{3,2,1,0:T(8,128)S(1)} collective-permute-done((f32[2,12,16,128]{3,2,1,0:T(8,128)S(1)}, f32[2,12,16,128]{3,2,1,0:T(8,128)S(1)}, u32[]{:S(2)}, u32[]{:S(2)}) %collective-permute-start) | collective-permute-done | bytes 196640 | tf_op jit(solution)/shard_map/ppermute | solution.py:574
  16.1 0.1 collective-permute-start.1
  16.2 1.6 %collective-permute-start.2 = (f32[2,12,8,128]{3,2,1,0:T(8,128)S(1)}, f32[2,12,8,128]{3,2,1,0:T(8,128)S(1)}, u32[]{:S(2)}, u32[]{:S(2)}) collective-permute-start(f32[2,12,8,128]{3,2,1,0:T(8,128)S(1)} %get-tuple-element.34), channel_id=1, source_target_pairs={{4,8},{8,4},{12,0},{0,12},{5,9},{9,5},{13,1},{1,13},{6,10},{10,6},... | collective-permute-start | bytes 294920 | tf_op jit(solution)/shard_map/ppermute | solution.py:593
  17.9 0.1 collective-permute-start.6
  18.0 0.5 %collective-permute-start.7 = (f32[2,2,4,8,128]{4,3,2,1,0:T(8,128)S(1)}, f32[2,2,4,8,128]{4,3,2,1,0:T(8,128)S(1)}, u32[]{:S(2)}, u32[]{:S(2)}) collective-permute-start(f32[2,2,4,8,128]{4,3,2,1,0:T(8,128)S(1)} %get-tuple-element.42), channel_id=1, source_target_pairs={{4,8},{8,4},{12,0},{0,12},{5,9},{9,5},{13,1},{1,13},{6,10},{10,6},... | collective-permute-start | bytes 196616 | tf_op jit(solution)/shard_map/ppermute | solution.py:593
  18.6 0.6 %own.1 = (f32[2,2,768,128]{3,2,1,0:T(8,128)S(1)}, f32[96,128]{1,0:T(8,128)S(1)}) custom-call(f32[2,12,16,128]{3,2,1,0:T(8,128)S(1)} %get-tuple-element.41.refs_0_, f32[2,12,16,128]{3,2,1,0:T(8,128)S(1)} %collective-permute-done.refs_1_, f32[2,2,4,16,128]{4,3,2,1,0:T(8,128)S(1)} %copy.9.refs_2_, f32[2,2,4,16,128]{4,3,2,1,0:T(8,128)S(1)} %copy.10.refs_3_), custom_call_target="tpu_custom_call" | custom-call | tf_op jit(solution)/shard_map/own/pallas_call | solution.py:607
  19.2 1.6 %collective-permute-start.12 = (f32[96,128]{1,0:T(8,128)S(1)}, f32[96,128]{1,0:T(8,128)S(1)}, u32[]{:S(2)}, u32[]{:S(2)}) collective-permute-start(f32[96,128]{1,0:T(8,128)S(1)} %get-tuple-element.21.refs_4_), channel_id=1, source_target_pairs={{0,8},{4,12},{8,0},{12,4},{1,9},{5,13},{9,1},{13,5},{2,10},{6,14},... | collective-permute-start | bytes 147464 | tf_op jit(solution)/shard_map/ppermute | solution.py:553
  20.7 0.0 collective-permute-done.6.refs_2_
  20.8 1.6 %collective-permute-done.7.refs_3_ = f32[2,2,4,8,128]{4,3,2,1,0:T(8,128)S(1)} collective-permute-done((f32[2,2,4,8,128]{4,3,2,1,0:T(8,128)S(1)}, f32[2,2,4,8,128]{4,3,2,1,0:T(8,128)S(1)}, u32[]{:S(2)}, u32[]{:S(2)}) %collective-permute-start.7) | collective-permute-done | bytes 65568 | tf_op jit(solution)/shard_map/ppermute | solution.py:593
  22.4 0.0 collective-permute-done.1.refs_0_
  22.4 0.0 collective-permute-done.2.refs_1_
  22.4 1.8 %widen.1 = (f32[2,2,768,128]{3,2,1,0:T(8,128)S(1)}, f32[2,96,8,128]{3,2,1,0:T(8,128)S(1)}, f32[2,96,8,128]{3,2,1,0:T(8,128)S(1)}, f32[2,96,8,128]{3,2,1,0:T(8,128)S(1)}, f32[96,128]{1,0:T(8,128)S(1)}) custom-call(f32[2,12,8,128]{3,2,1,0:T(8,128)S(1)} %collective-permute-done.1.refs_0_, ...), custom_call_target="tpu_custom_call", output_to_operand_aliasing={{0}: (4, {})} | custom-call | tf_op jit(solution)/shard_map/widen/pallas_call | solution.py:620
  24.2 1.3 %collective-permute-start.9 = (f32[96,128]{1,0:T(8,128)S(1)}, f32[96,128]{1,0:T(8,128)S(1)}, u32[]{:S(2)}, u32[]{:S(2)}) collective-permute-start(f32[96,128]{1,0:T(8,128)S(1)} %get-tuple-element.20.refs_0_), channel_id=1, source_target_pairs={{0,8},{4,12},{8,0},{12,4},{1,9},{5,13},{9,1},{13,5},{2,10},{6,14},... | collective-permute-start | bytes 147464 | tf_op jit(solution)/shard_map/ppermute | solution.py:553
  25.5 0.7 %collective-permute-start.11 = (f32[96,128]{1,0:T(8,128)S(1)}, f32[96,128]{1,0:T(8,128)S(1)}, u32[]{:S(2)}, u32[]{:S(2)}) collective-permute-start(f32[96,128]{1,0:T(8,128)S(1)} %get-tuple-element.21.refs_4_), channel_id=1, source_target_pairs={{0,4},{4,0},{8,12},{12,8},{1,5},{5,1},{9,13},{13,9},{2,6},{6,2},{1... | collective-permute-start | bytes 147464 | tf_op jit(solution)/shard_map/ppermute | solution.py:553
  26.2 0.0 collective-permute-done.12.refs_6_
  26.2 0.0 collective-permute-start.13
  26.2 0.5 %collective-permute-start.8 = (f32[96,128]{1,0:T(8,128)S(1)}, f32[96,128]{1,0:T(8,128)S(1)}, u32[]{:S(2)}, u32[]{:S(2)}) collective-permute-start(f32[96,128]{1,0:T(8,128)S(1)} %get-tuple-element.20.refs_0_), channel_id=1, source_target_pairs={{0,4},{4,0},{8,12},{12,8},{1,5},{5,1},{9,13},{13,9},{2,6},{6,2},{1... | collective-permute-start | bytes 147464 | tf_op jit(solution)/shard_map/ppermute | solution.py:553
  26.7 1.7 %collective-permute-done.9.refs_2_ = f32[96,128]{1,0:T(8,128)S(1)} collective-permute-done((f32[96,128]{1,0:T(8,128)S(1)}, f32[96,128]{1,0:T(8,128)S(1)}, u32[]{:S(2)}, u32[]{:S(2)}) %collective-permute-start.9) | collective-permute-done | bytes 49184 | tf_op jit(solution)/shard_map/ppermute | solution.py:553
  28.5 0.0 collective-permute-start.10
  28.5 0.0 collective-permute-done.11.refs_5_
  28.5 0.0 collective-permute-done.13.refs_7_
  28.5 0.0 collective-permute-done.8.refs_1_
  28.5 1.2 %collective-permute-done.10.refs_3_ = f32[96,128]{1,0:T(8,128)S(1)} collective-permute-done((f32[96,128]{1,0:T(8,128)S(1)}, f32[96,128]{1,0:T(8,128)S(1)}, u32[]{:S(2)}, u32[]{:S(2)}) %collective-permute-start.10) | collective-permute-done | bytes 49184 | tf_op jit(solution)/shard_map/ppermute | solution.py:553
  29.7 2.1 %cycle.1 = (f32[2,96,8,128]{3,2,1,0:T(8,128)S(1)}, f32[2,96,8,128]{3,2,1,0:T(8,128)S(1)}, f32[48,8,128]{2,1,0:T(8,128)S(1)}, f32[12,8,128]{2,1,0:T(8,128)S(1)}, f32[112,128]{1,0:T(8,128)S(1)}) custom-call(f32[96,128]{1,0:T(8,128)S(1)} %get-tuple-element.20.refs_0_, f32[96,128]{1,0:T(8,128)S(1)} %collective-permute-done.8.refs_1_, ...), custom_call_target="tpu_custom_call" | custom-call | tf_op jit(solution)/shard_map/cycle/pallas_call | solution.py:637
  31.8 1.7 %collective-permute-start.15 = (f32[112,128]{1,0:T(8,128)S(1)}, f32[112,128]{1,0:T(8,128)S(1)}, u32[]{:S(2)}, u32[]{:S(2)}) collective-permute-start(f32[112,128]{1,0:T(8,128)S(1)} %get-tuple-element.25.refs_0_), channel_id=1, source_target_pairs={{0,8},{4,12},{8,0},{12,4},{1,9},{5,13},{9,1},{13,5},{2,10},{6,14},... | collective-permute-start | bytes 172040 | tf_op jit(solution)/shard_map/ppermute | solution.py:553
  33.6 0.0 collective-permute-start.14
  33.6 2.5 %collective-permute-done.15.refs_2_ = f32[112,128]{1,0:T(8,128)S(1)} collective-permute-done((f32[112,128]{1,0:T(8,128)S(1)}, f32[112,128]{1,0:T(8,128)S(1)}, u32[]{:S(2)}, u32[]{:S(2)}) %collective-permute-start.15) | collective-permute-done | bytes 57376 | tf_op jit(solution)/shard_map/ppermute | solution.py:553
  36.1 0.0 collective-permute-start.16
  36.1 0.0 collective-permute-done.14.refs_1_
  36.1 1.2 %collective-permute-done.16.refs_3_ = f32[112,128]{1,0:T(8,128)S(1)} collective-permute-done((f32[112,128]{1,0:T(8,128)S(1)}, f32[112,128]{1,0:T(8,128)S(1)}, u32[]{:S(2)}, u32[]{:S(2)}) %collective-permute-start.16) | collective-permute-done | bytes 57376 | tf_op jit(solution)/shard_map/ppermute | solution.py:553
  37.3 3.0 %collective-permute-start.17 = (f32[16,128]{1,0:T(8,128)S(1)}, f32[16,128]{1,0:T(8,128)S(1)}, u32[]{:S(2)}, u32[]{:S(2)}) collective-permute-start(f32[16,128]{1,0:T(8,128)S(1)} %slice_add_fusion.refs_0_), channel_id=1, source_target_pairs={{1,0},{0,1},{3,2},{2,3},{5,4},{4,5},{7,6},{6,7},{9,8},{8,9},{11,10... | collective-permute-start | bytes 24584 | tf_op jit(solution)/shard_map/ppermute | solution.py:655
  40.3 1.2 %collective-permute-start.18 = (f32[16,128]{1,0:T(8,128)S(1)}, f32[16,128]{1,0:T(8,128)S(1)}, u32[]{:S(2)}, u32[]{:S(2)}) collective-permute-start(f32[16,128]{1,0:T(8,128)S(1)} %slice_add_fusion.refs_0_), channel_id=1, source_target_pairs={{2,0},{3,1},{0,2},{1,3},{6,4},{7,5},{4,6},{5,7},{10,8},{11,9},{8,1... | collective-permute-start | bytes 24584 | tf_op jit(solution)/shard_map/ppermute | solution.py:655
  41.5 1.3 %collective-permute-start.19 = (f32[16,128]{1,0:T(8,128)S(1)}, f32[16,128]{1,0:T(8,128)S(1)}, u32[]{:S(2)}, u32[]{:S(2)}) collective-permute-start(f32[16,128]{1,0:T(8,128)S(1)} %slice_add_fusion.refs_0_), channel_id=1, source_target_pairs={{3,0},{2,1},{1,2},{0,3},{7,4},{6,5},{5,6},{4,7},{11,8},{10,9},{9,1... | collective-permute-start | bytes 24584 | tf_op jit(solution)/shard_map/ppermute | solution.py:655
  42.8 0.0 copy-start
  42.8 2.2 %again.1.refs_5_ = f32[4,192,128]{2,1,0:T(8,128)S(1)} custom-call(f32[112,128]{1,0:T(8,128)S(1)} %get-tuple-element.25.refs_0_, f32[112,128]{1,0:T(8,128)S(1)} %collective-permute-done.14.refs_1_, f32[112,128]{1,0:T(8,128)S(1)} %collective-permute-done.15.refs_2_, f32[112,128]{1,0:T(8,128)S(1)} %collective-permute-done.16.refs_3_, ...), custom_call_target="tpu_custom_call" | custom-call | tf_op jit(solution)/shard_map/again/pallas_call | solution.py:656
  45.0 0.0 collective-permute-done.17.refs_1_
  45.0 0.0 collective-permute-done.18.refs_2_
  45.0 1.9 %collective-permute-done.19.refs_3_ = f32[16,128]{1,0:T(8,128)S(1)} collective-permute-done((f32[16,128]{1,0:T(8,128)S(1)}, f32[16,128]{1,0:T(8,128)S(1)}, u32[]{:S(2)}, u32[]{:S(2)}) %collective-permute-start.19) | collective-permute-done | bytes 8224 | tf_op jit(solution)/shard_map/ppermute | solution.py:655
  46.9 0.0 copy-done
  46.9 0.9 %update.1 = (f32[12,16,128]{2,1,0:T(8,128)}, f32[12,16,128]{2,1,0:T(8,128)}, f32[12,16,128]{2,1,0:T(8,128)}, f32[12,16,128]{2,1,0:T(8,128)}) custom-call(f32[16,128]{1,0:T(8,128)S(1)} %slice_add_fusion.refs_0_, f32[16,128]{1,0:T(8,128)S(1)} %collective-permute-done.17.refs_1_, f32[16,128]{1,0:T(8,128)S(1)} %collective-permute-done.18.refs_2_, ...), custom_call_target="tpu_custom_call" | custom-call | tf_op jit(solution)/shard_map/update/pallas_call | solution.py:670
  (10 shorter events, 0.2 us)
Async XLA Ops:
  1.8 5.4 %collective-permute-start.3 = (f32[2,4,16,128]{3,2,1,0:T(8,128)S(1)}, f32[2,4,16,128]{3,2,1,0:T(8,128)S(1)}, u32[]{:S(2)}, u32[]{:S(2)}) collective-permute-start(f32[2,4,16,128]{3,2,1,0:T(8,128)S(1)} %get-tuple-element.17), channel_id=1, source_target_pairs={{0,1},{1,0},{2,3},{3,2},{4,5},{5,4},{6,7},{7,6},{8,9},{9,8},{10,11... | collective-permute-start | bytes 196616 | tf_op jit(solution)/shard_map/ppermute | solution.py:576
  4.9 2.2 %collective-permute-start.4 = (f32[2,4,16,128]{3,2,1,0:T(8,128)S(1)}, f32[2,4,16,128]{3,2,1,0:T(8,128)S(1)}, u32[]{:S(2)}, u32[]{:S(2)}) collective-permute-start(f32[2,4,16,128]{3,2,1,0:T(8,128)S(1)} %get-tuple-element.18), channel_id=1, source_target_pairs={{1,2},{2,1},{5,6},{6,5},{9,10},{10,9},{13,14},{14,13},{0,4},{3,7},... | collective-permute-start | bytes 196616 | tf_op jit(solution)/shard_map/ppermute | solution.py:576
  7.1 6.4 %collective-permute-start.5 = (f32[2,2,4,16,128]{4,3,2,0,1:T(8,128)S(1)}, f32[2,2,4,16,128]{4,3,2,0,1:T(8,128)S(1)}, u32[]{:S(2)}, u32[]{:S(2)}) collective-permute-start(f32[2,2,4,16,128]{4,3,2,0,1:T(8,128)S(1)} %get-tuple-element.49), channel_id=1, source_target_pairs={{16,0},{0,16},{17,1},{1,17},{18,2},{2,18},{19,3},{3,19},{20,4},{4,... | collective-permute-start | bytes 393224 | tf_op jit(solution)/shard_map/ppermute | solution.py:580
  9.2 6.8 %collective-permute-start = (f32[2,12,16,128]{3,2,1,0:T(8,128)S(1)}, f32[2,12,16,128]{3,2,1,0:T(8,128)S(1)}, u32[]{:S(2)}, u32[]{:S(2)}) collective-permute-start(f32[2,12,16,128]{3,2,1,0:T(8,128)S(1)} %get-tuple-element.41.refs_0_), channel_id=1, source_target_pairs={{16,0},{0,16},{17,1},{1,17},{18,2},{2,18},{19,3},{3,19},{20,4},{4,... | collective-permute-start | bytes 589832 | tf_op jit(solution)/shard_map/ppermute | solution.py:574
  16.1 6.3 %collective-permute-start.1 = (f32[2,12,8,128]{3,2,1,0:T(8,128)S(1)}, f32[2,12,8,128]{3,2,1,0:T(8,128)S(1)}, u32[]{:S(2)}, u32[]{:S(2)}) collective-permute-start(f32[2,12,8,128]{3,2,1,0:T(8,128)S(1)} %get-tuple-element.35), channel_id=1, source_target_pairs={{0,4},{4,0},{8,12},{12,8},{1,5},{5,1},{9,13},{13,9},{2,6},{6,2},{1... | collective-permute-start | bytes 294920 | tf_op jit(solution)/shard_map/ppermute | solution.py:592
  16.2 6.2 %collective-permute-start.2 = (f32[2,12,8,128]{3,2,1,0:T(8,128)S(1)}, f32[2,12,8,128]{3,2,1,0:T(8,128)S(1)}, u32[]{:S(2)}, u32[]{:S(2)}) collective-permute-start(f32[2,12,8,128]{3,2,1,0:T(8,128)S(1)} %get-tuple-element.34), channel_id=1, source_target_pairs={{4,8},{8,4},{12,0},{0,12},{5,9},{9,5},{13,1},{1,13},{6,10},{10,6},... | collective-permute-start | bytes 294920 | tf_op jit(solution)/shard_map/ppermute | solution.py:593
  17.9 2.9 %collective-permute-start.6 = (f32[2,2,4,8,128]{4,3,2,1,0:T(8,128)S(1)}, f32[2,2,4,8,128]{4,3,2,1,0:T(8,128)S(1)}, u32[]{:S(2)}, u32[]{:S(2)}) collective-permute-start(f32[2,2,4,8,128]{4,3,2,1,0:T(8,128)S(1)} %get-tuple-element.43), channel_id=1, source_target_pairs={{0,4},{4,0},{8,12},{12,8},{1,5},{5,1},{9,13},{13,9},{2,6},{6,2},{1... | collective-permute-start | bytes 196616 | tf_op jit(solution)/shard_map/ppermute | solution.py:592
  18.0 4.4 %collective-permute-start.7 = (f32[2,2,4,8,128]{4,3,2,1,0:T(8,128)S(1)}, f32[2,2,4,8,128]{4,3,2,1,0:T(8,128)S(1)}, u32[]{:S(2)}, u32[]{:S(2)}) collective-permute-start(f32[2,2,4,8,128]{4,3,2,1,0:T(8,128)S(1)} %get-tuple-element.42), channel_id=1, source_target_pairs={{4,8},{8,4},{12,0},{0,12},{5,9},{9,5},{13,1},{1,13},{6,10},{10,6},... | collective-permute-start | bytes 196616 | tf_op jit(solution)/shard_map/ppermute | solution.py:593
  19.2 7.1 %collective-permute-start.12 = (f32[96,128]{1,0:T(8,128)S(1)}, f32[96,128]{1,0:T(8,128)S(1)}, u32[]{:S(2)}, u32[]{:S(2)}) collective-permute-start(f32[96,128]{1,0:T(8,128)S(1)} %get-tuple-element.21.refs_4_), channel_id=1, source_target_pairs={{0,8},{4,12},{8,0},{12,4},{1,9},{5,13},{9,1},{13,5},{2,10},{6,14},... | collective-permute-start | bytes 147464 | tf_op jit(solution)/shard_map/ppermute | solution.py:553
  24.2 4.3 %collective-permute-start.9 = (f32[96,128]{1,0:T(8,128)S(1)}, f32[96,128]{1,0:T(8,128)S(1)}, u32[]{:S(2)}, u32[]{:S(2)}) collective-permute-start(f32[96,128]{1,0:T(8,128)S(1)} %get-tuple-element.20.refs_0_), channel_id=1, source_target_pairs={{0,8},{4,12},{8,0},{12,4},{1,9},{5,13},{9,1},{13,5},{2,10},{6,14},... | collective-permute-start | bytes 147464 | tf_op jit(solution)/shard_map/ppermute | solution.py:553
  25.5 2.9 %collective-permute-start.11 = (f32[96,128]{1,0:T(8,128)S(1)}, f32[96,128]{1,0:T(8,128)S(1)}, u32[]{:S(2)}, u32[]{:S(2)}) collective-permute-start(f32[96,128]{1,0:T(8,128)S(1)} %get-tuple-element.21.refs_4_), channel_id=1, source_target_pairs={{0,4},{4,0},{8,12},{12,8},{1,5},{5,1},{9,13},{13,9},{2,6},{6,2},{1... | collective-permute-start | bytes 147464 | tf_op jit(solution)/shard_map/ppermute | solution.py:553
  26.2 2.3 %collective-permute-start.13 = (f32[96,128]{1,0:T(8,128)S(1)}, f32[96,128]{1,0:T(8,128)S(1)}, u32[]{:S(2)}, u32[]{:S(2)}) collective-permute-start(f32[96,128]{1,0:T(8,128)S(1)} %collective-permute-done.12.refs_6_), channel_id=1, source_target_pairs={{0,4},{4,0},{8,12},{12,8},{1,5},{5,1},{9,13},{13,9},{2,6},{6,2},{1... | collective-permute-start | bytes 147464 | tf_op jit(solution)/shard_map/ppermute | solution.py:553
  26.2 2.3 %collective-permute-start.8 = (f32[96,128]{1,0:T(8,128)S(1)}, f32[96,128]{1,0:T(8,128)S(1)}, u32[]{:S(2)}, u32[]{:S(2)}) collective-permute-start(f32[96,128]{1,0:T(8,128)S(1)} %get-tuple-element.20.refs_0_), channel_id=1, source_target_pairs={{0,4},{4,0},{8,12},{12,8},{1,5},{5,1},{9,13},{13,9},{2,6},{6,2},{1... | collective-permute-start | bytes 147464 | tf_op jit(solution)/shard_map/ppermute | solution.py:553
  28.5 1.2 %collective-permute-start.10 = (f32[96,128]{1,0:T(8,128)S(1)}, f32[96,128]{1,0:T(8,128)S(1)}, u32[]{:S(2)}, u32[]{:S(2)}) collective-permute-start(f32[96,128]{1,0:T(8,128)S(1)} %collective-permute-done.9.refs_2_), channel_id=1, source_target_pairs={{0,4},{4,0},{8,12},{12,8},{1,5},{5,1},{9,13},{13,9},{2,6},{6,2},{1... | collective-permute-start | bytes 147464 | tf_op jit(solution)/shard_map/ppermute | solution.py:553
  31.8 4.2 %collective-permute-start.15 = (f32[112,128]{1,0:T(8,128)S(1)}, f32[112,128]{1,0:T(8,128)S(1)}, u32[]{:S(2)}, u32[]{:S(2)}) collective-permute-start(f32[112,128]{1,0:T(8,128)S(1)} %get-tuple-element.25.refs_0_), channel_id=1, source_target_pairs={{0,8},{4,12},{8,0},{12,4},{1,9},{5,13},{9,1},{13,5},{2,10},{6,14},... | collective-permute-start | bytes 172040 | tf_op jit(solution)/shard_map/ppermute | solution.py:553
  33.6 2.5 %collective-permute-start.14 = (f32[112,128]{1,0:T(8,128)S(1)}, f32[112,128]{1,0:T(8,128)S(1)}, u32[]{:S(2)}, u32[]{:S(2)}) collective-permute-start(f32[112,128]{1,0:T(8,128)S(1)} %get-tuple-element.25.refs_0_), channel_id=1, source_target_pairs={{0,4},{4,0},{8,12},{12,8},{1,5},{5,1},{9,13},{13,9},{2,6},{6,2},{1... | collective-permute-start | bytes 172040 | tf_op jit(solution)/shard_map/ppermute | solution.py:553
  36.1 1.2 %collective-permute-start.16 = (f32[112,128]{1,0:T(8,128)S(1)}, f32[112,128]{1,0:T(8,128)S(1)}, u32[]{:S(2)}, u32[]{:S(2)}) collective-permute-start(f32[112,128]{1,0:T(8,128)S(1)} %collective-permute-done.15.refs_2_), channel_id=1, source_target_pairs={{0,4},{4,0},{8,12},{12,8},{1,5},{5,1},{9,13},{13,9},{2,6},{6,2},{1... | collective-permute-start | bytes 172040 | tf_op jit(solution)/shard_map/ppermute | solution.py:553
  37.3 7.7 %collective-permute-start.17 = (f32[16,128]{1,0:T(8,128)S(1)}, f32[16,128]{1,0:T(8,128)S(1)}, u32[]{:S(2)}, u32[]{:S(2)}) collective-permute-start(f32[16,128]{1,0:T(8,128)S(1)} %slice_add_fusion.refs_0_), channel_id=1, source_target_pairs={{1,0},{0,1},{3,2},{2,3},{5,4},{4,5},{7,6},{6,7},{9,8},{8,9},{11,10... | collective-permute-start | bytes 24584 | tf_op jit(solution)/shard_map/ppermute | solution.py:655
  40.3 4.7 %collective-permute-start.18 = (f32[16,128]{1,0:T(8,128)S(1)}, f32[16,128]{1,0:T(8,128)S(1)}, u32[]{:S(2)}, u32[]{:S(2)}) collective-permute-start(f32[16,128]{1,0:T(8,128)S(1)} %slice_add_fusion.refs_0_), channel_id=1, source_target_pairs={{2,0},{3,1},{0,2},{1,3},{6,4},{7,5},{4,6},{5,7},{10,8},{11,9},{8,1... | collective-permute-start | bytes 24584 | tf_op jit(solution)/shard_map/ppermute | solution.py:655
  41.5 5.4 %collective-permute-start.19 = (f32[16,128]{1,0:T(8,128)S(1)}, f32[16,128]{1,0:T(8,128)S(1)}, u32[]{:S(2)}, u32[]{:S(2)}) collective-permute-start(f32[16,128]{1,0:T(8,128)S(1)} %slice_add_fusion.refs_0_), channel_id=1, source_target_pairs={{3,0},{2,1},{1,2},{0,3},{7,4},{6,5},{5,6},{4,7},{11,8},{10,9},{9,1... | collective-permute-start | bytes 24584 | tf_op jit(solution)/shard_map/ppermute | solution.py:655
  42.8 4.1 %copy-start = (f32[12,16,128]{2,1,0:T(8,128)S(1)}, f32[12,16,128]{2,1,0:T(8,128)}, u32[]{:S(2)}) copy-start(f32[12,16,128]{2,1,0:T(8,128)} %refs_4_.1) | copy-start | bytes 294916
